TPU v7x, 128 devices: a whole 4x4x4 slice. The times are simulated.
128 devices in a mesh: island: 8 (over x_lo, z), shard: 16 (over y, x_hi, core).
Axes of the slice: x: 4 (x_hi: 2, x_lo: 2; x = x_hi * 2 + x_lo), y: 4, z: 4, core: 2. Of those that a mesh axis runs over, the one named last changes fastest.
Arguments:
- weight_master: float32 [4096, 4096], P('island', 'shard'), may hold values from -6 to 6
- gain_master: float32 [4096], P(('shard', 'island')), may hold values from 0.5 to 1.5
- weight_moment: float32 [4096, 4096], P('island', 'shard'), may hold values from -0.3 to 0.3
- gain_moment: float32 [4096], P(('shard', 'island')), may hold values from -0.3 to 0.3
- attended: bfloat16 [8, 2, 1536, 4096], P('island', None, 'shard'), may hold values from -6 to 6
- stream: bfloat16 [8, 2, 1536, 4096], P('island', None, None, 'shard'), may hold values from -6 to 6
- targets: bfloat16 [8, 2, 1536, 4096], P('island', None, None, 'shard'), may hold values from -6 to 6
Outputs:
- weight_updated: float32 [4096, 4096], P('island', 'shard')
- gain_updated: float32 [4096], P(('shard', 'island'))
- weight_velocity: float32 [4096, 4096], P('island', 'shard')
- gain_velocity: float32 [4096], P(('shard', 'island'))
All inputs are finite; a program needn't handle non-finite values.
Results may differ from a plain program's by a relative error of at most 0.0066.
Values may be sent and summed in bfloat16 or wider, within the bound.
No kernel may reach another device: no remote copies, remote signals or barrier semaphores. Data moves between devices by JAX's collectives and lax.ppermute only.
A program may use at most 192 MiB of HBM per device.

v0:
```python
import jax
import jax.numpy as jnp
from jax import lax
from jax.experimental import pallas as pl
from jax.experimental.pallas import tpu as pltpu
from jax.sharding import Mesh
from jax.sharding import PartitionSpec as P


D = 4096
STEPS = 2
SHARD = ("y", "xh", "c")
SHARD_ISLAND = ("y", "xh", "c", "island")


norm_epsilon = 1e-05
inner_rate = 0.05
beta_one = 0.9
beta_two = 0.95
adam_epsilon = 0.3
decay_rate = 0.1
outer_rate = 0.7
outer_momentum = 0.9


def core_swap(value):
    return lax.ppermute(value, "c", [(0, 1), (1, 0)])


def x_swap(value):
    return lax.ppermute(value, "xh", [(0, 1), (1, 0)])


def y_hop(value, way):
    pairs = []
    for y in range(4):
        for c in range(2):
            to = (y + (way if c == 0 else -way)) % 4
            pairs.append((y * 2 + c, to * 2 + c))
    return lax.ppermute(value, ("y", "c"), pairs)


def copy_for_each(value, axis):
    copies = jnp.broadcast_to(value, (lax.axis_size(axis), *value.shape))
    return lax.all_to_all(copies, axis, split_axis=0, concat_axis=0, tiled=True)


def gathered_pieces(own):
    a = y_hop(own, 1)
    b = y_hop(own, -1)
    x = x_swap(own)
    a2 = y_hop(x, 1)
    b2 = y_hop(x, -1)
    f = y_hop(a, 1)
    f2 = y_hop(b2, -1)
    return (own, x, a, b, a2, b2, f, f2)


BLOCK = 96


def forward_kernel(*refs):
    pieces, (weight, weight_other, flow, residual, rows_out, rows, weights, came, loaded, left) = (
        refs[:8],
        refs[8:],
    )
    y, xh, c = lax.axis_index("y"), lax.axis_index("xh"), lax.axis_index("c")
    d = 1 - 2 * c
    before, after, across = (y + 4 - d) % 4, (y + 4 + d) % 4, (y + 2) % 4
    places = [
        (py * 2 + px) * BLOCK
        for py, px in (
            (y, xh), (y, 1 - xh), (before, xh), (after, xh),
            (before, 1 - xh), (after, 1 - xh), (across, xh), (across, 1 - xh),
        )
    ]
    wide = weight.shape[1]
    loads = [
        pltpu.make_async_copy(source, weights.at[half], loaded.at[half])
        for half, source in enumerate((weight, weight_other))
    ]
    takes = [
        pltpu.make_async_copy(source, rows.at[pl.ds(at * BLOCK, BLOCK)], came.at[at])
        for at, source in enumerate(pieces)
    ]
    gives = [
        pltpu.make_async_copy(
            rows.at[pl.ds(at * BLOCK, BLOCK)],
            rows_out.at[pl.ds(pl.multiple_of(places[at], BLOCK), BLOCK)],
            left.at[at],
        )
        for at in range(8)
    ]
    loads[0].start()
    for take in takes[:4]:
        take.start()
    loads[1].start()
    for take in takes[4:]:
        take.start()
    for group in range(2):
        members = range(group * 4, group * 4 + 4)
        for at in members:
            takes[at].wait()
            gives[at].start()
        for half in range(2):
            if group == 0:
                loads[half].wait()
            projected = jnp.dot(
                rows[group * 4 * BLOCK : (group + 1) * 4 * BLOCK, :],
                weights[half],
                preferred_element_type=jnp.float32,
            )
            columns = slice(half * wide, (half + 1) * wide)
            for place, at in enumerate(members):
                to = pl.ds(pl.multiple_of(places[at], BLOCK), BLOCK)
                residual[to, columns] = (
                    flow[to, columns].astype(jnp.float32)
                    + projected[place * BLOCK : (place + 1) * BLOCK] * D ** (-0.5)
                )
    for give in gives:
        give.wait()


def forward(pieces, weight, weight_other, flow):
    anywhere = pl.BlockSpec(memory_space=pl.ANY)
    inside = pl.BlockSpec(memory_space=pltpu.VMEM)
    tokens, features = flow.shape
    depth = weight.shape[0]
    return pl.pallas_call(
        forward_kernel,
        out_shape=(
            jax.ShapeDtypeStruct((tokens, features), jnp.float32),
            jax.ShapeDtypeStruct((tokens, depth), jnp.bfloat16),
        ),
        in_specs=[anywhere] * 10 + [inside],
        out_specs=(inside, anywhere),
        scratch_shapes=[
            pltpu.VMEM((tokens, depth), jnp.bfloat16),
            pltpu.VMEM((2, *weight.shape), jnp.bfloat16),
            pltpu.SemaphoreType.DMA((8,)),
            pltpu.SemaphoreType.DMA((2,)),
            pltpu.SemaphoreType.DMA((8,)),
        ],
        compiler_params=pltpu.CompilerParams(vmem_limit_bytes=24 * 1024 * 1024),
        cost_estimate=pl.CostEstimate(
            flops=2 * tokens * depth * features,
            bytes_accessed=4 * tokens * depth + 2 * depth * features,
            transcendentals=0,
        ),
        name="forward",
    )(*pieces, weight, weight_other, flow)


def first_update(param, gradient, decay):
    return param - inner_rate * (gradient / (jnp.abs(gradient) + adam_epsilon) + decay * param)


def second_update(param, before, gradient, decay):
    beside = (1.0 - beta_one) / (1.0 - beta_one**2)
    first_hat = (beta_one * beside) * before + beside * gradient
    beside = (1.0 - beta_two) / (1.0 - beta_two**2)
    second_hat = (beta_two * beside) * (before * before) + beside * (gradient * gradient)
    root = second_hat * lax.rsqrt(jnp.maximum(second_hat, 1e-37))
    return param - inner_rate * (first_hat / (root + adam_epsilon) + decay * param)


def per_device(weight_master, gain_master, weight_moment, gain_moment, attended, stream, targets):
    islands = lax.axis_size("island")
    width_scale = D ** (-0.5)
    c = lax.axis_index("c")
    wide = weight_master.shape[1]

    pieces = [gathered_pieces(attended[0][step]) for step in range(STEPS)]

    anchor_low = copy_for_each(weight_master.astype(jnp.bfloat16), "island")
    anchor_low = anchor_low.reshape(D, wide)
    gain_low = copy_for_each(gain_master.astype(jnp.bfloat16), "island").reshape(wide)

    def token_half(value):
        blocks = value[0].reshape(STEPS, 8, 2, 96, wide)
        mine = lax.dynamic_index_in_dim(blocks, c, axis=2, keepdims=False)
        theirs = lax.dynamic_index_in_dim(blocks, 1 - c, axis=2, keepdims=False)
        both = jnp.concatenate([mine, core_swap(theirs)], axis=-1)
        return both.reshape(STEPS, 768, 2 * wide)

    stream_half = token_half(stream)
    target_half = token_half(targets)

    weight_anchor = anchor_low.astype(jnp.float32)
    weight_low = anchor_low
    gain_anchor = gain_low.astype(jnp.float32)
    gain = jnp.concatenate([gain_anchor, core_swap(gain_low).astype(jnp.float32)])
    weight = weight_anchor
    for step in range(STEPS):
        weight_other = core_swap(weight_low)
        residual, rows = forward(pieces[step], weight_low, weight_other, stream_half[step])
        goal = target_half[step].astype(jnp.float32)
        scaled = residual * gain
        sums = [
            jnp.sum(residual * residual, axis=1),
            jnp.sum(scaled * scaled, axis=1),
            jnp.sum(goal * scaled, axis=1),
        ]
        sums = jnp.concatenate(sums).reshape(1, -1)
        totals = copy_for_each(sums, ("y", "xh"))
        totals = jnp.sum(totals, axis=0).reshape(3, -1)
        inverse = lax.rsqrt(totals[0] / D + norm_epsilon)
        slope = (inverse * totals[1] - totals[2])[:, None]
        inverse = inverse[:, None]
        normed = residual * inverse * gain
        loss_grad = lax.optimization_barrier((normed - goal).astype(jnp.bfloat16))
        loss_grad = loss_grad.astype(jnp.float32)
        residual_grad = (
            inverse * (loss_grad * gain) - residual * inverse * inverse * inverse * slope / D
        ).astype(jnp.bfloat16)
        gain_grad = jnp.sum(loss_grad * residual * inverse, axis=0)

        def over_tokens(columns):
            return jnp.einsum(
                "td,tf->df", rows, residual_grad[:, columns], preferred_element_type=jnp.float32
            )

        other = over_tokens(slice(wide, None)).astype(jnp.bfloat16)
        other = core_swap(other)
        mine = over_tokens(slice(0, wide))
        weight_grad = (mine + other.astype(jnp.float32)) * width_scale
        gain_other = core_swap(gain_grad)
        gain_grad = gain_grad + jnp.concatenate([gain_other[wide:], gain_other[:wide]])
        if step == 0:
            weight = first_update(weight, weight_grad, decay_rate)
            gain = first_update(gain, gain_grad, 0.0)
            weight_low = weight.astype(jnp.bfloat16)
            weight, weight_before, gain_before, weight_low = lax.optimization_barrier(
                (weight, weight_grad, gain_grad, weight_low)
            )
        else:
            weight = second_update(weight, weight_before, weight_grad, decay_rate)
            gain = second_update(gain, gain_before, gain_grad, 0.0)

    def sent_and_summed(value):
        blocks = value.reshape(islands, value.shape[0] // islands, *value.shape[1:])
        arrived = lax.all_to_all(blocks, "island", split_axis=0, concat_axis=0, tiled=True)
        return arrived.astype(jnp.float32).sum(axis=0)

    weight_pseudo = sent_and_summed((weight_anchor - weight).astype(jnp.bfloat16)) / islands
    gain_pseudo = sent_and_summed((gain_anchor - gain[:wide]).astype(jnp.bfloat16)) / islands
    weight_velocity = outer_momentum * weight_moment + weight_pseudo
    gain_velocity = outer_momentum * gain_moment + gain_pseudo
    weight_updated = weight_master - outer_rate * (weight_pseudo + outer_momentum * weight_velocity)
    gain_updated = gain_master - outer_rate * (gain_pseudo + outer_momentum * gain_velocity)
    return (weight_updated, gain_updated, weight_velocity, gain_velocity)


def solution(mesh):
    torus = Mesh(
        mesh.devices.reshape(mesh.shape["island"], 4, 2, 2), ("island", "y", "xh", "c")
    )
    return jax.shard_map(
        per_device,
        mesh=torus,
        in_specs=(
            P("island", SHARD),
            P(SHARD_ISLAND),
            P("island", SHARD),
            P(SHARD_ISLAND),
            P("island", None, SHARD, None),
            P("island", None, None, SHARD),
            P("island", None, None, SHARD),
        ),
        out_specs=(P("island", SHARD), P(SHARD_ISLAND), P("island", SHARD), P(SHARD_ISLAND)),
        check_vma=False,
    )
```

profile of v0, /device:TPU:1, one launch (start us, length us, event | category | flops | bytes accessed | tf_op | source)
XLA Modules:
  0.0 282.2 jit_solution(4952589083671195878)
XLA Ops:
  3.2 6.8 %all-to-all-start = ((bf16[8,512,256]{2,1,0:T(8,128)(2,1)}), bf16[8,512,256]{2,1,0:T(8,128)(2,1)S(1)}, u32[]{:S(2)}, u32[]{:S(2)}) async-start(bf16[8,512,256]{2,1,0:T(8,128)(2,1)} %broadcast_in_dim.8), calls=%async_computation | async-start | bytes 4194304 | tf_op jit(solution)/shard_map/all_to_all | solution.py:45
  14.8 2.7 collective-permute-start.1
  17.6 18.6 %all-to-all-done = bf16[8,512,256]{2,1,0:T(8,128)(2,1)S(1)} async-done(((bf16[8,512,256]{2,1,0:T(8,128)(2,1)}), bf16[8,512,256]{2,1,0:T(8,128)(2,1)S(1)}, u32[]{:S(2)}, u32[]{:S(2)}) %all-to-all-start) | async-done | bytes 2097184 | tf_op jit(solution)/shard_map/all_to_all | solution.py:45
  36.8 3.7 %all-to-all-start.1 = ((bf16[8,1,32]{2,1,0:T(2,128)(2,1)}), bf16[8,1,32]{2,1,0:T(2,128)(2,1)S(1)}, u32[]{:S(2)}, u32[]{:S(2)}) async-start(bf16[8,1,32]{2,1,0:T(2,128)(2,1)} %broadcast_in_dim.9), calls=%async_computation.1 | async-start | bytes 8192 | tf_op jit(solution)/shard_map/all_to_all | solution.py:45
  42.1 2.7 dynamic-slice_bitcast_fusion.2
  44.8 8.6 %all-to-all-done.1 = bf16[8,1,32]{2,1,0:T(2,128)(2,1)S(1)} async-done(((bf16[8,1,32]{2,1,0:T(2,128)(2,1)}), bf16[8,1,32]{2,1,0:T(2,128)(2,1)S(1)}, u32[]{:S(2)}, u32[]{:S(2)}) %all-to-all-start.1) | async-done | bytes 544 | tf_op jit(solution)/shard_map/all_to_all | solution.py:45
  61.9 11.5 %collective-permute-done.4.refs_5_ = bf16[96,4096]{1,0:T(8,128)(2,1)S(1)} collective-permute-done((bf16[96,4096]{1,0:T(8,128)(2,1)}, bf16[96,4096]{1,0:T(8,128)(2,1)S(1)}, u32[]{:S(2)}, u32[]{:S(2)}) %collective-permute-start.4) | collective-permute-done | bytes 786464 | tf_op jit(solution)/shard_map/ppermute | solution.py:40
  77.6 12.6 %collective-permute-done.2.refs_3_ = bf16[96,4096]{1,0:T(8,128)(2,1)S(1)} collective-permute-done((bf16[96,4096]{1,0:T(8,128)(2,1)}, bf16[96,4096]{1,0:T(8,128)(2,1)S(1)}, u32[]{:S(2)}, u32[]{:S(2)}) %collective-permute-start.2) | collective-permute-done | bytes 786464 | tf_op jit(solution)/shard_map/ppermute | solution.py:40
  90.3 5.9 %collective-permute-done.5.refs_6_ = bf16[96,4096]{1,0:T(8,128)(2,1)S(1)} collective-permute-done((bf16[96,4096]{1,0:T(8,128)(2,1)}, bf16[96,4096]{1,0:T(8,128)(2,1)S(1)}, u32[]{:S(2)}, u32[]{:S(2)}) %collective-permute-start.5) | collective-permute-done | bytes 786464 | tf_op jit(solution)/shard_map/ppermute | solution.py:40
  96.2 6.8 %collective-permute-done.6.refs_7_ = bf16[96,4096]{1,0:T(8,128)(2,1)S(1)} collective-permute-done((bf16[96,4096]{1,0:T(8,128)(2,1)S(1)}, bf16[96,4096]{1,0:T(8,128)(2,1)S(1)}, u32[]{:S(2)}, u32[]{:S(2)}) %collective-permute-start.6) | collective-permute-done | bytes 786464 | tf_op jit(solution)/shard_map/ppermute | solution.py:40
  103.0 7.6 %forward.2 = (f32[768,512]{1,0:T(8,128)S(1)}, bf16[768,4096]{1,0:T(8,128)(2,1)S(1)}) custom-call(bf16[96,4096]{1,0:T(8,128)(2,1)} %get-tuple-element.49.refs_0_, bf16[96,4096]{1,0:T(8,128)(2,1)} %collective-permute-done.refs_1_, bf16[96,4096]{1,0:T(8,128)(2,1)} %collective-permute-done.1.refs_2_, bf16[96,4096]{1,0:T(8,128)(2,1)S(1)} %collective-permute-done.2.refs_3_, ...), custom_call_target="tpu_custom_call" | custom-call | flops 3221225472 | bytes 16777216 | tf_op jit(solution)/shard_map/forward/pallas_call | solution.py:129
  110.6 2.6 copy-done.7
  113.8 11.9 %all_to_all.35 = f32[8,1,2304]{2,1,0:T(1,128)S(1)} all-to-all(f32[8,1,2304]{2,1,0:T(1,128)S(1)} %broadcast_in_dim.10), channel_id=1, replica_groups=mesh['island'=8,'y'=4,'xh'=2,'c'=2] {'y','xh'}, dimensions={0} | all-to-all | bytes 147456 | tf_op jit(solution)/shard_map/all_to_all | solution.py:45
  130.8 3.8 %collective-permute-start.11 = (bf16[4096,256]{1,0:T(8,128)(2,1)S(1)}, bf16[4096,256]{1,0:T(8,128)(2,1)S(1)}, u32[]{:S(2)}, u32[]{:S(2)}) collective-permute-start(bf16[4096,256]{1,0:T(8,128)(2,1)S(1)} %convolution_convert_fusion.1), channel_id=1, source_target_pairs={{0,1},{1,0},{2,3},{3,2},{4,5},{5,4},{6,7},{7,6},{8,9},{9,8},{10,11... | collective-permute-start | bytes 6291464 | tf_op jit(solution)/shard_map/ppermute | solution.py:27
  135.2 3.2 %collective-permute-done.12 = f32[512]{0:T(512)S(1)} collective-permute-done((f32[512]{0:T(512)S(1)}, f32[512]{0:T(512)S(1)}, u32[]{:S(2)}, u32[]{:S(2)}) %collective-permute-start.12) | collective-permute-done | bytes 2080 | tf_op jit(solution)/shard_map/ppermute | solution.py:27
  138.5 6.5 %fusion.31 = (bf16[4096,256]{1,0:T(8,128)(2,1)S(1)}, f32[4096,256]{1,0:T(8,128)}, f32[4096,256]{1,0:T(8,128)}) fusion(bf16[8,512,256]{2,1,0:T(8,128)(2,1)S(1)} %copy-done.2, bf16[4096,256]{1,0:T(8,128)(2,1)S(1)} %collective-permute-done.11, bf16[768,4096]{1,0:T(8,128)(2,1)S(1)} %copy-done.8, bf16[768,512]{1,0:T(8,128)(2,1)S(1)} %get-tuple-element.43), kind=kOutput, calls=%fused_computation.84 | convolution fusion | flops 1623195648 | bytes 21364736 | tf_op jit(solution)/shard_map/td,tf->df/dot_general | solution.py:219
  146.3 8.6 %collective-permute-done.13.refs_1_ = bf16[96,4096]{1,0:T(8,128)(2,1)S(1)} collective-permute-done((bf16[96,4096]{1,0:T(8,128)(2,1)S(1)}, bf16[96,4096]{1,0:T(8,128)(2,1)S(1)}, u32[]{:S(2)}, u32[]{:S(2)}) %collective-permute-start.13) | collective-permute-done | bytes 786464 | tf_op jit(solution)/shard_map/ppermute | solution.py:31
  159.1 13.1 %collective-permute-done.17.refs_5_ = bf16[96,4096]{1,0:T(8,128)(2,1)S(1)} collective-permute-done((bf16[96,4096]{1,0:T(8,128)(2,1)S(1)}, bf16[96,4096]{1,0:T(8,128)(2,1)S(1)}, u32[]{:S(2)}, u32[]{:S(2)}) %collective-permute-start.17) | collective-permute-done | bytes 786464 | tf_op jit(solution)/shard_map/ppermute | solution.py:40
  172.1 16.8 %collective-permute-done.15.refs_3_ = bf16[96,4096]{1,0:T(8,128)(2,1)S(1)} collective-permute-done((bf16[96,4096]{1,0:T(8,128)(2,1)S(1)}, bf16[96,4096]{1,0:T(8,128)(2,1)S(1)}, u32[]{:S(2)}, u32[]{:S(2)}) %collective-permute-start.15) | collective-permute-done | bytes 786464 | tf_op jit(solution)/shard_map/ppermute | solution.py:40
  189.0 3.1 %collective-permute-done.18.refs_6_ = bf16[96,4096]{1,0:T(8,128)(2,1)S(1)} collective-permute-done((bf16[96,4096]{1,0:T(8,128)(2,1)S(1)}, bf16[96,4096]{1,0:T(8,128)(2,1)S(1)}, u32[]{:S(2)}, u32[]{:S(2)}) %collective-permute-start.18) | collective-permute-done | bytes 786464 | tf_op jit(solution)/shard_map/ppermute | solution.py:40
  192.1 8.6 %collective-permute-done.19.refs_7_ = bf16[96,4096]{1,0:T(8,128)(2,1)S(1)} collective-permute-done((bf16[96,4096]{1,0:T(8,128)(2,1)S(1)}, bf16[96,4096]{1,0:T(8,128)(2,1)S(1)}, u32[]{:S(2)}, u32[]{:S(2)}) %collective-permute-start.19) | collective-permute-done | bytes 786464 | tf_op jit(solution)/shard_map/ppermute | solution.py:40
  200.7 6.7 %forward.3 = (f32[768,512]{1,0:T(8,128)S(1)}, bf16[768,4096]{1,0:T(8,128)(2,1)S(1)}) custom-call(bf16[96,4096]{1,0:T(8,128)(2,1)S(1)} %get-tuple-element.48.refs_0_, bf16[96,4096]{1,0:T(8,128)(2,1)S(1)} %collective-permute-done.13.refs_1_, bf16[96,4096]{1,0:T(8,128)(2,1)S(1)} %collective-permute-done.14.refs_2_, ...), custom_call_target="tpu_custom_call" | custom-call | flops 3221225472 | bytes 16777216 | tf_op jit(solution)/shard_map/forward/pallas_call | solution.py:129
  207.4 2.6 copy-done.5
  210.6 9.1 %all_to_all.36 = f32[8,1,2304]{2,1,0:T(1,128)S(1)} all-to-all(f32[8,1,2304]{2,1,0:T(1,128)S(1)} %broadcast_in_dim.11), channel_id=1, replica_groups=mesh['island'=8,'y'=4,'xh'=2,'c'=2] {'y','xh'}, dimensions={0} | all-to-all | bytes 147456 | tf_op jit(solution)/shard_map/all_to_all | solution.py:45
  222.7 3.3 %convolution_convert_fusion = bf16[4096,256]{1,0:T(8,128)(2,1)} fusion(bf16[768,4096]{1,0:T(8,128)(2,1)S(1)} %copy-done.6, bf16[768,512]{1,0:T(8,128)(2,1)S(1)} %get-tuple-element.41), kind=kOutput, calls=%fused_computation.6 | convolution fusion | flops 1611661312 | bytes 8781824 | tf_op jit(solution)/shard_map/td,tf->df/dot_general | solution.py:219
  226.0 3.6 %collective-permute-start.21 = (bf16[4096,256]{1,0:T(8,128)(2,1)}, bf16[4096,256]{1,0:T(8,128)(2,1)}, u32[]{:S(2)}, u32[]{:S(2)}) collective-permute-start(bf16[4096,256]{1,0:T(8,128)(2,1)} %convolution_convert_fusion), channel_id=1, source_target_pairs={{0,1},{1,0},{2,3},{3,2},{4,5},{5,4},{6,7},{7,6},{8,9},{9,8},{10,11... | collective-permute-start | bytes 6291464 | tf_op jit(solution)/shard_map/ppermute | solution.py:27
  229.6 4.1 %collective-permute-done.22 = f32[512]{0:T(512)S(1)} collective-permute-done((f32[512]{0:T(512)S(1)}, f32[512]{0:T(512)S(1)}, u32[]{:S(2)}, u32[]{:S(2)}) %collective-permute-start.22) | collective-permute-done | bytes 2080 | tf_op jit(solution)/shard_map/ppermute | solution.py:27
  234.4 3.3 %all-to-all-start.5 = ((bf16[8,1,32]{2,1,0:T(2,128)(2,1)}), bf16[8,1,32]{2,1,0:T(2,128)(2,1)S(1)}, u32[]{:S(2)}, u32[]{:S(2)}) async-start(bf16[8,1,32]{2,1,0:T(2,128)(2,1)} %copy.15), calls=%async_computation.5 | async-start | bytes 8192 | tf_op jit(solution)/shard_map/all_to_all | solution.py:242
  237.8 5.4 %convolution_add_fusion = f32[4096,256]{1,0:T(8,128)S(1)} fusion(bf16[768,4096]{1,0:T(8,128)(2,1)} %copy-done.5, bf16[4096,256]{1,0:T(8,128)(2,1)} %collective-permute-done.21, bf16[768,512]{1,0:T(8,128)(2,1)S(1)} %get-tuple-element.41), kind=kOutput, calls=%fused_computation.3 | convolution fusion | flops 1612709888 | bytes 12976128 | tf_op jit(solution)/shard_map/td,tf->df/dot_general | solution.py:219
  244.2 4.1 %fusion.3 = bf16[4096,256]{1,0:T(8,128)(2,1)} fusion(f32[4096,256]{1,0:T(8,128)S(1)} %copy-done.11, f32[4096,256]{1,0:T(8,128)S(1)} %convolution_add_fusion, f32[4096,256]{1,0:T(8,128)S(1)} %copy-done.12, bf16[8,512,256]{2,1,0:T(8,128)(2,1)S(1)} %copy-done.3), kind=kLoop, calls=%fused_computation.10 | loop fusion | flops 20971520 | bytes 16777216 | tf_op jit(solution)/shard_map/convert_element_type | solution.py:245
  248.3 5.2 %all-to-all-start.4 = ((bf16[8,512,256]{2,1,0:T(8,128)(2,1)}), bf16[8,512,256]{2,1,0:T(8,128)(2,1)S(1)}, u32[]{:S(2)}, u32[]{:S(2)}) async-start(bf16[8,512,256]{2,1,0:T(8,128)(2,1)} %bitcast.40), calls=%async_computation.4 | async-start | bytes 4194304 | tf_op jit(solution)/shard_map/all_to_all | solution.py:242
  254.1 25.6 %all-to-all-done.4 = bf16[8,512,256]{2,1,0:T(8,128)(2,1)S(1)} async-done(((bf16[8,512,256]{2,1,0:T(8,128)(2,1)}), bf16[8,512,256]{2,1,0:T(8,128)(2,1)S(1)}, u32[]{:S(2)}, u32[]{:S(2)}) %all-to-all-start.4) | async-done | bytes 2097184 | tf_op jit(solution)/shard_map/all_to_all | solution.py:242
  (107 shorter events, 42.2 us)
Async XLA Ops:
  3.2 33.0 %all-to-all-start = ((bf16[8,512,256]{2,1,0:T(8,128)(2,1)}), bf16[8,512,256]{2,1,0:T(8,128)(2,1)S(1)}, u32[]{:S(2)}, u32[]{:S(2)}) async-start(bf16[8,512,256]{2,1,0:T(8,128)(2,1)} %broadcast_in_dim.8), calls=%async_computation | async-start | bytes 4194304 | tf_op jit(solution)/shard_map/all_to_all | solution.py:45
  12.4 44.6 %collective-permute-start = (bf16[96,4096]{1,0:T(8,128)(2,1)}, bf16[96,4096]{1,0:T(8,128)(2,1)}, u32[]{:S(2)}, u32[]{:S(2)}) collective-permute-start(bf16[96,4096]{1,0:T(8,128)(2,1)} %get-tuple-element.49.refs_0_), channel_id=1, source_target_pairs={{0,2},{2,0},{1,3},{3,1},{4,6},{6,4},{5,7},{7,5},{8,10},{10,8},{9,1... | collective-permute-start | bytes 2359304 | tf_op jit(solution)/shard_map/ppermute | solution.py:31
  14.8 43.4 %collective-permute-start.1 = (bf16[96,4096]{1,0:T(8,128)(2,1)}, bf16[96,4096]{1,0:T(8,128)(2,1)}, u32[]{:S(2)}, u32[]{:S(2)}) collective-permute-start(bf16[96,4096]{1,0:T(8,128)(2,1)} %get-tuple-element.49.refs_0_), channel_id=1, source_target_pairs={{0,4},{1,13},{4,8},{5,1},{8,12},{9,5},{12,0},{13,9},{2,6},{3,15},{... | collective-permute-start | bytes 2359304 | tf_op jit(solution)/shard_map/ppermute | solution.py:40
  36.8 16.6 %all-to-all-start.1 = ((bf16[8,1,32]{2,1,0:T(2,128)(2,1)}), bf16[8,1,32]{2,1,0:T(2,128)(2,1)S(1)}, u32[]{:S(2)}, u32[]{:S(2)}) async-start(bf16[8,1,32]{2,1,0:T(2,128)(2,1)} %broadcast_in_dim.9), calls=%async_computation.1 | async-start | bytes 8192 | tf_op jit(solution)/shard_map/all_to_all | solution.py:45
  40.4 62.6 %collective-permute-start.7 = (bf16[4096,256]{1,0:T(8,128)(2,1)S(1)}, bf16[4096,256]{1,0:T(8,128)(2,1)}, u32[]{:S(2)}, u32[]{:S(2)}) collective-permute-start(bf16[4096,256]{1,0:T(8,128)(2,1)S(1)} %bitcast.36), channel_id=1, source_target_pairs={{0,1},{1,0},{2,3},{3,2},{4,5},{5,4},{6,7},{7,6},{8,9},{9,8},{10,11... | collective-permute-start | bytes 6291464 | tf_op jit(solution)/shard_map/ppermute | solution.py:27
  44.8 14.8 %collective-permute-start.8 = (bf16[2,8,96,256]{3,2,1,0:T(8,128)(2,1)}, bf16[2,8,96,256]{3,2,1,0:T(8,128)(2,1)}, u32[]{:S(2)}, u32[]{:S(2)}) collective-permute-start(bf16[2,8,96,256]{3,2,1,0:T(8,128)(2,1)} %get-tuple-element.52), channel_id=1, source_target_pairs={{0,1},{1,0},{2,3},{3,2},{4,5},{5,4},{6,7},{7,6},{8,9},{9,8},{10,11... | collective-permute-start | bytes 2359304 | tf_op jit(solution)/shard_map/ppermute | solution.py:27
  53.5 21.0 %copy-start.13 = (bf16[2,8,96,256]{3,2,1,0:T(8,128)(2,1)S(1)}, bf16[2,8,96,256]{3,2,1,0:T(8,128)(2,1)}, u32[]{:S(2)}) copy-start(bf16[2,8,96,256]{3,2,1,0:T(8,128)(2,1)} %get-tuple-element.53) | copy-start | bytes 2359300
  53.5 3.3 %collective-permute-start.9 = (bf16[256]{0:T(256)(128)(2,1)S(1)}, bf16[256]{0:T(256)(128)(2,1)S(1)}, u32[]{:S(2)}, u32[]{:S(2)}) collective-permute-start(bf16[256]{0:T(256)(128)(2,1)S(1)} %reshape.173), channel_id=1, source_target_pairs={{0,1},{1,0},{2,3},{3,2},{4,5},{5,4},{6,7},{7,6},{8,9},{9,8},{10,11... | collective-permute-start | bytes 1544 | tf_op jit(solution)/shard_map/ppermute | solution.py:27
  56.8 4.2 %collective-permute-start.10 = (bf16[2,8,96,256]{3,2,1,0:T(8,128)(2,1)S(1)}, bf16[2,8,96,256]{3,2,1,0:T(8,128)(2,1)S(1)}, u32[]{:S(2)}, u32[]{:S(2)}) collective-permute-start(bf16[2,8,96,256]{3,2,1,0:T(8,128)(2,1)S(1)} %get-tuple-element.50), channel_id=1, source_target_pairs={{0,1},{1,0},{2,3},{3,2},{4,5},{5,4},{6,7},{7,6},{8,9},{9,8},{10,11... | collective-permute-start | bytes 2359304 | tf_op jit(solution)/shard_map/ppermute | solution.py:27
  57.0 16.5 %collective-permute-start.4 = (bf16[96,4096]{1,0:T(8,128)(2,1)}, bf16[96,4096]{1,0:T(8,128)(2,1)S(1)}, u32[]{:S(2)}, u32[]{:S(2)}) collective-permute-start(bf16[96,4096]{1,0:T(8,128)(2,1)} %collective-permute-done.refs_1_), channel_id=1, source_target_pairs={{0,12},{1,5},{4,0},{5,9},{8,4},{9,13},{12,8},{13,1},{2,14},{3,7},{... | collective-permute-start | bytes 2359304 | tf_op jit(solution)/shard_map/ppermute | solution.py:40
  58.3 32.0 %collective-permute-start.2 = (bf16[96,4096]{1,0:T(8,128)(2,1)}, bf16[96,4096]{1,0:T(8,128)(2,1)S(1)}, u32[]{:S(2)}, u32[]{:S(2)}) collective-permute-start(bf16[96,4096]{1,0:T(8,128)(2,1)} %get-tuple-element.49.refs_0_), channel_id=1, source_target_pairs={{0,12},{1,5},{4,0},{5,9},{8,4},{9,13},{12,8},{13,1},{2,14},{3,7},{... | collective-permute-start | bytes 2359304 | tf_op jit(solution)/shard_map/ppermute | solution.py:40
  59.6 36.6 %collective-permute-start.3 = (bf16[96,4096]{1,0:T(8,128)(2,1)}, bf16[96,4096]{1,0:T(8,128)(2,1)S(1)}, u32[]{:S(2)}, u32[]{:S(2)}) collective-permute-start(bf16[96,4096]{1,0:T(8,128)(2,1)} %collective-permute-done.refs_1_), channel_id=1, source_target_pairs={{0,4},{1,13},{4,8},{5,1},{8,12},{9,5},{12,0},{13,9},{2,6},{3,15},{... | collective-permute-start | bytes 2359304 | tf_op jit(solution)/shard_map/ppermute | solution.py:40
  60.9 35.2 %collective-permute-start.5 = (bf16[96,4096]{1,0:T(8,128)(2,1)}, bf16[96,4096]{1,0:T(8,128)(2,1)S(1)}, u32[]{:S(2)}, u32[]{:S(2)}) collective-permute-start(bf16[96,4096]{1,0:T(8,128)(2,1)} %collective-permute-done.1.refs_2_), channel_id=1, source_target_pairs={{0,4},{1,13},{4,8},{5,1},{8,12},{9,5},{12,0},{13,9},{2,6},{3,15},{... | collective-permute-start | bytes 2359304 | tf_op jit(solution)/shard_map/ppermute | solution.py:40
  73.4 29.6 %collective-permute-start.6 = (bf16[96,4096]{1,0:T(8,128)(2,1)S(1)}, bf16[96,4096]{1,0:T(8,128)(2,1)S(1)}, u32[]{:S(2)}, u32[]{:S(2)}) collective-permute-start(bf16[96,4096]{1,0:T(8,128)(2,1)S(1)} %collective-permute-done.4.refs_5_), channel_id=1, source_target_pairs={{0,12},{1,5},{4,0},{5,9},{8,4},{9,13},{12,8},{13,1},{2,14},{3,7},{... | collective-permute-start | bytes 2359304 | tf_op jit(solution)/shard_map/ppermute | solution.py:40
  76.6 26.4 %copy-start.1 = (bf16[8,512,256]{2,1,0:T(8,128)(2,1)S(1)}, bf16[8,512,256]{2,1,0:T(8,128)(2,1)}, u32[]{:S(2)}) copy-start(bf16[8,512,256]{2,1,0:T(8,128)(2,1)} %copy-done) | copy-start | bytes 6291460
  77.6 35.6 %copy-start.10 = (bf16[1,8,96,512]{3,2,1,0:T(8,128)(2,1)}, bf16[1,8,96,512]{3,2,1,0:T(8,128)(2,1)S(1)}, u32[]{:S(2)}) copy-start(bf16[1,8,96,512]{3,2,1,0:T(8,128)(2,1)S(1)} %get-tuple-element.45) | copy-start | bytes 2359300
  130.8 7.6 %collective-permute-start.11 = (bf16[4096,256]{1,0:T(8,128)(2,1)S(1)}, bf16[4096,256]{1,0:T(8,128)(2,1)S(1)}, u32[]{:S(2)}, u32[]{:S(2)}) collective-permute-start(bf16[4096,256]{1,0:T(8,128)(2,1)S(1)} %convolution_convert_fusion.1), channel_id=1, source_target_pairs={{0,1},{1,0},{2,3},{3,2},{4,5},{5,4},{6,7},{7,6},{8,9},{9,8},{10,11... | collective-permute-start | bytes 6291464 | tf_op jit(solution)/shard_map/ppermute | solution.py:27
  134.6 3.8 %collective-permute-start.12 = (f32[512]{0:T(512)S(1)}, f32[512]{0:T(512)S(1)}, u32[]{:S(2)}, u32[]{:S(2)}) collective-permute-start(f32[512]{0:T(512)S(1)} %get-tuple-element.42), channel_id=1, source_target_pairs={{0,1},{1,0},{2,3},{3,2},{4,5},{5,4},{6,7},{7,6},{8,9},{9,8},{10,11... | collective-permute-start | bytes 6152 | tf_op jit(solution)/shard_map/ppermute | solution.py:27
  134.7 20.2 %collective-permute-start.13 = (bf16[96,4096]{1,0:T(8,128)(2,1)S(1)}, bf16[96,4096]{1,0:T(8,128)(2,1)S(1)}, u32[]{:S(2)}, u32[]{:S(2)}) collective-permute-start(bf16[96,4096]{1,0:T(8,128)(2,1)S(1)} %get-tuple-element.48.refs_0_), channel_id=1, source_target_pairs={{0,2},{2,0},{1,3},{3,1},{4,6},{6,4},{5,7},{7,5},{8,10},{10,8},{9,1... | collective-permute-start | bytes 2359304 | tf_op jit(solution)/shard_map/ppermute | solution.py:31
  138.5 62.2 %copy-start.4 = (bf16[1,8,96,512]{3,2,1,0:T(8,128)(2,1)S(1)}, bf16[1,8,96,512]{3,2,1,0:T(8,128)(2,1)}, u32[]{:S(2)}) copy-start(bf16[1,8,96,512]{3,2,1,0:T(8,128)(2,1)} %get-tuple-element.46) | copy-start | bytes 2359300
  145.0 55.7 %collective-permute-start.20 = (bf16[4096,256]{1,0:T(8,128)(2,1)S(1)}, bf16[4096,256]{1,0:T(8,128)(2,1)S(1)}, u32[]{:S(2)}, u32[]{:S(2)}) collective-permute-start(bf16[4096,256]{1,0:T(8,128)(2,1)S(1)} %get-tuple-element.16.refs_8_), channel_id=1, source_target_pairs={{0,1},{1,0},{2,3},{3,2},{4,5},{5,4},{6,7},{7,6},{8,9},{9,8},{10,11... | collective-permute-start | bytes 6291464 | tf_op jit(solution)/shard_map/ppermute | solution.py:27
  145.4 12.5 %collective-permute-start.14 = (bf16[96,4096]{1,0:T(8,128)(2,1)S(1)}, bf16[96,4096]{1,0:T(8,128)(2,1)S(1)}, u32[]{:S(2)}, u32[]{:S(2)}) collective-permute-start(bf16[96,4096]{1,0:T(8,128)(2,1)S(1)} %get-tuple-element.48.refs_0_), channel_id=1, source_target_pairs={{0,4},{1,13},{4,8},{5,1},{8,12},{9,5},{12,0},{13,9},{2,6},{3,15},{... | collective-permute-start | bytes 2359304 | tf_op jit(solution)/shard_map/ppermute | solution.py:40
  154.9 17.2 %collective-permute-start.17 = (bf16[96,4096]{1,0:T(8,128)(2,1)S(1)}, bf16[96,4096]{1,0:T(8,128)(2,1)S(1)}, u32[]{:S(2)}, u32[]{:S(2)}) collective-permute-start(bf16[96,4096]{1,0:T(8,128)(2,1)S(1)} %collective-permute-done.13.refs_1_), channel_id=1, source_target_pairs={{0,12},{1,5},{4,0},{5,9},{8,4},{9,13},{12,8},{13,1},{2,14},{3,7},{... | collective-permute-start | bytes 2359304 | tf_op jit(solution)/shard_map/ppermute | solution.py:40
  155.2 33.8 %collective-permute-start.15 = (bf16[96,4096]{1,0:T(8,128)(2,1)S(1)}, bf16[96,4096]{1,0:T(8,128)(2,1)S(1)}, u32[]{:S(2)}, u32[]{:S(2)}) collective-permute-start(bf16[96,4096]{1,0:T(8,128)(2,1)S(1)} %get-tuple-element.48.refs_0_), channel_id=1, source_target_pairs={{0,12},{1,5},{4,0},{5,9},{8,4},{9,13},{12,8},{13,1},{2,14},{3,7},{... | collective-permute-start | bytes 2359304 | tf_op jit(solution)/shard_map/ppermute | solution.py:40
  155.6 36.5 %collective-permute-start.16 = (bf16[96,4096]{1,0:T(8,128)(2,1)S(1)}, bf16[96,4096]{1,0:T(8,128)(2,1)S(1)}, u32[]{:S(2)}, u32[]{:S(2)}) collective-permute-start(bf16[96,4096]{1,0:T(8,128)(2,1)S(1)} %collective-permute-done.13.refs_1_), channel_id=1, source_target_pairs={{0,4},{1,13},{4,8},{5,1},{8,12},{9,5},{12,0},{13,9},{2,6},{3,15},{... | collective-permute-start | bytes 2359304 | tf_op jit(solution)/shard_map/ppermute | solution.py:40
  157.9 34.2 %collective-permute-start.18 = (bf16[96,4096]{1,0:T(8,128)(2,1)S(1)}, bf16[96,4096]{1,0:T(8,128)(2,1)S(1)}, u32[]{:S(2)}, u32[]{:S(2)}) collective-permute-start(bf16[96,4096]{1,0:T(8,128)(2,1)S(1)} %collective-permute-done.14.refs_2_), channel_id=1, source_target_pairs={{0,4},{1,13},{4,8},{5,1},{8,12},{9,5},{12,0},{13,9},{2,6},{3,15},{... | collective-permute-start | bytes 2359304 | tf_op jit(solution)/shard_map/ppermute | solution.py:40
  172.1 28.6 %collective-permute-start.19 = (bf16[96,4096]{1,0:T(8,128)(2,1)S(1)}, bf16[96,4096]{1,0:T(8,128)(2,1)S(1)}, u32[]{:S(2)}, u32[]{:S(2)}) collective-permute-start(bf16[96,4096]{1,0:T(8,128)(2,1)S(1)} %collective-permute-done.17.refs_5_), channel_id=1, source_target_pairs={{0,12},{1,5},{4,0},{5,9},{8,4},{9,13},{12,8},{13,1},{2,14},{3,7},{... | collective-permute-start | bytes 2359304 | tf_op jit(solution)/shard_map/ppermute | solution.py:40
  226.0 11.8 %collective-permute-start.21 = (bf16[4096,256]{1,0:T(8,128)(2,1)}, bf16[4096,256]{1,0:T(8,128)(2,1)}, u32[]{:S(2)}, u32[]{:S(2)}) collective-permute-start(bf16[4096,256]{1,0:T(8,128)(2,1)} %convolution_convert_fusion), channel_id=1, source_target_pairs={{0,1},{1,0},{2,3},{3,2},{4,5},{5,4},{6,7},{7,6},{8,9},{9,8},{10,11... | collective-permute-start | bytes 6291464 | tf_op jit(solution)/shard_map/ppermute | solution.py:27
  229.6 4.1 %collective-permute-start.22 = (f32[512]{0:T(512)S(1)}, f32[512]{0:T(512)S(1)}, u32[]{:S(2)}, u32[]{:S(2)}) collective-permute-start(f32[512]{0:T(512)S(1)} %get-tuple-element.40), channel_id=1, source_target_pairs={{0,1},{1,0},{2,3},{3,2},{4,5},{5,4},{6,7},{7,6},{8,9},{9,8},{10,11... | collective-permute-start | bytes 6152 | tf_op jit(solution)/shard_map/ppermute | solution.py:27
  234.4 13.9 %all-to-all-start.5 = ((bf16[8,1,32]{2,1,0:T(2,128)(2,1)}), bf16[8,1,32]{2,1,0:T(2,128)(2,1)S(1)}, u32[]{:S(2)}, u32[]{:S(2)}) async-start(bf16[8,1,32]{2,1,0:T(2,128)(2,1)} %copy.15), calls=%async_computation.5 | async-start | bytes 8192 | tf_op jit(solution)/shard_map/all_to_all | solution.py:242
  248.3 31.4 %all-to-all-start.4 = ((bf16[8,512,256]{2,1,0:T(8,128)(2,1)}), bf16[8,512,256]{2,1,0:T(8,128)(2,1)S(1)}, u32[]{:S(2)}, u32[]{:S(2)}) async-start(bf16[8,512,256]{2,1,0:T(8,128)(2,1)} %bitcast.40), calls=%async_computation.4 | async-start | bytes 4194304 | tf_op jit(solution)/shard_map/all_to_all | solution.py:242
  253.5 26.5 %copy-start.14 = (f32[512,256]{1,0:T(8,128)S(1)}, f32[512,256]{1,0:T(8,128)}, u32[]{:S(2)}) copy-start(f32[512,256]{1,0:T(8,128)} %param.7) | copy-start | bytes 1572868
  (12 other events, 80.9 us)
where the time goes:
time: 283 us; the launch traced here: 282 us
  waiting for transfers between devices  147 us (52%)
  starting transfers between devices  47.1 us (17%)
  blocking collectives  21 us (7%)
  local copies, waits for them, and re-layouts  18.4 us (7%)
  matrix products  17.2 us (6%)
  other arithmetic  15.9 us (6%)
  Pallas kernels  14.3 us (5%)
    ppermute x12, waiting for transfers between devices, y_hop(): return lax.ppermute(value, ('y', 'c'), pairs)  78.5 us
    all_to_all x2, waiting for transfers between devices, copy_for_each(): return lax.all_to_all(copies, axis, split_axis=0, concat_axis=0, tiled=True)  27.2 us
    all_to_all x2, waiting for transfers between devices, sent_and_summed(): lax.all_to_all(blocks, 'island', split_axis=0, concat_axis=0, tiled=True)  25.6 us
    all_to_all x2, blocking collectives, copy_for_each(): return lax.all_to_all(copies, axis, split_axis=0, concat_axis=0, tiled=True)  21 us
    dot_general x4, matrix products, over_tokens(): jnp.einsum('td,tf->df', rows, residual_grad[:, columns], preferred_elemen...  17.2 us
    pallas_call x2, Pallas kernels, forward(): pl.pallas_call(forward_kernel, out_shape=(jax.ShapeDtypeStruct((tokens, f...  14.3 us
    ppermute x12, starting transfers between devices, y_hop(): return lax.ppermute(value, ('y', 'c'), pairs)  13.7 us
    ppermute x9, starting transfers between devices, core_swap(): return lax.ppermute(value, 'c', [(0, 1), (1, 0)])  11.5 us
  transfers between devices with their start and end apart: 27, of which 14 were waited for; matrix products, arithmetic and copies ran while one was open for 10% of the time, Pallas kernels for 0%

commit v1 on v0

--- a/solution.py
+++ b/solution.py
@@ -74,9 +74,11 @@
             (before, 1 - xh), (after, 1 - xh), (across, xh), (across, 1 - xh),
         )
     ]
-    wide = weight.shape[1]
+    wide = weight.shape[2]
     loads = [
-        pltpu.make_async_copy(source, weights.at[half], loaded.at[half])
+        pltpu.make_async_copy(
+            source.at[:, pl.ds(0, weights.shape[2])], weights.at[half], loaded.at[half]
+        )
         for half, source in enumerate((weight, weight_other))
     ]
     takes = [
@@ -107,7 +109,7 @@
                 loads[half].wait()
             projected = jnp.dot(
                 rows[group * 4 * BLOCK : (group + 1) * 4 * BLOCK, :],
-                weights[half],
+                weights[half].reshape(D, wide),
                 preferred_element_type=jnp.float32,
             )
             columns = slice(half * wide, (half + 1) * wide)
@@ -125,7 +127,8 @@
     anywhere = pl.BlockSpec(memory_space=pl.ANY)
     inside = pl.BlockSpec(memory_space=pltpu.VMEM)
     tokens, features = flow.shape
-    depth = weight.shape[0]
+    depth = D
+    islands, _, wide = weight.shape
     return pl.pallas_call(
         forward_kernel,
         out_shape=(
@@ -133,10 +136,10 @@
             jax.ShapeDtypeStruct((tokens, depth), jnp.bfloat16),
         ),
         in_specs=[anywhere] * 10 + [inside],
-        out_specs=(inside, anywhere),
+        out_specs=(inside, pl.BlockSpec(memory_space=pltpu.HBM)),
         scratch_shapes=[
             pltpu.VMEM((tokens, depth), jnp.bfloat16),
-            pltpu.VMEM((2, *weight.shape), jnp.bfloat16),
+            pltpu.VMEM((2, islands, depth // islands, wide), jnp.bfloat16),
             pltpu.SemaphoreType.DMA((8,)),
             pltpu.SemaphoreType.DMA((2,)),
             pltpu.SemaphoreType.DMA((8,)),
@@ -172,9 +175,17 @@
 
     pieces = [gathered_pieces(attended[0][step]) for step in range(STEPS)]
 
-    anchor_low = copy_for_each(weight_master.astype(jnp.bfloat16), "island")
-    anchor_low = anchor_low.reshape(D, wide)
-    gain_low = copy_for_each(gain_master.astype(jnp.bfloat16), "island").reshape(wide)
+    def with_gain(weight_rows, gain_rows):
+        filled = [(0, 0)] * (gain_rows.ndim - 1) + [(0, 15), (0, wide - gain_rows.shape[-1])]
+        return jnp.concatenate([weight_rows, jnp.pad(gain_rows[..., None, :], filled)], axis=-2)
+
+    owned, share = weight_master.shape[0], gain_master.shape[0]
+    packed = with_gain(weight_master.astype(jnp.bfloat16), gain_master.astype(jnp.bfloat16))
+    packed = copy_for_each(packed, "island")
+    packed_other = core_swap(packed)
+    anchor_low = packed[:, :owned].reshape(D, wide)
+    gain_anchor = packed[:, owned, :share].reshape(wide).astype(jnp.float32)
+    gain_other = packed_other[:, owned, :share].reshape(wide).astype(jnp.float32)
 
     def token_half(value):
         blocks = value[0].reshape(STEPS, 8, 2, 96, wide)
@@ -187,13 +198,15 @@
     target_half = token_half(targets)
 
     weight_anchor = anchor_low.astype(jnp.float32)
-    weight_low = anchor_low
-    gain_anchor = gain_low.astype(jnp.float32)
-    gain = jnp.concatenate([gain_anchor, core_swap(gain_low).astype(jnp.float32)])
+    gain = jnp.concatenate([gain_anchor, gain_other])
     weight = weight_anchor
     for step in range(STEPS):
-        weight_other = core_swap(weight_low)
-        residual, rows = forward(pieces[step], weight_low, weight_other, stream_half[step])
+        if step == 0:
+            held, held_other = packed, packed_other
+        else:
+            held = weight_low.reshape(islands, owned, wide)
+            held_other = core_swap(held)
+        residual, rows = forward(pieces[step], held, held_other, stream_half[step])
         goal = target_half[step].astype(jnp.float32)
         scaled = residual * gain
         sums = [
@@ -222,7 +235,7 @@
 
         other = over_tokens(slice(wide, None)).astype(jnp.bfloat16)
         other = core_swap(other)
-        mine = over_tokens(slice(0, wide))
+        mine = lax.optimization_barrier(over_tokens(slice(0, wide)))
         weight_grad = (mine + other.astype(jnp.float32)) * width_scale
         gain_other = core_swap(gain_grad)
         gain_grad = gain_grad + jnp.concatenate([gain_other[wide:], gain_other[:wide]])
@@ -237,13 +250,13 @@
             weight = second_update(weight, weight_before, weight_grad, decay_rate)
             gain = second_update(gain, gain_before, gain_grad, 0.0)
 
-    def sent_and_summed(value):
-        blocks = value.reshape(islands, value.shape[0] // islands, *value.shape[1:])
-        arrived = lax.all_to_all(blocks, "island", split_axis=0, concat_axis=0, tiled=True)
-        return arrived.astype(jnp.float32).sum(axis=0)
-
-    weight_pseudo = sent_and_summed((weight_anchor - weight).astype(jnp.bfloat16)) / islands
-    gain_pseudo = sent_and_summed((gain_anchor - gain[:wide]).astype(jnp.bfloat16)) / islands
+    sent = with_gain(
+        (weight_anchor - weight).astype(jnp.bfloat16).reshape(islands, owned, wide),
+        (gain_anchor - gain[:wide]).astype(jnp.bfloat16).reshape(islands, share),
+    )
+    arrived = lax.all_to_all(sent, "island", split_axis=0, concat_axis=0, tiled=True)
+    pseudo = arrived.astype(jnp.float32).sum(axis=0) / islands
+    weight_pseudo, gain_pseudo = pseudo[:owned], pseudo[owned, :share]
     weight_velocity = outer_momentum * weight_moment + weight_pseudo
     gain_velocity = outer_momentum * gain_moment + gain_pseudo
     weight_updated = weight_master - outer_rate * (weight_pseudo + outer_momentum * weight_velocity)

time: 283 us -> 280 us (0.989)
  blocking collectives: 21 us -> 84.1 us
  waiting for transfers between devices: 147 us -> 103 us
  starting transfers between devices: 47.1 us -> 27.3 us
  other arithmetic: 15.9 us -> 22.4 us
  matrix products: 17.2 us -> 10.9 us
    all_to_all x4 -> x0, waiting for transfers between devices: 52.8 us -> none  [the longest x2 27.2 us: copy_for_each(): return lax.all_to_all(copies, axis, split_axis=0, concat_axis=0, tiled=True)]
    all_to_all x2 -> x3, blocking collectives: 21 us -> 54.5 us  [copy_for_each(): return lax.all_to_all(copies, axis, split_axis=0, concat_axis=0, tiled=True)]
    all_to_all x0 -> x1, blocking collectives: none -> 29.6 us  [per_device(): lax.all_to_all(sent, 'island', split_axis=0, concat_axis=0, tiled=True)]
    all_to_all x4 -> x0, starting transfers between devices: 18.9 us -> none  [the longest x2 10.4 us: copy_for_each(): return lax.all_to_all(copies, axis, split_axis=0, concat_axis=0, tiled=True)]
    ppermute x2, waiting for transfers between devices: 8.64 us -> 23.3 us  [x_swap(): return lax.ppermute(value, 'xh', [(0, 1), (1, 0)])]
    convert_element_type x4 -> x6, other arithmetic: 5.19 us -> 15.2 us  [the longest x1 6.81 us: per_device(): (weight_anchor - weight).astype(jnp.bfloat16).reshape(islands, owned, wide)]
    ppermute x9 -> x8, waiting for transfers between devices: 7.35 us -> 0.93 us  [core_swap(): return lax.ppermute(value, 'c', [(0, 1), (1, 0)])]
    dot_general x4, matrix products: 17.2 us -> 10.9 us  [over_tokens(): jnp.einsum('td,tf->df', rows, residual_grad[:, columns], preferred_elemen...]
  transfers between devices with their start and end apart: 27 -> 22, of which waited for: 14 -> 12; matrix products, arithmetic and copies ran while one was open for 10% -> 6% of each run, Pallas kernels for 0% -> 0%
where the time goes in v1:
time: 280 us
  waiting for transfers between devices  103 us (37%)
  blocking collectives  84.1 us (30%)
  starting transfers between devices  27.3 us (10%)
  other arithmetic  22.4 us (8%)
  local copies, waits for them, and re-layouts  16.2 us (6%)
  Pallas kernels  14.6 us (5%)
  matrix products  10.9 us (4%)
    ppermute x12, waiting for transfers between devices, y_hop(): return lax.ppermute(value, ('y', 'c'), pairs)  79 us
    all_to_all x3, blocking collectives, copy_for_each(): return lax.all_to_all(copies, axis, split_axis=0, concat_axis=0, tiled=True)  54.5 us
    all_to_all x1, blocking collectives, per_device(): lax.all_to_all(sent, 'island', split_axis=0, concat_axis=0, tiled=True)  29.6 us
    ppermute x2, waiting for transfers between devices, x_swap(): return lax.ppermute(value, 'xh', [(0, 1), (1, 0)])  23.3 us
    pallas_call x2, Pallas kernels, forward(): pl.pallas_call(forward_kernel, out_shape=(jax.ShapeDtypeStruct((tokens, f...  14.6 us
    ppermute x12, starting transfers between devices, y_hop(): return lax.ppermute(value, ('y', 'c'), pairs)  13 us
    unnamed x38, local copies, waits for them, and re-layouts  12.1 us
    ppermute x8, starting transfers between devices, core_swap(): return lax.ppermute(value, 'c', [(0, 1), (1, 0)])  11.4 us
  transfers between devices with their start and end apart: 22, of which 12 were waited for; matrix products, arithmetic and copies ran while one was open for 6% of the time, Pallas kernels for 0%

profile of v1, /device:TPU:1, one launch (start us, length us, event | category | flops | bytes accessed | tf_op | source)
XLA Modules:
  0.0 279.8 jit_solution(7593440147968477080)
XLA Ops:
  2.5 33.4 %all_to_all.20.refs_8_ = bf16[8,528,256]{2,1,0:T(8,128)(2,1)S(1)} all-to-all(bf16[8,528,256]{2,1,0:T(8,128)(2,1)S(1)} %broadcast_in_dim.9), channel_id=1, replica_groups=mesh['island'=8,'y'=4,'xh'=2,'c'=2] {'island'}, dimensions={0} | all-to-all | bytes 4325376 | tf_op jit(solution)/shard_map/all_to_all | solution.py:45
  36.0 2.3 collective-permute-start.7
  39.3 2.5 collective-permute-start
  41.8 2.7 collective-permute-start.1
  46.9 13.2 %collective-permute-done.refs_1_ = bf16[96,4096]{1,0:T(8,128)(2,1)} collective-permute-done((bf16[96,4096]{1,0:T(8,128)(2,1)}, bf16[96,4096]{1,0:T(8,128)(2,1)}, u32[]{:S(2)}, u32[]{:S(2)}) %collective-permute-start) | collective-permute-done | bytes 786464 | tf_op jit(solution)/shard_map/ppermute | solution.py:31
  64.4 11.7 %collective-permute-done.4.refs_5_ = bf16[96,4096]{1,0:T(8,128)(2,1)} collective-permute-done((bf16[96,4096]{1,0:T(8,128)(2,1)}, bf16[96,4096]{1,0:T(8,128)(2,1)}, u32[]{:S(2)}, u32[]{:S(2)}) %collective-permute-start.4) | collective-permute-done | bytes 786464 | tf_op jit(solution)/shard_map/ppermute | solution.py:40
  80.5 12.4 %collective-permute-done.2.refs_3_ = bf16[96,4096]{1,0:T(8,128)(2,1)} collective-permute-done((bf16[96,4096]{1,0:T(8,128)(2,1)}, bf16[96,4096]{1,0:T(8,128)(2,1)}, u32[]{:S(2)}, u32[]{:S(2)}) %collective-permute-start.2) | collective-permute-done | bytes 786464 | tf_op jit(solution)/shard_map/ppermute | solution.py:40
  92.9 6.5 %collective-permute-done.5.refs_6_ = bf16[96,4096]{1,0:T(8,128)(2,1)} collective-permute-done((bf16[96,4096]{1,0:T(8,128)(2,1)}, bf16[96,4096]{1,0:T(8,128)(2,1)}, u32[]{:S(2)}, u32[]{:S(2)}) %collective-permute-start.5) | collective-permute-done | bytes 786464 | tf_op jit(solution)/shard_map/ppermute | solution.py:40
  99.4 6.8 %collective-permute-done.6.refs_7_ = bf16[96,4096]{1,0:T(8,128)(2,1)} collective-permute-done((bf16[96,4096]{1,0:T(8,128)(2,1)}, bf16[96,4096]{1,0:T(8,128)(2,1)}, u32[]{:S(2)}, u32[]{:S(2)}) %collective-permute-start.6) | collective-permute-done | bytes 786464 | tf_op jit(solution)/shard_map/ppermute | solution.py:40
  109.0 7.9 %forward.2 = (f32[768,512]{1,0:T(8,128)S(1)}, bf16[768,4096]{1,0:T(8,128)(2,1)S(1)}) custom-call(bf16[96,4096]{1,0:T(8,128)(2,1)} %get-tuple-element.50.refs_0_, bf16[96,4096]{1,0:T(8,128)(2,1)} %collective-permute-done.refs_1_, bf16[96,4096]{1,0:T(8,128)(2,1)} %collective-permute-done.1.refs_2_, bf16[96,4096]{1,0:T(8,128)(2,1)} %collective-permute-done.2.refs_3_, ...), custom_call_target="tpu_custom_call" | custom-call | flops 3221225472 | bytes 16777216 | tf_op jit(solution)/shard_map/forward/pallas_call | solution.py:132
  116.9 2.6 copy-done.5
  120.1 11.9 %all_to_all.21 = f32[8,1,2304]{2,1,0:T(1,128)S(1)} all-to-all(f32[8,1,2304]{2,1,0:T(1,128)S(1)} %broadcast_in_dim.10), channel_id=1, replica_groups=mesh['island'=8,'y'=4,'xh'=2,'c'=2] {'y','xh'}, dimensions={0} | all-to-all | bytes 147456 | tf_op jit(solution)/shard_map/all_to_all | solution.py:45
  133.1 1.7 copy-done.6
  134.9 2.0 convolution_convert_fusion.1
  136.8 4.2 %collective-permute-start.10 = (bf16[4096,256]{1,0:T(8,128)(2,1)S(1)}, bf16[4096,256]{1,0:T(8,128)(2,1)S(1)}, u32[]{:S(2)}, u32[]{:S(2)}) collective-permute-start(bf16[4096,256]{1,0:T(8,128)(2,1)S(1)} %convolution_convert_fusion.1), channel_id=1, source_target_pairs={{0,1},{1,0},{2,3},{3,2},{4,5},{5,4},{6,7},{7,6},{8,9},{9,8},{10,11... | collective-permute-start | bytes 6291464 | tf_op jit(solution)/shard_map/ppermute | solution.py:27
  142.3 1.8 fusion.26
  144.9 5.2 %fusion.35 = (bf16[4096,256]{1,0:T(8,128)(2,1)S(1)}, f32[4096,256]{1,0:T(8,128)}, f32[4096,256]{1,0:T(8,128)}) fusion(bf16[8,512,256]{2,1,0:T(8,128)(2,1)S(1)} %slice.127, f32[4096,256]{1,0:T(8,128)S(1)} %fusion.26, bf16[4096,256]{1,0:T(8,128)(2,1)S(1)} %collective-permute-done.10), kind=kLoop, calls=%fused_computation.93 | loop fusion | flops 12582912 | bytes 18874368 | tf_op jit(solution)/shard_map/convert_element_type | solution.py:245
  151.3 10.1 %collective-permute-done.12.refs_1_ = bf16[96,4096]{1,0:T(8,128)(2,1)S(1)} collective-permute-done((bf16[96,4096]{1,0:T(8,128)(2,1)S(1)}, bf16[96,4096]{1,0:T(8,128)(2,1)S(1)}, u32[]{:S(2)}, u32[]{:S(2)}) %collective-permute-start.12) | collective-permute-done | bytes 786464 | tf_op jit(solution)/shard_map/ppermute | solution.py:31
  162.0 2.3 collective-permute-start.15
  165.5 13.2 %collective-permute-done.16.refs_5_ = bf16[96,4096]{1,0:T(8,128)(2,1)S(1)} collective-permute-done((bf16[96,4096]{1,0:T(8,128)(2,1)S(1)}, bf16[96,4096]{1,0:T(8,128)(2,1)S(1)}, u32[]{:S(2)}, u32[]{:S(2)}) %collective-permute-start.16) | collective-permute-done | bytes 786464 | tf_op jit(solution)/shard_map/ppermute | solution.py:40
  178.7 16.8 %collective-permute-done.14.refs_3_ = bf16[96,4096]{1,0:T(8,128)(2,1)S(1)} collective-permute-done((bf16[96,4096]{1,0:T(8,128)(2,1)S(1)}, bf16[96,4096]{1,0:T(8,128)(2,1)S(1)}, u32[]{:S(2)}, u32[]{:S(2)}) %collective-permute-start.14) | collective-permute-done | bytes 786464 | tf_op jit(solution)/shard_map/ppermute | solution.py:40
  195.6 3.0 %collective-permute-done.17.refs_6_ = bf16[96,4096]{1,0:T(8,128)(2,1)S(1)} collective-permute-done((bf16[96,4096]{1,0:T(8,128)(2,1)S(1)}, bf16[96,4096]{1,0:T(8,128)(2,1)S(1)}, u32[]{:S(2)}, u32[]{:S(2)}) %collective-permute-start.17) | collective-permute-done | bytes 786464 | tf_op jit(solution)/shard_map/ppermute | solution.py:40
  198.5 8.6 %collective-permute-done.18.refs_7_ = bf16[96,4096]{1,0:T(8,128)(2,1)S(1)} collective-permute-done((bf16[96,4096]{1,0:T(8,128)(2,1)S(1)}, bf16[96,4096]{1,0:T(8,128)(2,1)S(1)}, u32[]{:S(2)}, u32[]{:S(2)}) %collective-permute-start.18) | collective-permute-done | bytes 786464 | tf_op jit(solution)/shard_map/ppermute | solution.py:40
  207.1 6.7 %forward.3 = (f32[768,512]{1,0:T(8,128)S(1)}, bf16[768,4096]{1,0:T(8,128)(2,1)S(1)}) custom-call(bf16[96,4096]{1,0:T(8,128)(2,1)S(1)} %get-tuple-element.49.refs_0_, bf16[96,4096]{1,0:T(8,128)(2,1)S(1)} %collective-permute-done.12.refs_1_, bf16[96,4096]{1,0:T(8,128)(2,1)S(1)} %collective-permute-done.13.refs_2_, ...), custom_call_target="tpu_custom_call" | custom-call | flops 3221225472 | bytes 16777216 | tf_op jit(solution)/shard_map/forward/pallas_call | solution.py:132
  213.9 2.6 copy-done.7
  217.1 9.1 %all_to_all.22 = f32[8,1,2304]{2,1,0:T(1,128)S(1)} all-to-all(f32[8,1,2304]{2,1,0:T(1,128)S(1)} %broadcast_in_dim.11), channel_id=1, replica_groups=mesh['island'=8,'y'=4,'xh'=2,'c'=2] {'y','xh'}, dimensions={0} | all-to-all | bytes 147456 | tf_op jit(solution)/shard_map/all_to_all | solution.py:45
  227.3 1.8 copy-done.8
  229.1 3.3 %convolution_convert_fusion = bf16[4096,256]{1,0:T(8,128)(2,1)} fusion(bf16[768,4096]{1,0:T(8,128)(2,1)S(1)} %copy-done.8, bf16[768,512]{1,0:T(8,128)(2,1)S(1)} %get-tuple-element.41), kind=kOutput, calls=%fused_computation.3 | convolution fusion | flops 1611661312 | bytes 8781824 | tf_op jit(solution)/shard_map/td,tf->df/dot_general | solution.py:232
  232.3 3.5 %collective-permute-start.20 = (bf16[4096,256]{1,0:T(8,128)(2,1)}, bf16[4096,256]{1,0:T(8,128)(2,1)}, u32[]{:S(2)}, u32[]{:S(2)}) collective-permute-start(bf16[4096,256]{1,0:T(8,128)(2,1)} %convolution_convert_fusion), channel_id=1, source_target_pairs={{0,1},{1,0},{2,3},{3,2},{4,5},{5,4},{6,7},{7,6},{8,9},{9,8},{10,11... | collective-permute-start | bytes 6291464 | tf_op jit(solution)/shard_map/ppermute | solution.py:27
  235.8 3.9 %fusion.23 = f32[4096,256]{1,0:T(8,128)} fusion(bf16[768,4096]{1,0:T(8,128)(2,1)S(1)} %copy-done.8, bf16[768,512]{1,0:T(8,128)(2,1)S(1)} %get-tuple-element.41), kind=kOutput, calls=%fused_computation.58 | convolution fusion | flops 1610612736 | bytes 10878976 | tf_op jit(solution)/shard_map/td,tf->df/dot_general | solution.py:232
  240.8 6.8 %fusion.3 = bf16[4096,256]{1,0:T(8,128)(2,1)S(1)} fusion(f32[4096,256]{1,0:T(8,128)} %get-tuple-element.14, f32[4096,256]{1,0:T(8,128)} %get-tuple-element.15, f32[4096,256]{1,0:T(8,128)} %fusion.23, bf16[4096,256]{1,0:T(8,128)(2,1)} %collective-permute-done.20, bf16[8,512,256]{2,1,0:T(8,128)(2,1)S(1)} %copy-done.10), kind=kLoop, calls=%fused_computation.10 | loop fusion | flops 23068672 | bytes 18874368 | tf_op jit(solution)/shard_map/convert_element_type | solution.py:254
  247.8 29.6 %all_to_all.23 = bf16[8,528,256]{2,1,0:T(8,128)(2,1)S(1)} all-to-all(bf16[8,528,256]{2,1,0:T(8,128)(2,1)S(1)} %fusion.4), channel_id=1, replica_groups=mesh['island'=8,'y'=4,'xh'=2,'c'=2] {'island'}, dimensions={0} | all-to-all | bytes 4325376 | tf_op jit(solution)/shard_map/all_to_all | solution.py:257
  (107 shorter events, 28.8 us)
Async XLA Ops:
  2.5 35.7 %copy-start.14 = (bf16[1,2,96,4096]{3,2,1,0:T(8,128)(2,1)S(1)}, bf16[1,2,96,4096]{3,2,1,0:T(8,128)(2,1)}, u32[]{:S(2)}) copy-start(bf16[1,2,96,4096]{3,2,1,0:T(8,128)(2,1)} %param.11) | copy-start | bytes 4718596
  36.0 43.6 %copy-start = (bf16[8,528,256]{2,1,0:T(8,128)(2,1)}, bf16[8,528,256]{2,1,0:T(8,128)(2,1)S(1)}, u32[]{:S(2)}) copy-start(bf16[8,528,256]{2,1,0:T(8,128)(2,1)S(1)} %all_to_all.20.refs_8_) | copy-start | bytes 6488068
  36.0 43.7 %collective-permute-start.7 = (bf16[8,528,256]{2,1,0:T(8,128)(2,1)S(1)}, bf16[8,528,256]{2,1,0:T(8,128)(2,1)}, u32[]{:S(2)}, u32[]{:S(2)}) collective-permute-start(bf16[8,528,256]{2,1,0:T(8,128)(2,1)S(1)} %all_to_all.20.refs_8_), channel_id=1, source_target_pairs={{0,1},{1,0},{2,3},{3,2},{4,5},{5,4},{6,7},{7,6},{8,9},{9,8},{10,11... | collective-permute-start | bytes 6488072 | tf_op jit(solution)/shard_map/ppermute | solution.py:27
  39.3 20.8 %collective-permute-start = (bf16[96,4096]{1,0:T(8,128)(2,1)}, bf16[96,4096]{1,0:T(8,128)(2,1)}, u32[]{:S(2)}, u32[]{:S(2)}) collective-permute-start(bf16[96,4096]{1,0:T(8,128)(2,1)} %get-tuple-element.50.refs_0_), channel_id=1, source_target_pairs={{0,2},{2,0},{1,3},{3,1},{4,6},{6,4},{5,7},{7,5},{8,10},{10,8},{9,1... | collective-permute-start | bytes 2359304 | tf_op jit(solution)/shard_map/ppermute | solution.py:31
  41.8 19.6 %collective-permute-start.1 = (bf16[96,4096]{1,0:T(8,128)(2,1)}, bf16[96,4096]{1,0:T(8,128)(2,1)}, u32[]{:S(2)}, u32[]{:S(2)}) collective-permute-start(bf16[96,4096]{1,0:T(8,128)(2,1)} %get-tuple-element.50.refs_0_), channel_id=1, source_target_pairs={{0,4},{1,13},{4,8},{5,1},{8,12},{9,5},{12,0},{13,9},{2,6},{3,15},{... | collective-permute-start | bytes 2359304 | tf_op jit(solution)/shard_map/ppermute | solution.py:40
  46.1 16.6 %collective-permute-start.8 = (bf16[2,8,96,256]{3,2,1,0:T(8,128)(2,1)S(1)}, bf16[2,8,96,256]{3,2,1,0:T(8,128)(2,1)S(1)}, u32[]{:S(2)}, u32[]{:S(2)}) collective-permute-start(bf16[2,8,96,256]{3,2,1,0:T(8,128)(2,1)S(1)} %get-tuple-element.53), channel_id=1, source_target_pairs={{0,1},{1,0},{2,3},{3,2},{4,5},{5,4},{6,7},{7,6},{8,9},{9,8},{10,11... | collective-permute-start | bytes 2359304 | tf_op jit(solution)/shard_map/ppermute | solution.py:27
  46.5 17.6 %collective-permute-start.9 = (bf16[2,8,96,256]{3,2,1,0:T(8,128)(2,1)S(1)}, bf16[2,8,96,256]{3,2,1,0:T(8,128)(2,1)S(1)}, u32[]{:S(2)}, u32[]{:S(2)}) collective-permute-start(bf16[2,8,96,256]{3,2,1,0:T(8,128)(2,1)S(1)} %get-tuple-element.51), channel_id=1, source_target_pairs={{0,1},{1,0},{2,3},{3,2},{4,5},{5,4},{6,7},{7,6},{8,9},{9,8},{10,11... | collective-permute-start | bytes 2359304 | tf_op jit(solution)/shard_map/ppermute | solution.py:27
  60.1 16.0 %collective-permute-start.4 = (bf16[96,4096]{1,0:T(8,128)(2,1)}, bf16[96,4096]{1,0:T(8,128)(2,1)}, u32[]{:S(2)}, u32[]{:S(2)}) collective-permute-start(bf16[96,4096]{1,0:T(8,128)(2,1)} %collective-permute-done.refs_1_), channel_id=1, source_target_pairs={{0,12},{1,5},{4,0},{5,9},{8,4},{9,13},{12,8},{13,1},{2,14},{3,7},{... | collective-permute-start | bytes 2359304 | tf_op jit(solution)/shard_map/ppermute | solution.py:40
  61.4 31.5 %collective-permute-start.2 = (bf16[96,4096]{1,0:T(8,128)(2,1)}, bf16[96,4096]{1,0:T(8,128)(2,1)}, u32[]{:S(2)}, u32[]{:S(2)}) collective-permute-start(bf16[96,4096]{1,0:T(8,128)(2,1)} %get-tuple-element.50.refs_0_), channel_id=1, source_target_pairs={{0,12},{1,5},{4,0},{5,9},{8,4},{9,13},{12,8},{13,1},{2,14},{3,7},{... | collective-permute-start | bytes 2359304 | tf_op jit(solution)/shard_map/ppermute | solution.py:40
  62.7 36.7 %collective-permute-start.3 = (bf16[96,4096]{1,0:T(8,128)(2,1)}, bf16[96,4096]{1,0:T(8,128)(2,1)}, u32[]{:S(2)}, u32[]{:S(2)}) collective-permute-start(bf16[96,4096]{1,0:T(8,128)(2,1)} %collective-permute-done.refs_1_), channel_id=1, source_target_pairs={{0,4},{1,13},{4,8},{5,1},{8,12},{9,5},{12,0},{13,9},{2,6},{3,15},{... | collective-permute-start | bytes 2359304 | tf_op jit(solution)/shard_map/ppermute | solution.py:40
  64.1 35.3 %collective-permute-start.5 = (bf16[96,4096]{1,0:T(8,128)(2,1)}, bf16[96,4096]{1,0:T(8,128)(2,1)}, u32[]{:S(2)}, u32[]{:S(2)}) collective-permute-start(bf16[96,4096]{1,0:T(8,128)(2,1)} %collective-permute-done.1.refs_2_), channel_id=1, source_target_pairs={{0,4},{1,13},{4,8},{5,1},{8,12},{9,5},{12,0},{13,9},{2,6},{3,15},{... | collective-permute-start | bytes 2359304 | tf_op jit(solution)/shard_map/ppermute | solution.py:40
  76.1 30.1 %collective-permute-start.6 = (bf16[96,4096]{1,0:T(8,128)(2,1)}, bf16[96,4096]{1,0:T(8,128)(2,1)}, u32[]{:S(2)}, u32[]{:S(2)}) collective-permute-start(bf16[96,4096]{1,0:T(8,128)(2,1)} %collective-permute-done.4.refs_5_), channel_id=1, source_target_pairs={{0,12},{1,5},{4,0},{5,9},{8,4},{9,13},{12,8},{13,1},{2,14},{3,7},{... | collective-permute-start | bytes 2359304 | tf_op jit(solution)/shard_map/ppermute | solution.py:40
  109.0 10.5 %copy-start.12 = (bf16[1,8,96,512]{3,2,1,0:T(8,128)(2,1)S(1)}, bf16[1,8,96,512]{3,2,1,0:T(8,128)(2,1)}, u32[]{:S(2)}) copy-start(bf16[1,8,96,512]{3,2,1,0:T(8,128)(2,1)} %get-tuple-element.46) | copy-start | bytes 2359300
  132.1 2.8 copy-start.6
  134.9 6.6 %copy-start.2 = (bf16[8,528,256]{2,1,0:T(8,128)(2,1)S(1)}, bf16[8,528,256]{2,1,0:T(8,128)(2,1)}, u32[]{:S(2)}) copy-start(bf16[8,528,256]{2,1,0:T(8,128)(2,1)} %copy-done) | copy-start | bytes 6488068
  136.8 8.0 %collective-permute-start.10 = (bf16[4096,256]{1,0:T(8,128)(2,1)S(1)}, bf16[4096,256]{1,0:T(8,128)(2,1)S(1)}, u32[]{:S(2)}, u32[]{:S(2)}) collective-permute-start(bf16[4096,256]{1,0:T(8,128)(2,1)S(1)} %convolution_convert_fusion.1), channel_id=1, source_target_pairs={{0,1},{1,0},{2,3},{3,2},{4,5},{5,4},{6,7},{7,6},{8,9},{9,8},{10,11... | collective-permute-start | bytes 6291464 | tf_op jit(solution)/shard_map/ppermute | solution.py:27
  141.0 20.3 %collective-permute-start.12 = (bf16[96,4096]{1,0:T(8,128)(2,1)S(1)}, bf16[96,4096]{1,0:T(8,128)(2,1)S(1)}, u32[]{:S(2)}, u32[]{:S(2)}) collective-permute-start(bf16[96,4096]{1,0:T(8,128)(2,1)S(1)} %get-tuple-element.49.refs_0_), channel_id=1, source_target_pairs={{0,2},{2,0},{1,3},{3,1},{4,6},{6,4},{5,7},{7,5},{8,10},{10,8},{9,1... | collective-permute-start | bytes 2359304 | tf_op jit(solution)/shard_map/ppermute | solution.py:31
  141.7 3.2 %copy-start.9 = (bf16[8,512,256]{2,1,0:T(8,128)(2,1)}, bf16[8,512,256]{2,1,0:T(8,128)(2,1)S(1)}, u32[]{:S(2)}) copy-start(bf16[8,512,256]{2,1,0:T(8,128)(2,1)S(1)} %slice.127) | copy-start | bytes 6291460
  141.7 3.2 %collective-permute-start.11 = (f32[512]{0:T(512)S(1)}, f32[512]{0:T(512)S(1)}, u32[]{:S(2)}, u32[]{:S(2)}) collective-permute-start(f32[512]{0:T(512)S(1)} %get-tuple-element.44), channel_id=1, source_target_pairs={{0,1},{1,0},{2,3},{3,2},{4,5},{5,4},{6,7},{7,6},{8,9},{9,8},{10,11... | collective-permute-start | bytes 6152 | tf_op jit(solution)/shard_map/ppermute | solution.py:27
  144.8 62.3 %copy-start.3 = (bf16[1,8,96,512]{3,2,1,0:T(8,128)(2,1)S(1)}, bf16[1,8,96,512]{3,2,1,0:T(8,128)(2,1)}, u32[]{:S(2)}) copy-start(bf16[1,8,96,512]{3,2,1,0:T(8,128)(2,1)} %get-tuple-element.47) | copy-start | bytes 2359300
  150.0 57.1 %collective-permute-start.19 = (bf16[8,512,256]{2,1,0:T(8,128)(2,1)S(1)}, bf16[8,512,256]{2,1,0:T(8,128)(2,1)S(1)}, u32[]{:S(2)}, u32[]{:S(2)}) collective-permute-start(bf16[8,512,256]{2,1,0:T(8,128)(2,1)S(1)} %bitcast.44), channel_id=1, source_target_pairs={{0,1},{1,0},{2,3},{3,2},{4,5},{5,4},{6,7},{7,6},{8,9},{9,8},{10,11... | collective-permute-start | bytes 6291464 | tf_op jit(solution)/shard_map/ppermute | solution.py:27
  150.4 13.9 %collective-permute-start.13 = (bf16[96,4096]{1,0:T(8,128)(2,1)S(1)}, bf16[96,4096]{1,0:T(8,128)(2,1)S(1)}, u32[]{:S(2)}, u32[]{:S(2)}) collective-permute-start(bf16[96,4096]{1,0:T(8,128)(2,1)S(1)} %get-tuple-element.49.refs_0_), channel_id=1, source_target_pairs={{0,4},{1,13},{4,8},{5,1},{8,12},{9,5},{12,0},{13,9},{2,6},{3,15},{... | collective-permute-start | bytes 2359304 | tf_op jit(solution)/shard_map/ppermute | solution.py:40
  161.4 17.3 %collective-permute-start.16 = (bf16[96,4096]{1,0:T(8,128)(2,1)S(1)}, bf16[96,4096]{1,0:T(8,128)(2,1)S(1)}, u32[]{:S(2)}, u32[]{:S(2)}) collective-permute-start(bf16[96,4096]{1,0:T(8,128)(2,1)S(1)} %collective-permute-done.12.refs_1_), channel_id=1, source_target_pairs={{0,12},{1,5},{4,0},{5,9},{8,4},{9,13},{12,8},{13,1},{2,14},{3,7},{... | collective-permute-start | bytes 2359304 | tf_op jit(solution)/shard_map/ppermute | solution.py:40
  161.6 33.9 %collective-permute-start.14 = (bf16[96,4096]{1,0:T(8,128)(2,1)S(1)}, bf16[96,4096]{1,0:T(8,128)(2,1)S(1)}, u32[]{:S(2)}, u32[]{:S(2)}) collective-permute-start(bf16[96,4096]{1,0:T(8,128)(2,1)S(1)} %get-tuple-element.49.refs_0_), channel_id=1, source_target_pairs={{0,12},{1,5},{4,0},{5,9},{8,4},{9,13},{12,8},{13,1},{2,14},{3,7},{... | collective-permute-start | bytes 2359304 | tf_op jit(solution)/shard_map/ppermute | solution.py:40
  162.0 36.5 %collective-permute-start.15 = (bf16[96,4096]{1,0:T(8,128)(2,1)S(1)}, bf16[96,4096]{1,0:T(8,128)(2,1)S(1)}, u32[]{:S(2)}, u32[]{:S(2)}) collective-permute-start(bf16[96,4096]{1,0:T(8,128)(2,1)S(1)} %collective-permute-done.12.refs_1_), channel_id=1, source_target_pairs={{0,4},{1,13},{4,8},{5,1},{8,12},{9,5},{12,0},{13,9},{2,6},{3,15},{... | collective-permute-start | bytes 2359304 | tf_op jit(solution)/shard_map/ppermute | solution.py:40
  164.3 34.2 %collective-permute-start.17 = (bf16[96,4096]{1,0:T(8,128)(2,1)S(1)}, bf16[96,4096]{1,0:T(8,128)(2,1)S(1)}, u32[]{:S(2)}, u32[]{:S(2)}) collective-permute-start(bf16[96,4096]{1,0:T(8,128)(2,1)S(1)} %collective-permute-done.13.refs_2_), channel_id=1, source_target_pairs={{0,4},{1,13},{4,8},{5,1},{8,12},{9,5},{12,0},{13,9},{2,6},{3,15},{... | collective-permute-start | bytes 2359304 | tf_op jit(solution)/shard_map/ppermute | solution.py:40
  178.7 28.4 %collective-permute-start.18 = (bf16[96,4096]{1,0:T(8,128)(2,1)S(1)}, bf16[96,4096]{1,0:T(8,128)(2,1)S(1)}, u32[]{:S(2)}, u32[]{:S(2)}) collective-permute-start(bf16[96,4096]{1,0:T(8,128)(2,1)S(1)} %collective-permute-done.16.refs_5_), channel_id=1, source_target_pairs={{0,12},{1,5},{4,0},{5,9},{8,4},{9,13},{12,8},{13,1},{2,14},{3,7},{... | collective-permute-start | bytes 2359304 | tf_op jit(solution)/shard_map/ppermute | solution.py:40
  207.1 9.4 %copy-start.11 = (bf16[1,8,96,512]{3,2,1,0:T(8,128)(2,1)S(1)}, bf16[1,8,96,512]{3,2,1,0:T(8,128)(2,1)}, u32[]{:S(2)}) copy-start(bf16[1,8,96,512]{3,2,1,0:T(8,128)(2,1)} %get-tuple-element.45) | copy-start | bytes 2359300
  226.3 2.8 copy-start.8
  232.3 8.5 %collective-permute-start.20 = (bf16[4096,256]{1,0:T(8,128)(2,1)}, bf16[4096,256]{1,0:T(8,128)(2,1)}, u32[]{:S(2)}, u32[]{:S(2)}) collective-permute-start(bf16[4096,256]{1,0:T(8,128)(2,1)} %convolution_convert_fusion), channel_id=1, source_target_pairs={{0,1},{1,0},{2,3},{3,2},{4,5},{5,4},{6,7},{7,6},{8,9},{9,8},{10,11... | collective-permute-start | bytes 6291464 | tf_op jit(solution)/shard_map/ppermute | solution.py:27
  235.8 5.0 %copy-start.10 = (bf16[8,512,256]{2,1,0:T(8,128)(2,1)S(1)}, bf16[8,512,256]{2,1,0:T(8,128)(2,1)}, u32[]{:S(2)}) copy-start(bf16[8,512,256]{2,1,0:T(8,128)(2,1)} %copy-done.9) | copy-start | bytes 6291460
  235.8 4.1 %collective-permute-start.21 = (f32[512]{0:T(512)S(1)}, f32[512]{0:T(512)S(1)}, u32[]{:S(2)}, u32[]{:S(2)}) collective-permute-start(f32[512]{0:T(512)S(1)} %get-tuple-element.42), channel_id=1, source_target_pairs={{0,1},{1,0},{2,3},{3,2},{4,5},{5,4},{6,7},{7,6},{8,9},{9,8},{10,11... | collective-permute-start | bytes 6152 | tf_op jit(solution)/shard_map/ppermute | solution.py:27
  (9 other events, 13.6 us)

commit v2 on v1

v2 whole, which is shorter than its diff:
```python
import jax
import jax.numpy as jnp
from jax import lax
from jax.experimental import pallas as pl
from jax.experimental.pallas import tpu as pltpu
from jax.sharding import Mesh
from jax.sharding import PartitionSpec as P


D = 4096
STEPS = 2
SHARD = ("y", "xh", "c")
ISLAND = ("xl", "z")
SHARD_ISLAND = ("y", "xh", "c", "xl", "z")


norm_epsilon = 1e-05
inner_rate = 0.05
beta_one = 0.9
beta_two = 0.95
adam_epsilon = 0.3
decay_rate = 0.1
outer_rate = 0.7
outer_momentum = 0.9


def core_swap(value):
    return lax.ppermute(value, "c", [(0, 1), (1, 0)])


def x_swap(value):
    return lax.ppermute(value, "xh", [(0, 1), (1, 0)])


def y_hop(value, way):
    pairs = []
    for y in range(4):
        for c in range(2):
            to = (y + (way if c == 0 else -way)) % 4
            pairs.append((y * 2 + c, to * 2 + c))
    return lax.ppermute(value, ("y", "c"), pairs)


def copy_for_each(value, axis):
    copies = jnp.broadcast_to(value, (lax.axis_size(axis), *value.shape))
    return lax.all_to_all(copies, axis, split_axis=0, concat_axis=0, tiled=True)


def gathered_pieces(own):
    a = y_hop(own, 1)
    b = y_hop(own, -1)
    x = x_swap(own)
    a2 = y_hop(x, 1)
    b2 = y_hop(x, -1)
    f = y_hop(a, 1)
    f2 = y_hop(b2, -1)
    return (own, x, a, b, a2, b2, f, f2)


BLOCK = 96
VMEM_LIMIT = 44 * 1024 * 1024


LETTERS = "oxabcefg"
SOON = ("oxabf", "oxabce")
LATE = ("ceg", "fg")


def forward_kernel(letters, pieces, weight, weight_other, flow, residual_out, rows_out, rows, weights, made, came, loaded, left, sent):
    y, xh, c = lax.axis_index("y"), lax.axis_index("xh"), lax.axis_index("c")
    d = 1 - 2 * c
    before, after, across = (y + 4 - d) % 4, (y + 4 + d) % 4, (y + 2) % 4
    blocks = (
        (y, xh), (y, 1 - xh), (before, xh), (after, xh),
        (before, 1 - xh), (after, 1 - xh), (across, xh), (across, 1 - xh),
    )
    places = []
    for letter in letters:
        py, px = blocks[LETTERS.index(letter)]
        places.append(pl.ds(pl.multiple_of((py * 2 + px) * BLOCK, BLOCK), BLOCK))
    own = [pl.ds(at * BLOCK, BLOCK) for at in range(len(letters))]
    islands, owned, wide = weights.shape[1:]

    def loads_of(half, source):
        if len(source.shape) == 3:
            return [pltpu.make_async_copy(source, weights.at[half], loaded.at[half, 0])]
        return [
            pltpu.make_async_copy(
                source.at[:, xl, pl.ds(0, owned)],
                weights.at[half, pl.ds(xl * (islands // 2), islands // 2)],
                loaded.at[half, xl],
            )
            for xl in range(2)
        ]

    loads = [loads_of(0, weight), loads_of(1, weight_other)]
    takes = [
        pltpu.make_async_copy(source, rows.at[at], came.at[i])
        for i, (at, source) in enumerate(zip(own, pieces))
    ]
    gives = [
        pltpu.make_async_copy(rows.at[at], rows_out.at[to], left.at[i])
        for i, (at, to) in enumerate(zip(own, places))
    ]
    sends = [
        pltpu.make_async_copy(made.at[at], residual_out.at[to], sent.at[i])
        for i, (at, to) in enumerate(zip(own, places))
    ]
    for copy in (*loads[0], *takes, *loads[1]):
        copy.start()
    for take, give in zip(takes, gives):
        take.wait()
        give.start()
    for half in range(2):
        for load in loads[half]:
            load.wait()
        projected = jnp.dot(
            rows[...],
            weights[half].reshape(islands * owned, wide),
            preferred_element_type=jnp.float32,
        )
        columns = slice(half * wide, (half + 1) * wide)
        for at, (mine, to) in enumerate(zip(own, places)):
            made[mine, columns] = (
                flow[to, columns].astype(jnp.float32)
                + projected[at * BLOCK : (at + 1) * BLOCK] * D ** (-0.5)
            )
    for send in sends:
        send.start()
    for copy in (*gives, *sends):
        copy.wait()


def forward(letters, pieces, weight, weight_other, flow, earlier=()):
    anywhere = pl.BlockSpec(memory_space=pl.ANY)
    inside = pl.BlockSpec(memory_space=pltpu.VMEM)
    count = len(letters)
    tokens, features = flow.shape
    islands, owned, wide = 8, D // 8, features // 2

    def kernel(*refs):
        rest = refs[count : count + 3] + refs[count + 3 + len(earlier) :]
        forward_kernel(letters, refs[:count], *rest)

    return pl.pallas_call(
        kernel,
        out_shape=(
            jax.ShapeDtypeStruct((tokens, features), jnp.float32),
            jax.ShapeDtypeStruct((tokens, D), jnp.bfloat16),
        ),
        in_specs=[anywhere] * (count + 2) + [inside] + [anywhere] * len(earlier),
        out_specs=(anywhere, anywhere),
        scratch_shapes=[
            pltpu.VMEM((count * BLOCK, D), jnp.bfloat16),
            pltpu.VMEM((2, islands, owned, wide), jnp.bfloat16),
            pltpu.VMEM((count * BLOCK, features), jnp.float32),
            pltpu.SemaphoreType.DMA((count,)),
            pltpu.SemaphoreType.DMA((2, 2)),
            pltpu.SemaphoreType.DMA((count,)),
            pltpu.SemaphoreType.DMA((count,)),
        ],
        input_output_aliases={count + 3 + i: i for i in range(len(earlier))},
        compiler_params=pltpu.CompilerParams(vmem_limit_bytes=VMEM_LIMIT),
        cost_estimate=pl.CostEstimate(
            flops=2 * count * BLOCK * D * features,
            bytes_accessed=4 * count * BLOCK * D + 2 * D * features,
            transcendentals=0,
        ),
        name="forward",
    )(*pieces, weight, weight_other, flow, *earlier)


def first_update(param, gradient, decay):
    return param - inner_rate * (gradient / (jnp.abs(gradient) + adam_epsilon) + decay * param)


def second_change(anchor, change, before, gradient, decay):
    beside = (1.0 - beta_one) / (1.0 - beta_one**2)
    first_hat = (beta_one * beside) * before + beside * gradient
    beside = (1.0 - beta_two) / (1.0 - beta_two**2)
    second_hat = (beta_two * beside) * (before * before) + beside * (gradient * gradient)
    root = second_hat * lax.rsqrt(jnp.maximum(second_hat, 1e-37))
    param = anchor - change
    return change + inner_rate * (first_hat / (root + adam_epsilon) + decay * param)


def per_device(weight_master, gain_master, weight_moment, gain_moment, attended, stream, targets):
    islands = lax.axis_size(ISLAND)
    width_scale = D ** (-0.5)
    c = lax.axis_index("c")
    wide = weight_master.shape[1]

    pieces = [gathered_pieces(attended[0][step]) for step in range(STEPS)]

    def with_gain(weight_rows, gain_rows):
        filled = [(0, 0)] * (gain_rows.ndim - 1) + [(0, 15), (0, wide - gain_rows.shape[-1])]
        return jnp.concatenate([weight_rows, jnp.pad(gain_rows[..., None, :], filled)], axis=-2)

    owned, share = weight_master.shape[0], gain_master.shape[0]
    packed = with_gain(weight_master.astype(jnp.bfloat16), gain_master.astype(jnp.bfloat16))
    beyond = lax.ppermute(packed, "xl", [(0, 1), (1, 0)])
    low = lax.axis_index("xl") == 0
    pair = jnp.stack([jnp.where(low, packed, beyond), jnp.where(low, beyond, packed)])
    packed = copy_for_each(pair, "z")
    packed_other = core_swap(packed)

    def in_island_order(value):
        return jnp.swapaxes(value, 0, 1)

    slabs = [packed[z, xl, :owned] for xl in range(2) for z in range(4)]
    anchor_low = lax.optimization_barrier(jnp.concatenate(slabs, axis=0))
    gain_anchor = in_island_order(packed[:, :, owned, :share]).reshape(wide).astype(jnp.float32)
    gain_other = in_island_order(packed_other[:, :, owned, :share]).reshape(wide)
    gain_other = gain_other.astype(jnp.float32)

    def token_half(value):
        blocks = value[0].reshape(STEPS, 8, 2, 96, wide)
        mine = lax.dynamic_index_in_dim(blocks, c, axis=2, keepdims=False)
        theirs = lax.dynamic_index_in_dim(blocks, 1 - c, axis=2, keepdims=False)
        both = jnp.concatenate([mine, core_swap(theirs)], axis=-1)
        return both.reshape(STEPS, 768, 2 * wide)

    stream_half = token_half(stream)
    target_half = token_half(targets)

    weight_anchor = anchor_low.astype(jnp.float32)
    gain = jnp.concatenate([gain_anchor, gain_other])
    for step in range(STEPS):
        if step == 0:
            held, held_other = packed, packed_other
        else:
            held = weight_low.reshape(islands, owned, wide)
            held_other = core_swap(held)
        earlier = ()
        for letters in (SOON[step], LATE[step]):
            some = [pieces[step][LETTERS.index(letter)] for letter in letters]
            earlier = forward(letters, some, held, held_other, stream_half[step], earlier)
        residual, rows = earlier
        goal = target_half[step].astype(jnp.float32)
        scaled = residual * gain
        sums = [
            jnp.sum(residual * residual, axis=1),
            jnp.sum(scaled * scaled, axis=1),
            jnp.sum(goal * scaled, axis=1),
        ]
        sums = jnp.concatenate(sums).reshape(1, -1)
        totals = copy_for_each(sums, ("y", "xh"))
        totals = jnp.sum(totals, axis=0).reshape(3, -1)
        inverse = lax.rsqrt(totals[0] / D + norm_epsilon)
        slope = (inverse * totals[1] - totals[2])[:, None]
        inverse = inverse[:, None]
        normed = residual * inverse * gain
        loss_grad = lax.optimization_barrier((normed - goal).astype(jnp.bfloat16))
        loss_grad = loss_grad.astype(jnp.float32)
        residual_grad = (
            inverse * (loss_grad * gain) - residual * inverse * inverse * inverse * slope / D
        ).astype(jnp.bfloat16)
        gain_grad = jnp.sum(loss_grad * residual * inverse, axis=0)

        def over_tokens(columns):
            return jnp.einsum(
                "td,tf->df", rows, residual_grad[:, columns], preferred_element_type=jnp.float32
            )

        other = over_tokens(slice(wide, None)).astype(jnp.bfloat16)
        other = core_swap(other)
        mine = lax.optimization_barrier(over_tokens(slice(0, wide)))
        weight_grad = (mine + other.astype(jnp.float32)) * width_scale
        gain_other = core_swap(gain_grad)
        gain_grad = gain_grad + jnp.concatenate([gain_other[wide:], gain_other[:wide]])
        if step == 0:
            weight_low = first_update(weight_anchor, weight_grad, decay_rate)
            weight_change = (weight_anchor - weight_low).astype(jnp.bfloat16)
            weight_before = weight_grad.astype(jnp.bfloat16)
            weight_low = weight_low.astype(jnp.bfloat16)
            gain_first = gain
            gain_before, gain = gain_grad, first_update(gain, gain_grad, 0.0)
            weight_change, weight_before, weight_low = lax.optimization_barrier(
                (weight_change, weight_before, weight_low)
            )
        else:
            weight_change = second_change(
                weight_anchor,
                weight_change.astype(jnp.float32),
                weight_before.astype(jnp.float32),
                weight_grad,
                decay_rate,
            )
            gain_change = second_change(gain_first, gain_first - gain, gain_before, gain_grad, 0.0)

    sent = with_gain(
        weight_change.astype(jnp.bfloat16).reshape(islands, owned, wide),
        gain_change[:wide].astype(jnp.bfloat16).reshape(islands, share),
    )
    arrived = lax.all_to_all(sent, ISLAND, split_axis=0, concat_axis=0, tiled=True)
    pseudo = arrived.astype(jnp.float32).sum(axis=0) / islands
    weight_pseudo, gain_pseudo = pseudo[:owned], pseudo[owned, :share]
    weight_velocity = outer_momentum * weight_moment + weight_pseudo
    gain_velocity = outer_momentum * gain_moment + gain_pseudo
    weight_updated = weight_master - outer_rate * (weight_pseudo + outer_momentum * weight_velocity)
    gain_updated = gain_master - outer_rate * (gain_pseudo + outer_momentum * gain_velocity)
    return (weight_updated, gain_updated, weight_velocity, gain_velocity)


def solution(mesh):
    torus = Mesh(mesh.devices.reshape(2, 4, 4, 2, 2), (*ISLAND, *SHARD))
    return jax.shard_map(
        per_device,
        mesh=torus,
        in_specs=(
            P(ISLAND, SHARD),
            P(SHARD_ISLAND),
            P(ISLAND, SHARD),
            P(SHARD_ISLAND),
            P(ISLAND, None, SHARD, None),
            P(ISLAND, None, None, SHARD),
            P(ISLAND, None, None, SHARD),
        ),
        out_specs=(P(ISLAND, SHARD), P(SHARD_ISLAND), P(ISLAND, SHARD), P(SHARD_ISLAND)),
        check_vma=False,
    )
```

time: 280 us -> 278 us (level)
  waiting for transfers between devices: 103 us -> 87.9 us
  blocking collectives: 84.1 us -> 69.1 us
  starting transfers between devices: 27.3 us -> 41.3 us
  Pallas kernels: 14.6 us -> 26.2 us
  matrix products: 10.9 us -> 16.8 us
    ppermute x12, waiting for transfers between devices: 79 us -> 60.9 us  [y_hop(): return lax.ppermute(value, ('y', 'c'), pairs)]
    all_to_all x3 -> x2, blocking collectives: 54.5 us -> 39.5 us  [copy_for_each(): return lax.all_to_all(copies, axis, split_axis=0, concat_axis=0, tiled=True)]
    pallas_call x2 -> x4, Pallas kernels: 14.6 us -> 26.2 us  [forward(): pl.pallas_call(kernel, out_shape=(jax.ShapeDtypeStruct((tokens, features)...]
    ppermute x2, waiting for transfers between devices: 23.3 us -> 13.3 us  [x_swap(): return lax.ppermute(value, 'xh', [(0, 1), (1, 0)])]
    all_to_all x0 -> x1, waiting for transfers between devices: none -> 6 us  [copy_for_each(): return lax.all_to_all(copies, axis, split_axis=0, concat_axis=0, tiled=True)]
    dot_general x4, matrix products: 10.9 us -> 16.8 us  [over_tokens(): jnp.einsum('td,tf->df', rows, residual_grad[:, columns], preferred_elemen...]
    ppermute x0 -> x1, waiting for transfers between devices: none -> 5.77 us  [per_device(): beyond = lax.ppermute(packed, 'xl', [(0, 1), (1, 0)])]
    all_to_all x0 -> x1, starting transfers between devices: none -> 5.67 us  [copy_for_each(): return lax.all_to_all(copies, axis, split_axis=0, concat_axis=0, tiled=True)]
  transfers between devices with their start and end apart: 22 -> 24, of which waited for: 12 -> 13; matrix products, arithmetic and copies ran while one was open for 6% -> 10% of each run, Pallas kernels for 0% -> 8%
where the time goes in v2:
time: 278 us; the launch traced here: 277 us
  waiting for transfers between devices  87.9 us (32%)
  blocking collectives  69.1 us (25%)
  starting transfers between devices  41.3 us (15%)
  Pallas kernels  26.2 us (9%)
  other arithmetic  20.9 us (8%)
  matrix products  16.8 us (6%)
  local copies, waits for them, and re-layouts  14.1 us (5%)
    ppermute x12, waiting for transfers between devices, y_hop(): return lax.ppermute(value, ('y', 'c'), pairs)  60.9 us
    all_to_all x2, blocking collectives, copy_for_each(): return lax.all_to_all(copies, axis, split_axis=0, concat_axis=0, tiled=True)  39.5 us
    all_to_all x1, blocking collectives, per_device(): lax.all_to_all(sent, ISLAND, split_axis=0, concat_axis=0, tiled=True)  29.6 us
    pallas_call x4, Pallas kernels, forward(): pl.pallas_call(kernel, out_shape=(jax.ShapeDtypeStruct((tokens, features)...  26.2 us
    dot_general x4, matrix products, over_tokens(): jnp.einsum('td,tf->df', rows, residual_grad[:, columns], preferred_elemen...  16.8 us
    ppermute x8, starting transfers between devices, core_swap(): return lax.ppermute(value, 'c', [(0, 1), (1, 0)])  14.7 us
    ppermute x12, starting transfers between devices, y_hop(): return lax.ppermute(value, ('y', 'c'), pairs)  13.3 us
    ppermute x2, waiting for transfers between devices, x_swap(): return lax.ppermute(value, 'xh', [(0, 1), (1, 0)])  13.3 us
  transfers between devices with their start and end apart: 24, of which 13 were waited for; matrix products, arithmetic and copies ran while one was open for 10% of the time, Pallas kernels for 8%

profile of v2, /device:TPU:1, one launch (start us, length us, event | category | flops | bytes accessed | tf_op | source)
XLA Modules:
  0.0 277.4 jit_solution(15417999530067150697)
XLA Ops:
  2.4 2.1 collective-permute-start
  4.5 5.8 %collective-permute-done = bf16[528,256]{1,0:T(8,128)(2,1)S(1)} collective-permute-done((bf16[528,256]{1,0:T(8,128)(2,1)S(1)}, bf16[528,256]{1,0:T(8,128)(2,1)S(1)}, u32[]{:S(2)}, u32[]{:S(2)}) %collective-permute-start) | collective-permute-done | bytes 270368 | tf_op jit(solution)/shard_map/ppermute | solution.py:201
  10.6 30.4 %all_to_all.20.refs_5_.refs_3_ = bf16[4,2,528,256]{3,2,1,0:T(8,128)(2,1)S(1)} all-to-all(bf16[4,2,528,256]{3,2,1,0:T(8,128)(2,1)S(1)} %broadcast_in_dim.9), channel_id=1, replica_groups=mesh['xl'=2,'z'=4,'y'=4,'xh'=2,'c'=2] {'z'}, dimensions={0} | all-to-all | bytes 4325376 | tf_op jit(solution)/shard_map/all_to_all | solution.py:46
  41.0 3.0 %collective-permute-start.5 = (bf16[4,2,528,256]{3,2,1,0:T(8,128)(2,1)S(1)}, bf16[4,2,528,256]{3,2,1,0:T(8,128)(2,1)}, u32[]{:S(2)}, u32[]{:S(2)}) collective-permute-start(bf16[4,2,528,256]{3,2,1,0:T(8,128)(2,1)S(1)} %all_to_all.20.refs_5_.refs_3_), channel_id=1, source_target_pairs={{0,1},{1,0},{2,3},{3,2},{4,5},{5,4},{6,7},{7,6},{8,9},{9,8},{10,11... | collective-permute-start | bytes 6488072 | tf_op jit(solution)/shard_map/ppermute | solution.py:28
  45.2 2.7 collective-permute-start.1
  50.0 2.7 collective-permute-start.7
  52.9 13.3 %collective-permute-done.1.refs_1_ = bf16[96,4096]{1,0:T(8,128)(2,1)} collective-permute-done((bf16[96,4096]{1,0:T(8,128)(2,1)}, bf16[96,4096]{1,0:T(8,128)(2,1)}, u32[]{:S(2)}, u32[]{:S(2)}) %collective-permute-start.1) | collective-permute-done | bytes 786464 | tf_op jit(solution)/shard_map/ppermute | solution.py:32
  70.4 11.8 %collective-permute-done.3.refs_1_ = bf16[96,4096]{1,0:T(8,128)(2,1)} collective-permute-done((bf16[96,4096]{1,0:T(8,128)(2,1)}, bf16[96,4096]{1,0:T(8,128)(2,1)}, u32[]{:S(2)}, u32[]{:S(2)}) %collective-permute-start.3) | collective-permute-done | bytes 786464 | tf_op jit(solution)/shard_map/ppermute | solution.py:41
  85.6 2.8 collective-permute-start.14
  89.2 9.9 %collective-permute-done.8.refs_3_ = bf16[96,4096]{1,0:T(8,128)(2,1)} collective-permute-done((bf16[96,4096]{1,0:T(8,128)(2,1)}, bf16[96,4096]{1,0:T(8,128)(2,1)}, u32[]{:S(2)}, u32[]{:S(2)}) %collective-permute-start.8) | collective-permute-done | bytes 786464 | tf_op jit(solution)/shard_map/ppermute | solution.py:41
  100.3 9.3 %forward.4 = (f32[768,512]{1,0:T(8,128)S(1)}, bf16[768,4096]{1,0:T(8,128)(2,1)}) custom-call(bf16[96,4096]{1,0:T(8,128)(2,1)} %get-tuple-element.57.refs_0_, bf16[96,4096]{1,0:T(8,128)(2,1)} %collective-permute-done.1.refs_1_, bf16[96,4096]{1,0:T(8,128)(2,1)} %collective-permute-done.7.refs_2_, bf16[96,4096]{1,0:T(8,128)(2,1)} %collective-permute-done.8.refs_3_, ...), custom_call_target="tpu_custom_call" | custom-call | flops 2013265920 | bytes 12058624 | tf_op jit(solution)/shard_map/forward/pallas_call | solution.py:145
  109.6 2.7 collective-permute-done.4.refs_2_
  112.3 5.8 %forward.5 = (f32[768,512]{1,0:T(8,128)S(1)}, bf16[768,4096]{1,0:T(8,128)(2,1)}) custom-call(bf16[96,4096]{1,0:T(8,128)(2,1)} %collective-permute-done.2.refs_0_, bf16[96,4096]{1,0:T(8,128)(2,1)} %collective-permute-done.3.refs_1_, bf16[96,4096]{1,0:T(8,128)(2,1)} %collective-permute-done.4.refs_2_, ...), custom_call_target="tpu_custom_call", output_to_operand_aliasing={{0}: (6, {}), {1}: (7, {})} | custom-call | flops 1207959552 | bytes 8912896 | tf_op jit(solution)/shard_map/forward/pallas_call | solution.py:145
  120.5 5.7 %all-to-all-start.1 = ((f32[8,1,2304]{2,1,0:T(1,128)}), f32[8,1,2304]{2,1,0:T(1,128)S(1)}, u32[]{:S(2)}, u32[]{:S(2)}) async-start(f32[8,1,2304]{2,1,0:T(1,128)} %broadcast_in_dim.10), calls=%async_computation.1 | async-start | bytes 147456 | tf_op jit(solution)/shard_map/all_to_all | solution.py:46
  126.9 6.0 %all-to-all-done.1 = f32[8,1,2304]{2,1,0:T(1,128)S(1)} async-done(((f32[8,1,2304]{2,1,0:T(1,128)}), f32[8,1,2304]{2,1,0:T(1,128)S(1)}, u32[]{:S(2)}, u32[]{:S(2)}) %all-to-all-start.1) | async-done | bytes 73760 | tf_op jit(solution)/shard_map/all_to_all | solution.py:46
  133.0 2.0 fusion.25
  135.8 4.8 %convolution_convert_fusion.1 = bf16[4096,256]{1,0:T(8,128)(2,1)S(1)} fusion(bf16[768,4096]{1,0:T(8,128)(2,1)} %get-tuple-element.17, bf16[768,512]{1,0:T(8,128)(2,1)S(1)} %get-tuple-element.48), kind=kOutput, calls=%fused_computation.8 | convolution fusion | flops 1611661312 | bytes 8781824 | tf_op jit(solution)/shard_map/td,tf->df/dot_general | solution.py:261
  140.6 6.2 %collective-permute-start.11 = (bf16[4096,256]{1,0:T(8,128)(2,1)S(1)}, bf16[4096,256]{1,0:T(8,128)(2,1)S(1)}, u32[]{:S(2)}, u32[]{:S(2)}) collective-permute-start(bf16[4096,256]{1,0:T(8,128)(2,1)S(1)} %convolution_convert_fusion.1), channel_id=1, source_target_pairs={{0,1},{1,0},{2,3},{3,2},{4,5},{5,4},{6,7},{7,6},{8,9},{9,8},{10,11... | collective-permute-start | bytes 6291464 | tf_op jit(solution)/shard_map/ppermute | solution.py:28
  150.7 3.5 %fusion.59 = (bf16[4096,256]{1,0:T(8,128)(2,1)S(1)}, bf16[4096,256]{1,0:T(8,128)(2,1)}, bf16[4096,256]{1,0:T(8,128)(2,1)}) fusion(f32[4096,256]{1,0:T(8,128)S(1)} %fusion.35, bf16[4096,256]{1,0:T(8,128)(2,1)S(1)} %collective-permute-done.11, bf16[4096,256]{1,0:T(8,128)(2,1)S(1)} %fusion.38), kind=kLoop, calls=%fused_computation.139 | loop fusion | flops 15728640 | bytes 14680064 | tf_op jit(solution)/shard_map/convert_element_type | solution.py:275
  156.3 2.4 collective-permute-start.19
  158.7 14.0 %collective-permute-done.12.refs_2_ = bf16[96,4096]{1,0:T(8,128)(2,1)S(1)} collective-permute-done((bf16[96,4096]{1,0:T(8,128)(2,1)S(1)}, bf16[96,4096]{1,0:T(8,128)(2,1)S(1)}, u32[]{:S(2)}, u32[]{:S(2)}) %collective-permute-start.12) | collective-permute-done | bytes 786464 | tf_op jit(solution)/shard_map/ppermute | solution.py:41
  172.7 3.1 %collective-permute-start.20 = (f32[512]{0:T(512)S(1)}, f32[512]{0:T(512)S(1)}, u32[]{:S(2)}, u32[]{:S(2)}) collective-permute-start(f32[512]{0:T(512)S(1)} %get-tuple-element.47), channel_id=1, source_target_pairs={{0,1},{1,0},{2,3},{3,2},{4,5},{5,4},{6,7},{7,6},{8,9},{9,8},{10,11... | collective-permute-start | bytes 6152 | tf_op jit(solution)/shard_map/ppermute | solution.py:28
  177.9 15.4 %collective-permute-done.18.refs_3_ = bf16[96,4096]{1,0:T(8,128)(2,1)S(1)} collective-permute-done((bf16[96,4096]{1,0:T(8,128)(2,1)S(1)}, bf16[96,4096]{1,0:T(8,128)(2,1)S(1)}, u32[]{:S(2)}, u32[]{:S(2)}) %collective-permute-start.18) | collective-permute-done | bytes 786464 | tf_op jit(solution)/shard_map/ppermute | solution.py:41
  194.6 8.2 %forward.6 = (f32[768,512]{1,0:T(8,128)S(1)}, bf16[768,4096]{1,0:T(8,128)(2,1)}) custom-call(bf16[96,4096]{1,0:T(8,128)(2,1)S(1)} %copy-done.6, bf16[96,4096]{1,0:T(8,128)(2,1)} %collective-permute-done.14.refs_1_, bf16[96,4096]{1,0:T(8,128)(2,1)S(1)} %collective-permute-done.12.refs_2_, bf16[96,4096]{1,0:T(8,128)(2,1)S(1)} %collective-permute-done.18.refs_3_, ...), custom_call_target="tpu_custom_call" | custom-call | flops 2415919104 | bytes 13631488 | tf_op jit(solution)/shard_map/forward/pallas_call | solution.py:145
  202.9 3.5 %collective-permute-done.13.refs_0_ = bf16[96,4096]{1,0:T(8,128)(2,1)S(1)} collective-permute-done((bf16[96,4096]{1,0:T(8,128)(2,1)S(1)}, bf16[96,4096]{1,0:T(8,128)(2,1)S(1)}, u32[]{:S(2)}, u32[]{:S(2)}) %collective-permute-start.13) | collective-permute-done | bytes 786464 | tf_op jit(solution)/shard_map/ppermute | solution.py:41
  206.4 2.9 %collective-permute-done.16.refs_1_ = bf16[96,4096]{1,0:T(8,128)(2,1)S(1)} collective-permute-done((bf16[96,4096]{1,0:T(8,128)(2,1)S(1)}, bf16[96,4096]{1,0:T(8,128)(2,1)S(1)}, u32[]{:S(2)}, u32[]{:S(2)}) %collective-permute-start.16) | collective-permute-done | bytes 786464 | tf_op jit(solution)/shard_map/ppermute | solution.py:41
  210.9 2.9 %forward.7 = (f32[768,512]{1,0:T(8,128)S(1)}, bf16[768,4096]{1,0:T(8,128)(2,1)}) custom-call(bf16[96,4096]{1,0:T(8,128)(2,1)S(1)} %collective-permute-done.13.refs_0_, bf16[96,4096]{1,0:T(8,128)(2,1)S(1)} %collective-permute-done.16.refs_1_, bf16[8,512,256]{2,1,0:T(8,128)(2,1)S(1)} %bitcast.91, ...), custom_call_target="tpu_custom_call", output_to_operand_aliasing={{0}: (5, {}), {1}: (6, {})} | custom-call | flops 805306368 | bytes 7340032 | tf_op jit(solution)/shard_map/forward/pallas_call | solution.py:145
  214.4 9.1 %all_to_all.21 = f32[8,1,2304]{2,1,0:T(1,128)S(1)} all-to-all(f32[8,1,2304]{2,1,0:T(1,128)S(1)} %broadcast_in_dim.11), channel_id=1, replica_groups=mesh['xl'=2,'z'=4,'y'=4,'xh'=2,'c'=2] {'y','xh'}, dimensions={0} | all-to-all | bytes 147456 | tf_op jit(solution)/shard_map/all_to_all | solution.py:46
  226.4 3.3 %convolution_convert_fusion = bf16[4096,256]{1,0:T(8,128)(2,1)} fusion(bf16[768,4096]{1,0:T(8,128)(2,1)S(1)} %copy-done.12, bf16[768,512]{1,0:T(8,128)(2,1)S(1)} %get-tuple-element.45), kind=kOutput, calls=%fused_computation.7 | convolution fusion | flops 1611661312 | bytes 8781824 | tf_op jit(solution)/shard_map/td,tf->df/dot_general | solution.py:261
  231.6 6.8 %fusion.32 = f32[4096,256]{1,0:T(8,128)} fusion(bf16[768,4096]{1,0:T(8,128)(2,1)} %get-tuple-element.24, bf16[768,512]{1,0:T(8,128)(2,1)S(1)} %get-tuple-element.45), kind=kOutput, calls=%fused_computation.72 | convolution fusion | flops 1610612736 | bytes 10878976 | tf_op jit(solution)/shard_map/td,tf->df/dot_general | solution.py:261
  238.7 6.0 %fusion.1 = bf16[4096,256]{1,0:T(8,128)(2,1)S(1)} fusion(bf16[4096,256]{1,0:T(8,128)(2,1)} %get-tuple-element.19, bf16[4096,256]{1,0:T(8,128)(2,1)} %get-tuple-element.20, bf16[4096,256]{1,0:T(8,128)(2,1)S(1)} %copy-done.9, f32[4096,256]{1,0:T(8,128)} %fusion.32, bf16[4096,256]{1,0:T(8,128)(2,1)} %collective-permute-done.21), kind=kLoop, calls=%fused_computation.12 | loop fusion | flops 25165824 | bytes 14680064 | tf_op jit(solution)/shard_map/convert_element_type | solution.py:292
  245.0 29.6 %all_to_all.22 = bf16[8,528,256]{2,1,0:T(8,128)(2,1)S(1)} all-to-all(bf16[8,528,256]{2,1,0:T(8,128)(2,1)S(1)} %fusion.13), channel_id=1, replica_groups=mesh['xl'=2,'z'=4,'y'=4,'xh'=2,'c'=2] {'xl','z'}, dimensions={0} | all-to-all | bytes 4325376 | tf_op jit(solution)/shard_map/all_to_all | solution.py:295
  (136 shorter events, 38.5 us)
Async XLA Ops:
  2.4 7.9 %collective-permute-start = (bf16[528,256]{1,0:T(8,128)(2,1)S(1)}, bf16[528,256]{1,0:T(8,128)(2,1)S(1)}, u32[]{:S(2)}, u32[]{:S(2)}) collective-permute-start(bf16[528,256]{1,0:T(8,128)(2,1)S(1)} %fusion.37), channel_id=1, source_target_pairs={{0,64},{64,0},{1,65},{65,1},{2,66},{66,2},{3,67},{67,3},{4,68},{68... | collective-permute-start | bytes 811016 | tf_op jit(solution)/shard_map/ppermute | solution.py:201
  10.6 33.3 %copy-start.14 = (bf16[1,2,96,4096]{3,2,1,0:T(8,128)(2,1)S(1)}, bf16[1,2,96,4096]{3,2,1,0:T(8,128)(2,1)}, u32[]{:S(2)}) copy-start(bf16[1,2,96,4096]{3,2,1,0:T(8,128)(2,1)} %param.11) | copy-start | bytes 4718596
  41.0 44.7 %collective-permute-start.5 = (bf16[4,2,528,256]{3,2,1,0:T(8,128)(2,1)S(1)}, bf16[4,2,528,256]{3,2,1,0:T(8,128)(2,1)}, u32[]{:S(2)}, u32[]{:S(2)}) collective-permute-start(bf16[4,2,528,256]{3,2,1,0:T(8,128)(2,1)S(1)} %all_to_all.20.refs_5_.refs_3_), channel_id=1, source_target_pairs={{0,1},{1,0},{2,3},{3,2},{4,5},{5,4},{6,7},{7,6},{8,9},{9,8},{10,11... | collective-permute-start | bytes 6488072 | tf_op jit(solution)/shard_map/ppermute | solution.py:28
  45.2 20.9 %collective-permute-start.1 = (bf16[96,4096]{1,0:T(8,128)(2,1)}, bf16[96,4096]{1,0:T(8,128)(2,1)}, u32[]{:S(2)}, u32[]{:S(2)}) collective-permute-start(bf16[96,4096]{1,0:T(8,128)(2,1)} %get-tuple-element.57.refs_0_), channel_id=1, source_target_pairs={{0,2},{2,0},{1,3},{3,1},{4,6},{6,4},{5,7},{7,5},{8,10},{10,8},{9,1... | collective-permute-start | bytes 2359304 | tf_op jit(solution)/shard_map/ppermute | solution.py:32
  49.6 17.9 %collective-permute-start.6 = (bf16[2,8,96,256]{3,2,1,0:T(8,128)(2,1)S(1)}, bf16[2,8,96,256]{3,2,1,0:T(8,128)(2,1)S(1)}, u32[]{:S(2)}, u32[]{:S(2)}) collective-permute-start(bf16[2,8,96,256]{3,2,1,0:T(8,128)(2,1)S(1)} %get-tuple-element.55), channel_id=1, source_target_pairs={{0,1},{1,0},{2,3},{3,2},{4,5},{5,4},{6,7},{7,6},{8,9},{9,8},{10,11... | collective-permute-start | bytes 2359304 | tf_op jit(solution)/shard_map/ppermute | solution.py:28
  50.0 18.8 %collective-permute-start.7 = (bf16[96,4096]{1,0:T(8,128)(2,1)}, bf16[96,4096]{1,0:T(8,128)(2,1)}, u32[]{:S(2)}, u32[]{:S(2)}) collective-permute-start(bf16[96,4096]{1,0:T(8,128)(2,1)} %get-tuple-element.57.refs_0_), channel_id=1, source_target_pairs={{0,4},{1,13},{4,8},{5,1},{8,12},{9,5},{12,0},{13,9},{2,6},{3,15},{... | collective-permute-start | bytes 2359304 | tf_op jit(solution)/shard_map/ppermute | solution.py:41
  52.8 17.3 %collective-permute-start.10 = (bf16[2,8,96,256]{3,2,1,0:T(8,128)(2,1)S(1)}, bf16[2,8,96,256]{3,2,1,0:T(8,128)(2,1)S(1)}, u32[]{:S(2)}, u32[]{:S(2)}) collective-permute-start(bf16[2,8,96,256]{3,2,1,0:T(8,128)(2,1)S(1)} %get-tuple-element.53), channel_id=1, source_target_pairs={{0,1},{1,0},{2,3},{3,2},{4,5},{5,4},{6,7},{7,6},{8,9},{9,8},{10,11... | collective-permute-start | bytes 2359304 | tf_op jit(solution)/shard_map/ppermute | solution.py:28
  66.2 16.1 %collective-permute-start.3 = (bf16[96,4096]{1,0:T(8,128)(2,1)}, bf16[96,4096]{1,0:T(8,128)(2,1)}, u32[]{:S(2)}, u32[]{:S(2)}) collective-permute-start(bf16[96,4096]{1,0:T(8,128)(2,1)} %collective-permute-done.1.refs_1_), channel_id=1, source_target_pairs={{0,12},{1,5},{4,0},{5,9},{8,4},{9,13},{12,8},{13,1},{2,14},{3,7},{... | collective-permute-start | bytes 2359304 | tf_op jit(solution)/shard_map/ppermute | solution.py:41
  67.5 31.7 %collective-permute-start.8 = (bf16[96,4096]{1,0:T(8,128)(2,1)}, bf16[96,4096]{1,0:T(8,128)(2,1)}, u32[]{:S(2)}, u32[]{:S(2)}) collective-permute-start(bf16[96,4096]{1,0:T(8,128)(2,1)} %get-tuple-element.57.refs_0_), channel_id=1, source_target_pairs={{0,12},{1,5},{4,0},{5,9},{8,4},{9,13},{12,8},{13,1},{2,14},{3,7},{... | collective-permute-start | bytes 2359304 | tf_op jit(solution)/shard_map/ppermute | solution.py:41
  68.8 30.4 %collective-permute-start.9 = (bf16[96,4096]{1,0:T(8,128)(2,1)}, bf16[96,4096]{1,0:T(8,128)(2,1)}, u32[]{:S(2)}, u32[]{:S(2)}) collective-permute-start(bf16[96,4096]{1,0:T(8,128)(2,1)} %collective-permute-done.7.refs_2_), channel_id=1, source_target_pairs={{0,4},{1,13},{4,8},{5,1},{8,12},{9,5},{12,0},{13,9},{2,6},{3,15},{... | collective-permute-start | bytes 2359304 | tf_op jit(solution)/shard_map/ppermute | solution.py:41
  70.1 39.4 %collective-permute-start.2 = (bf16[96,4096]{1,0:T(8,128)(2,1)}, bf16[96,4096]{1,0:T(8,128)(2,1)}, u32[]{:S(2)}, u32[]{:S(2)}) collective-permute-start(bf16[96,4096]{1,0:T(8,128)(2,1)} %collective-permute-done.1.refs_1_), channel_id=1, source_target_pairs={{0,4},{1,13},{4,8},{5,1},{8,12},{9,5},{12,0},{13,9},{2,6},{3,15},{... | collective-permute-start | bytes 2359304 | tf_op jit(solution)/shard_map/ppermute | solution.py:41
  82.3 30.0 %collective-permute-start.4 = (bf16[96,4096]{1,0:T(8,128)(2,1)}, bf16[96,4096]{1,0:T(8,128)(2,1)}, u32[]{:S(2)}, u32[]{:S(2)}) collective-permute-start(bf16[96,4096]{1,0:T(8,128)(2,1)} %collective-permute-done.3.refs_1_), channel_id=1, source_target_pairs={{0,12},{1,5},{4,0},{5,9},{8,4},{9,13},{12,8},{13,1},{2,14},{3,7},{... | collective-permute-start | bytes 2359304 | tf_op jit(solution)/shard_map/ppermute | solution.py:41
  85.6 69.8 %collective-permute-start.14 = (bf16[96,4096]{1,0:T(8,128)(2,1)}, bf16[96,4096]{1,0:T(8,128)(2,1)}, u32[]{:S(2)}, u32[]{:S(2)}) collective-permute-start(bf16[96,4096]{1,0:T(8,128)(2,1)} %get-tuple-element.58.refs_0_), channel_id=1, source_target_pairs={{0,2},{2,0},{1,3},{3,1},{4,6},{6,4},{5,7},{7,5},{8,10},{10,8},{9,1... | collective-permute-start | bytes 2359304 | tf_op jit(solution)/shard_map/ppermute | solution.py:32
  100.3 12.0 %copy-start.5 = (bf16[1,8,96,512]{3,2,1,0:T(8,128)(2,1)S(1)}, bf16[1,8,96,512]{3,2,1,0:T(8,128)(2,1)}, u32[]{:S(2)}) copy-start(bf16[1,8,96,512]{3,2,1,0:T(8,128)(2,1)} %get-tuple-element.52) | copy-start | bytes 2359300
  112.3 7.0 %copy-start.11 = (bf16[1,8,96,512]{3,2,1,0:T(8,128)(2,1)S(1)}, bf16[1,8,96,512]{3,2,1,0:T(8,128)(2,1)}, u32[]{:S(2)}) copy-start(bf16[1,8,96,512]{3,2,1,0:T(8,128)(2,1)} %get-tuple-element.50) | copy-start | bytes 2359300
  120.5 12.4 %all-to-all-start.1 = ((f32[8,1,2304]{2,1,0:T(1,128)}), f32[8,1,2304]{2,1,0:T(1,128)S(1)}, u32[]{:S(2)}, u32[]{:S(2)}) async-start(f32[8,1,2304]{2,1,0:T(1,128)} %broadcast_in_dim.10), calls=%async_computation.1 | async-start | bytes 147456 | tf_op jit(solution)/shard_map/all_to_all | solution.py:46
  135.8 11.3 %slice-start = ((s8[6291456]{0:T(1024)(128)(4,1)}), s8[4194304]{0:T(1024)(128)(4,1)S(1)}, s32[]{:S(2)}) async-start(s8[6291456]{0:T(1024)(128)(4,1)} %bitcast.97), calls=%async_computation.4 | async-start | bytes 8388608
  135.8 11.1 %copy-start.7 = (bf16[4096,256]{1,0:T(8,128)(2,1)S(1)}, bf16[4096,256]{1,0:T(8,128)(2,1)}, u32[]{:S(2)}) copy-start(bf16[4096,256]{1,0:T(8,128)(2,1)} %fusion.45) | copy-start | bytes 6291460
  135.8 11.3 %slice-start.1 = ((s8[6291456]{0:T(1024)(128)(4,1)}), s8[2097152]{0:T(1024)(128)(4,1)S(1)}, s32[]{:S(2)}) async-start(s8[6291456]{0:T(1024)(128)(4,1)} %bitcast.97), calls=%async_computation.5 | async-start | bytes 4194304
  140.6 10.0 %collective-permute-start.11 = (bf16[4096,256]{1,0:T(8,128)(2,1)S(1)}, bf16[4096,256]{1,0:T(8,128)(2,1)S(1)}, u32[]{:S(2)}, u32[]{:S(2)}) collective-permute-start(bf16[4096,256]{1,0:T(8,128)(2,1)S(1)} %convolution_convert_fusion.1), channel_id=1, source_target_pairs={{0,1},{1,0},{2,3},{3,2},{4,5},{5,4},{6,7},{7,6},{8,9},{9,8},{10,11... | collective-permute-start | bytes 6291464 | tf_op jit(solution)/shard_map/ppermute | solution.py:28
  149.0 5.6 %copy-start.6 = (bf16[96,4096]{1,0:T(8,128)(2,1)S(1)}, bf16[96,4096]{1,0:T(8,128)(2,1)}, u32[]{:S(2)}) copy-start(bf16[96,4096]{1,0:T(8,128)(2,1)} %get-tuple-element.58.refs_0_) | copy-start | bytes 2359300
  154.2 39.1 %collective-permute-start.17 = (bf16[8,512,256]{2,1,0:T(8,128)(2,1)S(1)}, bf16[8,512,256]{2,1,0:T(8,128)(2,1)S(1)}, u32[]{:S(2)}, u32[]{:S(2)}) collective-permute-start(bf16[8,512,256]{2,1,0:T(8,128)(2,1)S(1)} %bitcast.89), channel_id=1, source_target_pairs={{0,1},{1,0},{2,3},{3,2},{4,5},{5,4},{6,7},{7,6},{8,9},{9,8},{10,11... | collective-permute-start | bytes 6291464 | tf_op jit(solution)/shard_map/ppermute | solution.py:28
  154.6 18.2 %collective-permute-start.12 = (bf16[96,4096]{1,0:T(8,128)(2,1)S(1)}, bf16[96,4096]{1,0:T(8,128)(2,1)S(1)}, u32[]{:S(2)}, u32[]{:S(2)}) collective-permute-start(bf16[96,4096]{1,0:T(8,128)(2,1)S(1)} %copy-done.6), channel_id=1, source_target_pairs={{0,4},{1,13},{4,8},{5,1},{8,12},{9,5},{12,0},{13,9},{2,6},{3,15},{... | collective-permute-start | bytes 2359304 | tf_op jit(solution)/shard_map/ppermute | solution.py:41
  155.4 21.0 %collective-permute-start.15 = (bf16[96,4096]{1,0:T(8,128)(2,1)}, bf16[96,4096]{1,0:T(8,128)(2,1)S(1)}, u32[]{:S(2)}, u32[]{:S(2)}) collective-permute-start(bf16[96,4096]{1,0:T(8,128)(2,1)} %collective-permute-done.14.refs_1_), channel_id=1, source_target_pairs={{0,12},{1,5},{4,0},{5,9},{8,4},{9,13},{12,8},{13,1},{2,14},{3,7},{... | collective-permute-start | bytes 2359304 | tf_op jit(solution)/shard_map/ppermute | solution.py:41
  156.0 37.3 %collective-permute-start.18 = (bf16[96,4096]{1,0:T(8,128)(2,1)S(1)}, bf16[96,4096]{1,0:T(8,128)(2,1)S(1)}, u32[]{:S(2)}, u32[]{:S(2)}) collective-permute-start(bf16[96,4096]{1,0:T(8,128)(2,1)S(1)} %copy-done.6), channel_id=1, source_target_pairs={{0,12},{1,5},{4,0},{5,9},{8,4},{9,13},{12,8},{13,1},{2,14},{3,7},{... | collective-permute-start | bytes 2359304 | tf_op jit(solution)/shard_map/ppermute | solution.py:41
  156.3 37.0 %collective-permute-start.19 = (bf16[96,4096]{1,0:T(8,128)(2,1)}, bf16[96,4096]{1,0:T(8,128)(2,1)S(1)}, u32[]{:S(2)}, u32[]{:S(2)}) collective-permute-start(bf16[96,4096]{1,0:T(8,128)(2,1)} %collective-permute-done.14.refs_1_), channel_id=1, source_target_pairs={{0,4},{1,13},{4,8},{5,1},{8,12},{9,5},{12,0},{13,9},{2,6},{3,15},{... | collective-permute-start | bytes 2359304 | tf_op jit(solution)/shard_map/ppermute | solution.py:41
  172.7 3.9 %collective-permute-start.20 = (f32[512]{0:T(512)S(1)}, f32[512]{0:T(512)S(1)}, u32[]{:S(2)}, u32[]{:S(2)}) collective-permute-start(f32[512]{0:T(512)S(1)} %get-tuple-element.47), channel_id=1, source_target_pairs={{0,1},{1,0},{2,3},{3,2},{4,5},{5,4},{6,7},{7,6},{8,9},{9,8},{10,11... | collective-permute-start | bytes 6152 | tf_op jit(solution)/shard_map/ppermute | solution.py:28
  176.4 30.0 %collective-permute-start.13 = (bf16[96,4096]{1,0:T(8,128)(2,1)S(1)}, bf16[96,4096]{1,0:T(8,128)(2,1)S(1)}, u32[]{:S(2)}, u32[]{:S(2)}) collective-permute-start(bf16[96,4096]{1,0:T(8,128)(2,1)S(1)} %collective-permute-done.12.refs_2_), channel_id=1, source_target_pairs={{0,4},{1,13},{4,8},{5,1},{8,12},{9,5},{12,0},{13,9},{2,6},{3,15},{... | collective-permute-start | bytes 2359304 | tf_op jit(solution)/shard_map/ppermute | solution.py:41
  176.6 32.7 %collective-permute-start.16 = (bf16[96,4096]{1,0:T(8,128)(2,1)S(1)}, bf16[96,4096]{1,0:T(8,128)(2,1)S(1)}, u32[]{:S(2)}, u32[]{:S(2)}) collective-permute-start(bf16[96,4096]{1,0:T(8,128)(2,1)S(1)} %collective-permute-done.15.refs_5_), channel_id=1, source_target_pairs={{0,12},{1,5},{4,0},{5,9},{8,4},{9,13},{12,8},{13,1},{2,14},{3,7},{... | collective-permute-start | bytes 2359304 | tf_op jit(solution)/shard_map/ppermute | solution.py:41
  229.7 9.0 %collective-permute-start.21 = (bf16[4096,256]{1,0:T(8,128)(2,1)}, bf16[4096,256]{1,0:T(8,128)(2,1)}, u32[]{:S(2)}, u32[]{:S(2)}) collective-permute-start(bf16[4096,256]{1,0:T(8,128)(2,1)} %convolution_convert_fusion), channel_id=1, source_target_pairs={{0,1},{1,0},{2,3},{3,2},{4,5},{5,4},{6,7},{7,6},{8,9},{9,8},{10,11... | collective-permute-start | bytes 6291464 | tf_op jit(solution)/shard_map/ppermute | solution.py:28
  231.3 7.4 %copy-start.9 = (bf16[4096,256]{1,0:T(8,128)(2,1)S(1)}, bf16[4096,256]{1,0:T(8,128)(2,1)}, u32[]{:S(2)}) copy-start(bf16[4096,256]{1,0:T(8,128)(2,1)} %copy-done.8) | copy-start | bytes 6291460
  231.3 7.2 %collective-permute-start.22 = (f32[512]{0:T(512)S(1)}, f32[512]{0:T(512)S(1)}, u32[]{:S(2)}, u32[]{:S(2)}) collective-permute-start(f32[512]{0:T(512)S(1)} %get-tuple-element.46), channel_id=1, source_target_pairs={{0,1},{1,0},{2,3},{3,2},{4,5},{5,4},{6,7},{7,6},{8,9},{9,8},{10,11... | collective-permute-start | bytes 6152 | tf_op jit(solution)/shard_map/ppermute | solution.py:28
  (13 other events, 27.7 us)

commit v3 on v2

--- a/solution.py
+++ b/solution.py
@@ -58,7 +58,7 @@
 
 
 BLOCK = 96
-VMEM_LIMIT = 44 * 1024 * 1024
+VMEM_LIMIT = 46 * 1024 * 1024
 
 
 LETTERS = "oxabcefg"
@@ -66,7 +66,7 @@
 LATE = ("ceg", "fg")
 
 
-def forward_kernel(letters, pieces, weight, weight_other, flow, residual_out, rows_out, rows, weights, made, came, loaded, left, sent):
+def forward_kernel(letters, pieces, weight, weight_other, flow, residual_out, rows_out, rows, made, came, left, sent):
     y, xh, c = lax.axis_index("y"), lax.axis_index("xh"), lax.axis_index("c")
     d = 1 - 2 * c
     before, after, across = (y + 4 - d) % 4, (y + 4 + d) % 4, (y + 2) % 4
@@ -79,21 +79,8 @@
         py, px = blocks[LETTERS.index(letter)]
         places.append(pl.ds(pl.multiple_of((py * 2 + px) * BLOCK, BLOCK), BLOCK))
     own = [pl.ds(at * BLOCK, BLOCK) for at in range(len(letters))]
-    islands, owned, wide = weights.shape[1:]
-
-    def loads_of(half, source):
-        if len(source.shape) == 3:
-            return [pltpu.make_async_copy(source, weights.at[half], loaded.at[half, 0])]
-        return [
-            pltpu.make_async_copy(
-                source.at[:, xl, pl.ds(0, owned)],
-                weights.at[half, pl.ds(xl * (islands // 2), islands // 2)],
-                loaded.at[half, xl],
-            )
-            for xl in range(2)
-        ]
-
-    loads = [loads_of(0, weight), loads_of(1, weight_other)]
+    owned, wide = D // 8, flow.shape[1] // 2
+
     takes = [
         pltpu.make_async_copy(source, rows.at[at], came.at[i])
         for i, (at, source) in enumerate(zip(own, pieces))
@@ -106,19 +93,23 @@
         pltpu.make_async_copy(made.at[at], residual_out.at[to], sent.at[i])
         for i, (at, to) in enumerate(zip(own, places))
     ]
-    for copy in (*loads[0], *takes, *loads[1]):
-        copy.start()
+    for take in takes:
+        take.start()
     for take, give in zip(takes, gives):
         take.wait()
         give.start()
-    for half in range(2):
-        for load in loads[half]:
-            load.wait()
-        projected = jnp.dot(
-            rows[...],
-            weights[half].reshape(islands * owned, wide),
-            preferred_element_type=jnp.float32,
-        )
+    for half, source in enumerate((weight, weight_other)):
+        projected = 0.0
+        for slab in range(8):
+            if len(source.shape) == 3:
+                part = source[slab]
+            else:
+                part = source[slab % 4, slab // 4, :owned]
+            projected += jnp.dot(
+                rows[:, slab * owned : (slab + 1) * owned],
+                part,
+                preferred_element_type=jnp.float32,
+            )
         columns = slice(half * wide, (half + 1) * wide)
         for at, (mine, to) in enumerate(zip(own, places)):
             made[mine, columns] = (
@@ -136,7 +127,6 @@
     inside = pl.BlockSpec(memory_space=pltpu.VMEM)
     count = len(letters)
     tokens, features = flow.shape
-    islands, owned, wide = 8, D // 8, features // 2
 
     def kernel(*refs):
         rest = refs[count : count + 3] + refs[count + 3 + len(earlier) :]
@@ -148,14 +138,12 @@
             jax.ShapeDtypeStruct((tokens, features), jnp.float32),
             jax.ShapeDtypeStruct((tokens, D), jnp.bfloat16),
         ),
-        in_specs=[anywhere] * (count + 2) + [inside] + [anywhere] * len(earlier),
+        in_specs=[anywhere] * count + [inside] * 3 + [anywhere] * len(earlier),
         out_specs=(anywhere, anywhere),
         scratch_shapes=[
             pltpu.VMEM((count * BLOCK, D), jnp.bfloat16),
-            pltpu.VMEM((2, islands, owned, wide), jnp.bfloat16),
             pltpu.VMEM((count * BLOCK, features), jnp.float32),
             pltpu.SemaphoreType.DMA((count,)),
-            pltpu.SemaphoreType.DMA((2, 2)),
             pltpu.SemaphoreType.DMA((count,)),
             pltpu.SemaphoreType.DMA((count,)),
         ],
@@ -264,7 +252,9 @@
 
         other = over_tokens(slice(wide, None)).astype(jnp.bfloat16)
         other = core_swap(other)
-        mine = lax.optimization_barrier(over_tokens(slice(0, wide)))
+        mine = over_tokens(slice(0, wide))
+        if step == 0:
+            mine = lax.optimization_barrier(mine)
         weight_grad = (mine + other.astype(jnp.float32)) * width_scale
         gain_other = core_swap(gain_grad)
         gain_grad = gain_grad + jnp.concatenate([gain_other[wide:], gain_other[:wide]])

time: 278 us -> 277 us (level)
  waiting for transfers between devices: 87.9 us -> 92.9 us
  Pallas kernels: 26.2 us -> 23.3 us
    ppermute x8, waiting for transfers between devices: 1.93 us -> 5.74 us  [core_swap(): return lax.ppermute(value, 'c', [(0, 1), (1, 0)])]
    pallas_call x4, Pallas kernels: 26.2 us -> 23.3 us  [forward(): pl.pallas_call(kernel, out_shape=(jax.ShapeDtypeStruct((tokens, features)...]
    unnamed x52 -> x62, local copies, waits for them, and re-layouts: 8.83 us -> 10.4 us
  transfers between devices with their start and end apart: 24 -> 24, of which waited for: 13 -> 14; matrix products, arithmetic and copies ran while one was open for 10% -> 8% of each run, Pallas kernels for 8% -> 8%
where the time goes in v3:
time: 277 us; the launch traced here: 276 us
  waiting for transfers between devices  92.9 us (34%)
  blocking collectives  69.1 us (25%)
  starting transfers between devices  40.2 us (15%)
  Pallas kernels  23.3 us (8%)
  other arithmetic  18.2 us (7%)
  local copies, waits for them, and re-layouts  15.7 us (6%)
  matrix products  15.5 us (6%)
    ppermute x12, waiting for transfers between devices, y_hop(): return lax.ppermute(value, ('y', 'c'), pairs)  62.4 us
    all_to_all x2, blocking collectives, copy_for_each(): return lax.all_to_all(copies, axis, split_axis=0, concat_axis=0, tiled=True)  39.5 us
    all_to_all x1, blocking collectives, per_device(): lax.all_to_all(sent, ISLAND, split_axis=0, concat_axis=0, tiled=True)  29.6 us
    pallas_call x4, Pallas kernels, forward(): pl.pallas_call(kernel, out_shape=(jax.ShapeDtypeStruct((tokens, features)...  23.3 us
    dot_general x4, matrix products, over_tokens(): jnp.einsum('td,tf->df', rows, residual_grad[:, columns], preferred_elemen...  15.5 us
    ppermute x8, starting transfers between devices, core_swap(): return lax.ppermute(value, 'c', [(0, 1), (1, 0)])  13.6 us
    ppermute x12, starting transfers between devices, y_hop(): return lax.ppermute(value, ('y', 'c'), pairs)  13.3 us
    ppermute x2, waiting for transfers between devices, x_swap(): return lax.ppermute(value, 'xh', [(0, 1), (1, 0)])  13 us
  transfers between devices with their start and end apart: 24, of which 14 were waited for; matrix products, arithmetic and copies ran while one was open for 8% of the time, Pallas kernels for 8%

profile of v3, /device:TPU:1, one launch (start us, length us, event | category | flops | bytes accessed | tf_op | source)
XLA Modules:
  0.0 276.1 jit_solution(13960472188519952460)
XLA Ops:
  2.4 2.1 collective-permute-start
  4.5 5.8 %collective-permute-done = bf16[528,256]{1,0:T(8,128)(2,1)S(1)} collective-permute-done((bf16[528,256]{1,0:T(8,128)(2,1)S(1)}, bf16[528,256]{1,0:T(8,128)(2,1)S(1)}, u32[]{:S(2)}, u32[]{:S(2)}) %collective-permute-start) | collective-permute-done | bytes 270368 | tf_op jit(solution)/shard_map/ppermute | solution.py:189
  10.6 30.4 %all_to_all.20.refs_5_.refs_3_ = bf16[4,2,528,256]{3,2,1,0:T(8,128)(2,1)S(1)} all-to-all(bf16[4,2,528,256]{3,2,1,0:T(8,128)(2,1)S(1)} %broadcast_in_dim.9), channel_id=1, replica_groups=mesh['xl'=2,'z'=4,'y'=4,'xh'=2,'c'=2] {'z'}, dimensions={0} | all-to-all | bytes 4325376 | tf_op jit(solution)/shard_map/all_to_all | solution.py:46
  41.0 3.0 %collective-permute-start.5 = (bf16[4,2,528,256]{3,2,1,0:T(8,128)(2,1)S(1)}, bf16[4,2,528,256]{3,2,1,0:T(8,128)(2,1)}, u32[]{:S(2)}, u32[]{:S(2)}) collective-permute-start(bf16[4,2,528,256]{3,2,1,0:T(8,128)(2,1)S(1)} %all_to_all.20.refs_5_.refs_3_), channel_id=1, source_target_pairs={{0,1},{1,0},{2,3},{3,2},{4,5},{5,4},{6,7},{7,6},{8,9},{9,8},{10,11... | collective-permute-start | bytes 6488072 | tf_op jit(solution)/shard_map/ppermute | solution.py:28
  45.3 2.7 collective-permute-start.1
  50.1 2.7 collective-permute-start.7
  53.0 13.0 %collective-permute-done.1.refs_1_ = bf16[96,4096]{1,0:T(8,128)(2,1)} collective-permute-done((bf16[96,4096]{1,0:T(8,128)(2,1)}, bf16[96,4096]{1,0:T(8,128)(2,1)}, u32[]{:S(2)}, u32[]{:S(2)}) %collective-permute-start.1) | collective-permute-done | bytes 786464 | tf_op jit(solution)/shard_map/ppermute | solution.py:32
  70.3 11.7 %collective-permute-done.3.refs_1_ = bf16[96,4096]{1,0:T(8,128)(2,1)} collective-permute-done((bf16[96,4096]{1,0:T(8,128)(2,1)}, bf16[96,4096]{1,0:T(8,128)(2,1)}, u32[]{:S(2)}, u32[]{:S(2)}) %collective-permute-start.3) | collective-permute-done | bytes 786464 | tf_op jit(solution)/shard_map/ppermute | solution.py:41
  85.5 2.8 %collective-permute-start.14 = (bf16[96,4096]{1,0:T(8,128)(2,1)}, bf16[96,4096]{1,0:T(8,128)(2,1)}, u32[]{:S(2)}, u32[]{:S(2)}) collective-permute-start(bf16[96,4096]{1,0:T(8,128)(2,1)} %get-tuple-element.58.refs_0_), channel_id=1, source_target_pairs={{0,2},{2,0},{1,3},{3,1},{4,6},{6,4},{5,7},{7,5},{8,10},{10,8},{9,1... | collective-permute-start | bytes 2359304 | tf_op jit(solution)/shard_map/ppermute | solution.py:32
  89.1 9.8 %collective-permute-done.8.refs_3_ = bf16[96,4096]{1,0:T(8,128)(2,1)} collective-permute-done((bf16[96,4096]{1,0:T(8,128)(2,1)}, bf16[96,4096]{1,0:T(8,128)(2,1)}, u32[]{:S(2)}, u32[]{:S(2)}) %collective-permute-start.8) | collective-permute-done | bytes 786464 | tf_op jit(solution)/shard_map/ppermute | solution.py:41
  100.0 8.2 %forward.4 = (f32[768,512]{1,0:T(8,128)S(1)}, bf16[768,4096]{1,0:T(8,128)(2,1)}) custom-call(bf16[96,4096]{1,0:T(8,128)(2,1)} %get-tuple-element.57.refs_0_, bf16[96,4096]{1,0:T(8,128)(2,1)} %collective-permute-done.1.refs_1_, bf16[96,4096]{1,0:T(8,128)(2,1)} %collective-permute-done.7.refs_2_, bf16[96,4096]{1,0:T(8,128)(2,1)} %collective-permute-done.8.refs_3_, ...), custom_call_target="tpu_custom_call" | custom-call | flops 2013265920 | bytes 12058624 | tf_op jit(solution)/shard_map/forward/pallas_call | solution.py:135
  108.2 4.0 %collective-permute-done.4.refs_2_ = bf16[96,4096]{1,0:T(8,128)(2,1)} collective-permute-done((bf16[96,4096]{1,0:T(8,128)(2,1)}, bf16[96,4096]{1,0:T(8,128)(2,1)}, u32[]{:S(2)}, u32[]{:S(2)}) %collective-permute-start.4) | collective-permute-done | bytes 786464 | tf_op jit(solution)/shard_map/ppermute | solution.py:41
  112.2 5.5 %forward.5 = (f32[768,512]{1,0:T(8,128)S(1)}, bf16[768,4096]{1,0:T(8,128)(2,1)}) custom-call(bf16[96,4096]{1,0:T(8,128)(2,1)} %collective-permute-done.2.refs_0_, bf16[96,4096]{1,0:T(8,128)(2,1)} %collective-permute-done.3.refs_1_, bf16[96,4096]{1,0:T(8,128)(2,1)} %collective-permute-done.4.refs_2_, ...), custom_call_target="tpu_custom_call", output_to_operand_aliasing={{0}: (6, {}), {1}: (7, {})} | custom-call | flops 1207959552 | bytes 8912896 | tf_op jit(solution)/shard_map/forward/pallas_call | solution.py:135
  120.1 5.7 %all-to-all-start.1 = ((f32[8,1,2304]{2,1,0:T(1,128)}), f32[8,1,2304]{2,1,0:T(1,128)S(1)}, u32[]{:S(2)}, u32[]{:S(2)}) async-start(f32[8,1,2304]{2,1,0:T(1,128)} %broadcast_in_dim.10), calls=%async_computation.1 | async-start | bytes 147456 | tf_op jit(solution)/shard_map/all_to_all | solution.py:46
  126.5 6.0 %all-to-all-done.1 = f32[8,1,2304]{2,1,0:T(1,128)S(1)} async-done(((f32[8,1,2304]{2,1,0:T(1,128)}), f32[8,1,2304]{2,1,0:T(1,128)S(1)}, u32[]{:S(2)}, u32[]{:S(2)}) %all-to-all-start.1) | async-done | bytes 73760 | tf_op jit(solution)/shard_map/all_to_all | solution.py:46
  132.6 2.0 fusion.25
  135.4 4.8 %convolution_convert_fusion.1 = bf16[4096,256]{1,0:T(8,128)(2,1)S(1)} fusion(bf16[768,4096]{1,0:T(8,128)(2,1)} %get-tuple-element.17, bf16[768,512]{1,0:T(8,128)(2,1)S(1)} %get-tuple-element.48), kind=kOutput, calls=%fused_computation.9 | convolution fusion | flops 1611661312 | bytes 8781824 | tf_op jit(solution)/shard_map/td,tf->df/dot_general | solution.py:249
  140.2 5.3 %collective-permute-start.11 = (bf16[4096,256]{1,0:T(8,128)(2,1)S(1)}, bf16[4096,256]{1,0:T(8,128)(2,1)S(1)}, u32[]{:S(2)}, u32[]{:S(2)}) collective-permute-start(bf16[4096,256]{1,0:T(8,128)(2,1)S(1)} %convolution_convert_fusion.1), channel_id=1, source_target_pairs={{0,1},{1,0},{2,3},{3,2},{4,5},{5,4},{6,7},{7,6},{8,9},{9,8},{10,11... | collective-permute-start | bytes 6291464 | tf_op jit(solution)/shard_map/ppermute | solution.py:28
  149.3 3.4 %fusion.58 = (bf16[4096,256]{1,0:T(8,128)(2,1)S(1)}, bf16[4096,256]{1,0:T(8,128)(2,1)}, bf16[4096,256]{1,0:T(8,128)(2,1)}) fusion(f32[4096,256]{1,0:T(8,128)S(1)} %fusion.34, bf16[4096,256]{1,0:T(8,128)(2,1)S(1)} %collective-permute-done.11, bf16[4096,256]{1,0:T(8,128)(2,1)S(1)} %fusion.37), kind=kLoop, calls=%fused_computation.139 | loop fusion | flops 15728640 | bytes 14680064 | tf_op jit(solution)/shard_map/convert_element_type | solution.py:265
  154.9 2.4 collective-permute-start.19
  157.3 14.0 %collective-permute-done.12.refs_2_ = bf16[96,4096]{1,0:T(8,128)(2,1)S(1)} collective-permute-done((bf16[96,4096]{1,0:T(8,128)(2,1)S(1)}, bf16[96,4096]{1,0:T(8,128)(2,1)S(1)}, u32[]{:S(2)}, u32[]{:S(2)}) %collective-permute-start.12) | collective-permute-done | bytes 786464 | tf_op jit(solution)/shard_map/ppermute | solution.py:41
  171.3 3.1 %collective-permute-start.20 = (f32[512]{0:T(512)S(1)}, f32[512]{0:T(512)S(1)}, u32[]{:S(2)}, u32[]{:S(2)}) collective-permute-start(f32[512]{0:T(512)S(1)} %get-tuple-element.47), channel_id=1, source_target_pairs={{0,1},{1,0},{2,3},{3,2},{4,5},{5,4},{6,7},{7,6},{8,9},{9,8},{10,11... | collective-permute-start | bytes 6152 | tf_op jit(solution)/shard_map/ppermute | solution.py:28
  176.5 15.4 %collective-permute-done.18.refs_3_ = bf16[96,4096]{1,0:T(8,128)(2,1)S(1)} collective-permute-done((bf16[96,4096]{1,0:T(8,128)(2,1)S(1)}, bf16[96,4096]{1,0:T(8,128)(2,1)S(1)}, u32[]{:S(2)}, u32[]{:S(2)}) %collective-permute-start.18) | collective-permute-done | bytes 786464 | tf_op jit(solution)/shard_map/ppermute | solution.py:41
  193.2 7.7 %forward.6 = (f32[768,512]{1,0:T(8,128)S(1)}, bf16[768,4096]{1,0:T(8,128)(2,1)}) custom-call(bf16[96,4096]{1,0:T(8,128)(2,1)S(1)} %copy-done.9, bf16[96,4096]{1,0:T(8,128)(2,1)} %collective-permute-done.14.refs_1_, bf16[96,4096]{1,0:T(8,128)(2,1)S(1)} %collective-permute-done.12.refs_2_, bf16[96,4096]{1,0:T(8,128)(2,1)S(1)} %collective-permute-done.18.refs_3_, ...), custom_call_target="tpu_custom_call" | custom-call | flops 2415919104 | bytes 13631488 | tf_op jit(solution)/shard_map/forward/pallas_call | solution.py:135
  201.0 4.1 %collective-permute-done.13.refs_0_ = bf16[96,4096]{1,0:T(8,128)(2,1)S(1)} collective-permute-done((bf16[96,4096]{1,0:T(8,128)(2,1)S(1)}, bf16[96,4096]{1,0:T(8,128)(2,1)S(1)}, u32[]{:S(2)}, u32[]{:S(2)}) %collective-permute-start.13) | collective-permute-done | bytes 786464 | tf_op jit(solution)/shard_map/ppermute | solution.py:41
  205.0 2.9 %collective-permute-done.16.refs_1_ = bf16[96,4096]{1,0:T(8,128)(2,1)S(1)} collective-permute-done((bf16[96,4096]{1,0:T(8,128)(2,1)S(1)}, bf16[96,4096]{1,0:T(8,128)(2,1)S(1)}, u32[]{:S(2)}, u32[]{:S(2)}) %collective-permute-start.16) | collective-permute-done | bytes 786464 | tf_op jit(solution)/shard_map/ppermute | solution.py:41
  213.6 9.1 %all_to_all.21 = f32[8,1,2304]{2,1,0:T(1,128)S(1)} all-to-all(f32[8,1,2304]{2,1,0:T(1,128)S(1)} %broadcast_in_dim.11), channel_id=1, replica_groups=mesh['xl'=2,'z'=4,'y'=4,'xh'=2,'c'=2] {'y','xh'}, dimensions={0} | all-to-all | bytes 147456 | tf_op jit(solution)/shard_map/all_to_all | solution.py:46
  225.6 3.3 %convolution_convert_fusion = bf16[4096,256]{1,0:T(8,128)(2,1)} fusion(bf16[768,4096]{1,0:T(8,128)(2,1)S(1)} %copy-done.17, bf16[768,512]{1,0:T(8,128)(2,1)S(1)} %get-tuple-element.45), kind=kOutput, calls=%fused_computation.8 | convolution fusion | flops 1611661312 | bytes 8781824 | tf_op jit(solution)/shard_map/td,tf->df/dot_general | solution.py:249
  230.5 3.8 %collective-permute-done.22 = f32[512]{0:T(512)S(1)} collective-permute-done((f32[512]{0:T(512)S(1)}, f32[512]{0:T(512)S(1)}, u32[]{:S(2)}, u32[]{:S(2)}) %collective-permute-start.22) | collective-permute-done | bytes 2080 | tf_op jit(solution)/shard_map/ppermute | solution.py:28
  234.6 5.5 %convolution_add_fusion = f32[4096,256]{1,0:T(8,128)S(1)} fusion(bf16[768,4096]{1,0:T(8,128)(2,1)} %get-tuple-element.24, bf16[4096,256]{1,0:T(8,128)(2,1)} %collective-permute-done.21, bf16[768,512]{1,0:T(8,128)(2,1)S(1)} %get-tuple-element.45), kind=kOutput, calls=%fused_computation.7 | convolution fusion | flops 1612709888 | bytes 12976128 | tf_op jit(solution)/shard_map/td,tf->df/dot_general | solution.py:249
  240.2 3.3 %fusion.1 = bf16[4096,256]{1,0:T(8,128)(2,1)S(1)} fusion(bf16[4096,256]{1,0:T(8,128)(2,1)S(1)} %copy-done.13, bf16[4096,256]{1,0:T(8,128)(2,1)S(1)} %copy-done.14, bf16[4096,256]{1,0:T(8,128)(2,1)S(1)} %copy-done.12, f32[4096,256]{1,0:T(8,128)S(1)} %convolution_add_fusion), kind=kLoop, calls=%fused_computation.13 | loop fusion | flops 23068672 | bytes 12582912 | tf_op jit(solution)/shard_map/convert_element_type | solution.py:282
  243.7 29.6 %all_to_all.22 = bf16[8,528,256]{2,1,0:T(8,128)(2,1)S(1)} all-to-all(bf16[8,528,256]{2,1,0:T(8,128)(2,1)S(1)} %fusion.13), channel_id=1, replica_groups=mesh['xl'=2,'z'=4,'y'=4,'xh'=2,'c'=2] {'xl','z'}, dimensions={0} | all-to-all | bytes 4325376 | tf_op jit(solution)/shard_map/all_to_all | solution.py:285
  (146 shorter events, 41.9 us)
Async XLA Ops:
  2.4 7.9 %collective-permute-start = (bf16[528,256]{1,0:T(8,128)(2,1)S(1)}, bf16[528,256]{1,0:T(8,128)(2,1)S(1)}, u32[]{:S(2)}, u32[]{:S(2)}) collective-permute-start(bf16[528,256]{1,0:T(8,128)(2,1)S(1)} %fusion.36), channel_id=1, source_target_pairs={{0,64},{64,0},{1,65},{65,1},{2,66},{66,2},{3,67},{67,3},{4,68},{68... | collective-permute-start | bytes 811016 | tf_op jit(solution)/shard_map/ppermute | solution.py:189
  10.6 33.4 %copy-start.19 = (bf16[1,2,96,4096]{3,2,1,0:T(8,128)(2,1)S(1)}, bf16[1,2,96,4096]{3,2,1,0:T(8,128)(2,1)}, u32[]{:S(2)}) copy-start(bf16[1,2,96,4096]{3,2,1,0:T(8,128)(2,1)} %param.11) | copy-start | bytes 4718596
  41.0 44.5 %copy-start = (bf16[4,2,528,256]{3,2,1,0:T(8,128)(2,1)}, bf16[4,2,528,256]{3,2,1,0:T(8,128)(2,1)S(1)}, u32[]{:S(2)}) copy-start(bf16[4,2,528,256]{3,2,1,0:T(8,128)(2,1)S(1)} %all_to_all.20.refs_5_.refs_3_) | copy-start | bytes 6488068
  41.0 44.6 %collective-permute-start.5 = (bf16[4,2,528,256]{3,2,1,0:T(8,128)(2,1)S(1)}, bf16[4,2,528,256]{3,2,1,0:T(8,128)(2,1)}, u32[]{:S(2)}, u32[]{:S(2)}) collective-permute-start(bf16[4,2,528,256]{3,2,1,0:T(8,128)(2,1)S(1)} %all_to_all.20.refs_5_.refs_3_), channel_id=1, source_target_pairs={{0,1},{1,0},{2,3},{3,2},{4,5},{5,4},{6,7},{7,6},{8,9},{9,8},{10,11... | collective-permute-start | bytes 6488072 | tf_op jit(solution)/shard_map/ppermute | solution.py:28
  45.3 20.8 %collective-permute-start.1 = (bf16[96,4096]{1,0:T(8,128)(2,1)}, bf16[96,4096]{1,0:T(8,128)(2,1)}, u32[]{:S(2)}, u32[]{:S(2)}) collective-permute-start(bf16[96,4096]{1,0:T(8,128)(2,1)} %get-tuple-element.57.refs_0_), channel_id=1, source_target_pairs={{0,2},{2,0},{1,3},{3,1},{4,6},{6,4},{5,7},{7,5},{8,10},{10,8},{9,1... | collective-permute-start | bytes 2359304 | tf_op jit(solution)/shard_map/ppermute | solution.py:32
  49.6 17.7 %collective-permute-start.6 = (bf16[2,8,96,256]{3,2,1,0:T(8,128)(2,1)S(1)}, bf16[2,8,96,256]{3,2,1,0:T(8,128)(2,1)S(1)}, u32[]{:S(2)}, u32[]{:S(2)}) collective-permute-start(bf16[2,8,96,256]{3,2,1,0:T(8,128)(2,1)S(1)} %get-tuple-element.55), channel_id=1, source_target_pairs={{0,1},{1,0},{2,3},{3,2},{4,5},{5,4},{6,7},{7,6},{8,9},{9,8},{10,11... | collective-permute-start | bytes 2359304 | tf_op jit(solution)/shard_map/ppermute | solution.py:28
  50.1 18.6 %collective-permute-start.7 = (bf16[96,4096]{1,0:T(8,128)(2,1)}, bf16[96,4096]{1,0:T(8,128)(2,1)}, u32[]{:S(2)}, u32[]{:S(2)}) collective-permute-start(bf16[96,4096]{1,0:T(8,128)(2,1)} %get-tuple-element.57.refs_0_), channel_id=1, source_target_pairs={{0,4},{1,13},{4,8},{5,1},{8,12},{9,5},{12,0},{13,9},{2,6},{3,15},{... | collective-permute-start | bytes 2359304 | tf_op jit(solution)/shard_map/ppermute | solution.py:41
  53.0 17.1 %collective-permute-start.10 = (bf16[2,8,96,256]{3,2,1,0:T(8,128)(2,1)S(1)}, bf16[2,8,96,256]{3,2,1,0:T(8,128)(2,1)S(1)}, u32[]{:S(2)}, u32[]{:S(2)}) collective-permute-start(bf16[2,8,96,256]{3,2,1,0:T(8,128)(2,1)S(1)} %get-tuple-element.53), channel_id=1, source_target_pairs={{0,1},{1,0},{2,3},{3,2},{4,5},{5,4},{6,7},{7,6},{8,9},{9,8},{10,11... | collective-permute-start | bytes 2359304 | tf_op jit(solution)/shard_map/ppermute | solution.py:28
  66.1 16.0 %collective-permute-start.3 = (bf16[96,4096]{1,0:T(8,128)(2,1)}, bf16[96,4096]{1,0:T(8,128)(2,1)}, u32[]{:S(2)}, u32[]{:S(2)}) collective-permute-start(bf16[96,4096]{1,0:T(8,128)(2,1)} %collective-permute-done.1.refs_1_), channel_id=1, source_target_pairs={{0,12},{1,5},{4,0},{5,9},{8,4},{9,13},{12,8},{13,1},{2,14},{3,7},{... | collective-permute-start | bytes 2359304 | tf_op jit(solution)/shard_map/ppermute | solution.py:41
  67.4 31.5 %collective-permute-start.8 = (bf16[96,4096]{1,0:T(8,128)(2,1)}, bf16[96,4096]{1,0:T(8,128)(2,1)}, u32[]{:S(2)}, u32[]{:S(2)}) collective-permute-start(bf16[96,4096]{1,0:T(8,128)(2,1)} %get-tuple-element.57.refs_0_), channel_id=1, source_target_pairs={{0,12},{1,5},{4,0},{5,9},{8,4},{9,13},{12,8},{13,1},{2,14},{3,7},{... | collective-permute-start | bytes 2359304 | tf_op jit(solution)/shard_map/ppermute | solution.py:41
  68.7 30.2 %collective-permute-start.9 = (bf16[96,4096]{1,0:T(8,128)(2,1)}, bf16[96,4096]{1,0:T(8,128)(2,1)}, u32[]{:S(2)}, u32[]{:S(2)}) collective-permute-start(bf16[96,4096]{1,0:T(8,128)(2,1)} %collective-permute-done.7.refs_2_), channel_id=1, source_target_pairs={{0,4},{1,13},{4,8},{5,1},{8,12},{9,5},{12,0},{13,9},{2,6},{3,15},{... | collective-permute-start | bytes 2359304 | tf_op jit(solution)/shard_map/ppermute | solution.py:41
  70.0 38.2 %collective-permute-start.2 = (bf16[96,4096]{1,0:T(8,128)(2,1)}, bf16[96,4096]{1,0:T(8,128)(2,1)}, u32[]{:S(2)}, u32[]{:S(2)}) collective-permute-start(bf16[96,4096]{1,0:T(8,128)(2,1)} %collective-permute-done.1.refs_1_), channel_id=1, source_target_pairs={{0,4},{1,13},{4,8},{5,1},{8,12},{9,5},{12,0},{13,9},{2,6},{3,15},{... | collective-permute-start | bytes 2359304 | tf_op jit(solution)/shard_map/ppermute | solution.py:41
  82.0 30.1 %collective-permute-start.4 = (bf16[96,4096]{1,0:T(8,128)(2,1)}, bf16[96,4096]{1,0:T(8,128)(2,1)}, u32[]{:S(2)}, u32[]{:S(2)}) collective-permute-start(bf16[96,4096]{1,0:T(8,128)(2,1)} %collective-permute-done.3.refs_1_), channel_id=1, source_target_pairs={{0,12},{1,5},{4,0},{5,9},{8,4},{9,13},{12,8},{13,1},{2,14},{3,7},{... | collective-permute-start | bytes 2359304 | tf_op jit(solution)/shard_map/ppermute | solution.py:41
  85.5 68.5 %collective-permute-start.14 = (bf16[96,4096]{1,0:T(8,128)(2,1)}, bf16[96,4096]{1,0:T(8,128)(2,1)}, u32[]{:S(2)}, u32[]{:S(2)}) collective-permute-start(bf16[96,4096]{1,0:T(8,128)(2,1)} %get-tuple-element.58.refs_0_), channel_id=1, source_target_pairs={{0,2},{2,0},{1,3},{3,1},{4,6},{6,4},{5,7},{7,5},{8,10},{10,8},{9,1... | collective-permute-start | bytes 2359304 | tf_op jit(solution)/shard_map/ppermute | solution.py:32
  100.0 12.2 %copy-start.1 = (bf16[4,2,528,256]{3,2,1,0:T(8,128)(2,1)S(1)}, bf16[4,2,528,256]{3,2,1,0:T(8,128)(2,1)}, u32[]{:S(2)}) copy-start(bf16[4,2,528,256]{3,2,1,0:T(8,128)(2,1)} %copy-done) | copy-start | bytes 6488068
  112.2 6.7 %copy-start.16 = (bf16[1,8,96,512]{3,2,1,0:T(8,128)(2,1)S(1)}, bf16[1,8,96,512]{3,2,1,0:T(8,128)(2,1)}, u32[]{:S(2)}) copy-start(bf16[1,8,96,512]{3,2,1,0:T(8,128)(2,1)} %get-tuple-element.50) | copy-start | bytes 2359300
  120.1 12.4 %all-to-all-start.1 = ((f32[8,1,2304]{2,1,0:T(1,128)}), f32[8,1,2304]{2,1,0:T(1,128)S(1)}, u32[]{:S(2)}, u32[]{:S(2)}) async-start(f32[8,1,2304]{2,1,0:T(1,128)} %broadcast_in_dim.10), calls=%async_computation.1 | async-start | bytes 147456 | tf_op jit(solution)/shard_map/all_to_all | solution.py:46
  135.4 10.4 %slice-start = ((s8[6291456]{0:T(1024)(128)(4,1)}), s8[4194304]{0:T(1024)(128)(4,1)S(1)}, s32[]{:S(2)}) async-start(s8[6291456]{0:T(1024)(128)(4,1)} %bitcast.97), calls=%async_computation.4 | async-start | bytes 8388608
  135.4 10.2 %copy-start.10 = (bf16[4096,256]{1,0:T(8,128)(2,1)S(1)}, bf16[4096,256]{1,0:T(8,128)(2,1)}, u32[]{:S(2)}) copy-start(bf16[4096,256]{1,0:T(8,128)(2,1)} %fusion.44) | copy-start | bytes 6291460
  135.4 10.3 %slice-start.1 = ((s8[6291456]{0:T(1024)(128)(4,1)}), s8[2097152]{0:T(1024)(128)(4,1)S(1)}, s32[]{:S(2)}) async-start(s8[6291456]{0:T(1024)(128)(4,1)} %bitcast.97), calls=%async_computation.5 | async-start | bytes 4194304
  140.2 9.1 %collective-permute-start.11 = (bf16[4096,256]{1,0:T(8,128)(2,1)S(1)}, bf16[4096,256]{1,0:T(8,128)(2,1)S(1)}, u32[]{:S(2)}, u32[]{:S(2)}) collective-permute-start(bf16[4096,256]{1,0:T(8,128)(2,1)S(1)} %convolution_convert_fusion.1), channel_id=1, source_target_pairs={{0,1},{1,0},{2,3},{3,2},{4,5},{5,4},{6,7},{7,6},{8,9},{9,8},{10,11... | collective-permute-start | bytes 6291464 | tf_op jit(solution)/shard_map/ppermute | solution.py:28
  152.8 39.1 %copy-start.4 = (bf16[4096,256]{1,0:T(8,128)(2,1)}, bf16[4096,256]{1,0:T(8,128)(2,1)S(1)}, u32[]{:S(2)}) copy-start(bf16[4096,256]{1,0:T(8,128)(2,1)S(1)} %get-tuple-element.21) | copy-start | bytes 6291460
  152.8 39.1 %collective-permute-start.17 = (bf16[8,512,256]{2,1,0:T(8,128)(2,1)S(1)}, bf16[8,512,256]{2,1,0:T(8,128)(2,1)S(1)}, u32[]{:S(2)}, u32[]{:S(2)}) collective-permute-start(bf16[8,512,256]{2,1,0:T(8,128)(2,1)S(1)} %bitcast.89), channel_id=1, source_target_pairs={{0,1},{1,0},{2,3},{3,2},{4,5},{5,4},{6,7},{7,6},{8,9},{9,8},{10,11... | collective-permute-start | bytes 6291464 | tf_op jit(solution)/shard_map/ppermute | solution.py:28
  153.1 18.2 %collective-permute-start.12 = (bf16[96,4096]{1,0:T(8,128)(2,1)S(1)}, bf16[96,4096]{1,0:T(8,128)(2,1)S(1)}, u32[]{:S(2)}, u32[]{:S(2)}) collective-permute-start(bf16[96,4096]{1,0:T(8,128)(2,1)S(1)} %copy-done.9), channel_id=1, source_target_pairs={{0,4},{1,13},{4,8},{5,1},{8,12},{9,5},{12,0},{13,9},{2,6},{3,15},{... | collective-permute-start | bytes 2359304 | tf_op jit(solution)/shard_map/ppermute | solution.py:41
  154.0 21.0 %collective-permute-start.15 = (bf16[96,4096]{1,0:T(8,128)(2,1)}, bf16[96,4096]{1,0:T(8,128)(2,1)S(1)}, u32[]{:S(2)}, u32[]{:S(2)}) collective-permute-start(bf16[96,4096]{1,0:T(8,128)(2,1)} %collective-permute-done.14.refs_1_), channel_id=1, source_target_pairs={{0,12},{1,5},{4,0},{5,9},{8,4},{9,13},{12,8},{13,1},{2,14},{3,7},{... | collective-permute-start | bytes 2359304 | tf_op jit(solution)/shard_map/ppermute | solution.py:41
  154.6 37.3 %collective-permute-start.18 = (bf16[96,4096]{1,0:T(8,128)(2,1)S(1)}, bf16[96,4096]{1,0:T(8,128)(2,1)S(1)}, u32[]{:S(2)}, u32[]{:S(2)}) collective-permute-start(bf16[96,4096]{1,0:T(8,128)(2,1)S(1)} %copy-done.9), channel_id=1, source_target_pairs={{0,12},{1,5},{4,0},{5,9},{8,4},{9,13},{12,8},{13,1},{2,14},{3,7},{... | collective-permute-start | bytes 2359304 | tf_op jit(solution)/shard_map/ppermute | solution.py:41
  154.9 37.0 %collective-permute-start.19 = (bf16[96,4096]{1,0:T(8,128)(2,1)}, bf16[96,4096]{1,0:T(8,128)(2,1)S(1)}, u32[]{:S(2)}, u32[]{:S(2)}) collective-permute-start(bf16[96,4096]{1,0:T(8,128)(2,1)} %collective-permute-done.14.refs_1_), channel_id=1, source_target_pairs={{0,4},{1,13},{4,8},{5,1},{8,12},{9,5},{12,0},{13,9},{2,6},{3,15},{... | collective-permute-start | bytes 2359304 | tf_op jit(solution)/shard_map/ppermute | solution.py:41
  171.3 3.9 %collective-permute-start.20 = (f32[512]{0:T(512)S(1)}, f32[512]{0:T(512)S(1)}, u32[]{:S(2)}, u32[]{:S(2)}) collective-permute-start(f32[512]{0:T(512)S(1)} %get-tuple-element.47), channel_id=1, source_target_pairs={{0,1},{1,0},{2,3},{3,2},{4,5},{5,4},{6,7},{7,6},{8,9},{9,8},{10,11... | collective-permute-start | bytes 6152 | tf_op jit(solution)/shard_map/ppermute | solution.py:28
  175.0 30.0 %collective-permute-start.13 = (bf16[96,4096]{1,0:T(8,128)(2,1)S(1)}, bf16[96,4096]{1,0:T(8,128)(2,1)S(1)}, u32[]{:S(2)}, u32[]{:S(2)}) collective-permute-start(bf16[96,4096]{1,0:T(8,128)(2,1)S(1)} %collective-permute-done.12.refs_2_), channel_id=1, source_target_pairs={{0,4},{1,13},{4,8},{5,1},{8,12},{9,5},{12,0},{13,9},{2,6},{3,15},{... | collective-permute-start | bytes 2359304 | tf_op jit(solution)/shard_map/ppermute | solution.py:41
  175.2 32.7 %collective-permute-start.16 = (bf16[96,4096]{1,0:T(8,128)(2,1)S(1)}, bf16[96,4096]{1,0:T(8,128)(2,1)S(1)}, u32[]{:S(2)}, u32[]{:S(2)}) collective-permute-start(bf16[96,4096]{1,0:T(8,128)(2,1)S(1)} %collective-permute-done.15.refs_5_), channel_id=1, source_target_pairs={{0,12},{1,5},{4,0},{5,9},{8,4},{9,13},{12,8},{13,1},{2,14},{3,7},{... | collective-permute-start | bytes 2359304 | tf_op jit(solution)/shard_map/ppermute | solution.py:41
  228.9 5.7 %collective-permute-start.21 = (bf16[4096,256]{1,0:T(8,128)(2,1)}, bf16[4096,256]{1,0:T(8,128)(2,1)}, u32[]{:S(2)}, u32[]{:S(2)}) collective-permute-start(bf16[4096,256]{1,0:T(8,128)(2,1)} %convolution_convert_fusion), channel_id=1, source_target_pairs={{0,1},{1,0},{2,3},{3,2},{4,5},{5,4},{6,7},{7,6},{8,9},{9,8},{10,11... | collective-permute-start | bytes 6291464 | tf_op jit(solution)/shard_map/ppermute | solution.py:28
  230.2 4.1 %collective-permute-start.22 = (f32[512]{0:T(512)S(1)}, f32[512]{0:T(512)S(1)}, u32[]{:S(2)}, u32[]{:S(2)}) collective-permute-start(f32[512]{0:T(512)S(1)} %get-tuple-element.46), channel_id=1, source_target_pairs={{0,1},{1,0},{2,3},{3,2},{4,5},{5,4},{6,7},{7,6},{8,9},{9,8},{10,11... | collective-permute-start | bytes 6152 | tf_op jit(solution)/shard_map/ppermute | solution.py:28
  (18 other events, 50.6 us)

commit v4 on v3

--- a/solution.py
+++ b/solution.py
@@ -58,15 +58,13 @@
 
 
 BLOCK = 96
-VMEM_LIMIT = 46 * 1024 * 1024
+VMEM_LIMIT = 40 * 1024 * 1024
 
 
 LETTERS = "oxabcefg"
-SOON = ("oxabf", "oxabce")
-LATE = ("ceg", "fg")
-
-
-def forward_kernel(letters, pieces, weight, weight_other, flow, residual_out, rows_out, rows, made, came, left, sent):
+
+
+def forward_kernel(letters, pieces, weight, weight_other, flow, residual_out, rows_out, rows, weights, held, made, came, loaded, streamed, left, sent):
     y, xh, c = lax.axis_index("y"), lax.axis_index("xh"), lax.axis_index("c")
     d = 1 - 2 * c
     before, after, across = (y + 4 - d) % 4, (y + 4 + d) % 4, (y + 2) % 4
@@ -81,6 +79,16 @@
     own = [pl.ds(at * BLOCK, BLOCK) for at in range(len(letters))]
     owned, wide = D // 8, flow.shape[1] // 2
 
+    loads = [
+        pltpu.make_async_copy(
+            source.at[:, pl.ds(0, owned)], weights.at[half], loaded.at[half]
+        )
+        for half, source in enumerate((weight, weight_other))
+    ]
+    flows = [
+        pltpu.make_async_copy(flow.at[to], held.at[at], streamed.at[i])
+        for i, (at, to) in enumerate(zip(own, places))
+    ]
     takes = [
         pltpu.make_async_copy(source, rows.at[at], came.at[i])
         for i, (at, source) in enumerate(zip(own, pieces))
@@ -93,29 +101,20 @@
         pltpu.make_async_copy(made.at[at], residual_out.at[to], sent.at[i])
         for i, (at, to) in enumerate(zip(own, places))
     ]
-    for take in takes:
-        take.start()
+    for copy in (loads[0], *takes, *flows, loads[1]):
+        copy.start()
     for take, give in zip(takes, gives):
         take.wait()
         give.start()
-    for half, source in enumerate((weight, weight_other)):
-        projected = 0.0
-        for slab in range(8):
-            if len(source.shape) == 3:
-                part = source[slab]
-            else:
-                part = source[slab % 4, slab // 4, :owned]
-            projected += jnp.dot(
-                rows[:, slab * owned : (slab + 1) * owned],
-                part,
-                preferred_element_type=jnp.float32,
-            )
+    for load in flows:
+        load.wait()
+    for half in range(2):
+        loads[half].wait()
+        projected = jnp.dot(
+            rows[...], weights[half].reshape(D, wide), preferred_element_type=jnp.float32
+        )
         columns = slice(half * wide, (half + 1) * wide)
-        for at, (mine, to) in enumerate(zip(own, places)):
-            made[mine, columns] = (
-                flow[to, columns].astype(jnp.float32)
-                + projected[at * BLOCK : (at + 1) * BLOCK] * D ** (-0.5)
-            )
+        made[:, columns] = held[:, columns].astype(jnp.float32) + projected * D ** (-0.5)
     for send in sends:
         send.start()
     for copy in (*gives, *sends):
@@ -124,7 +123,6 @@
 
 def forward(letters, pieces, weight, weight_other, flow, earlier=()):
     anywhere = pl.BlockSpec(memory_space=pl.ANY)
-    inside = pl.BlockSpec(memory_space=pltpu.VMEM)
     count = len(letters)
     tokens, features = flow.shape
 
@@ -138,11 +136,15 @@
             jax.ShapeDtypeStruct((tokens, features), jnp.float32),
             jax.ShapeDtypeStruct((tokens, D), jnp.bfloat16),
         ),
-        in_specs=[anywhere] * count + [inside] * 3 + [anywhere] * len(earlier),
+        in_specs=[anywhere] * (count + 3 + len(earlier)),
         out_specs=(anywhere, anywhere),
         scratch_shapes=[
             pltpu.VMEM((count * BLOCK, D), jnp.bfloat16),
+            pltpu.VMEM((2, 8, D // 8, features // 2), jnp.bfloat16),
+            pltpu.VMEM((count * BLOCK, features), jnp.bfloat16),
             pltpu.VMEM((count * BLOCK, features), jnp.float32),
+            pltpu.SemaphoreType.DMA((count,)),
+            pltpu.SemaphoreType.DMA((2,)),
             pltpu.SemaphoreType.DMA((count,)),
             pltpu.SemaphoreType.DMA((count,)),
             pltpu.SemaphoreType.DMA((count,)),
@@ -186,20 +188,11 @@
 
     owned, share = weight_master.shape[0], gain_master.shape[0]
     packed = with_gain(weight_master.astype(jnp.bfloat16), gain_master.astype(jnp.bfloat16))
-    beyond = lax.ppermute(packed, "xl", [(0, 1), (1, 0)])
-    low = lax.axis_index("xl") == 0
-    pair = jnp.stack([jnp.where(low, packed, beyond), jnp.where(low, beyond, packed)])
-    packed = copy_for_each(pair, "z")
+    packed = copy_for_each(packed, ISLAND)
     packed_other = core_swap(packed)
-
-    def in_island_order(value):
-        return jnp.swapaxes(value, 0, 1)
-
-    slabs = [packed[z, xl, :owned] for xl in range(2) for z in range(4)]
-    anchor_low = lax.optimization_barrier(jnp.concatenate(slabs, axis=0))
-    gain_anchor = in_island_order(packed[:, :, owned, :share]).reshape(wide).astype(jnp.float32)
-    gain_other = in_island_order(packed_other[:, :, owned, :share]).reshape(wide)
-    gain_other = gain_other.astype(jnp.float32)
+    anchor_low = packed[:, :owned].reshape(D, wide)
+    gain_anchor = packed[:, owned, :share].reshape(wide).astype(jnp.float32)
+    gain_other = packed_other[:, owned, :share].reshape(wide).astype(jnp.float32)
 
     def token_half(value):
         blocks = value[0].reshape(STEPS, 8, 2, 96, wide)
@@ -219,11 +212,7 @@
         else:
             held = weight_low.reshape(islands, owned, wide)
             held_other = core_swap(held)
-        earlier = ()
-        for letters in (SOON[step], LATE[step]):
-            some = [pieces[step][LETTERS.index(letter)] for letter in letters]
-            earlier = forward(letters, some, held, held_other, stream_half[step], earlier)
-        residual, rows = earlier
+        residual, rows = forward(LETTERS, pieces[step], held, held_other, stream_half[step])
         goal = target_half[step].astype(jnp.float32)
         scaled = residual * gain
         sums = [
@@ -252,10 +241,8 @@
 
         other = over_tokens(slice(wide, None)).astype(jnp.bfloat16)
         other = core_swap(other)
-        mine = over_tokens(slice(0, wide))
-        if step == 0:
-            mine = lax.optimization_barrier(mine)
-        weight_grad = (mine + other.astype(jnp.float32)) * width_scale
+        mine = lax.optimization_barrier(over_tokens(slice(0, wide)).astype(jnp.bfloat16))
+        weight_grad = (mine.astype(jnp.float32) + other.astype(jnp.float32)) * width_scale
         gain_other = core_swap(gain_grad)
         gain_grad = gain_grad + jnp.concatenate([gain_other[wide:], gain_other[:wide]])
         if step == 0:

time: 277 us -> 287 us (1.036)
  blocking collectives: 69.1 us -> 84.1 us
  starting transfers between devices: 40.2 us -> 29 us
  waiting for transfers between devices: 92.9 us -> 102 us
  local copies, waits for them, and re-layouts: 15.7 us -> 12.2 us
    all_to_all x2 -> x3, blocking collectives: 39.5 us -> 54.5 us  [copy_for_each(): return lax.all_to_all(copies, axis, split_axis=0, concat_axis=0, tiled=True)]
    ppermute x12, waiting for transfers between devices: 62.4 us -> 76.6 us  [y_hop(): return lax.ppermute(value, ('y', 'c'), pairs)]
    ppermute x2, waiting for transfers between devices: 13 us -> 24.7 us  [x_swap(): return lax.ppermute(value, 'xh', [(0, 1), (1, 0)])]
    all_to_all x1 -> x0, waiting for transfers between devices: 6.01 us -> none  [copy_for_each(): return lax.all_to_all(copies, axis, split_axis=0, concat_axis=0, tiled=True)]
    ppermute x1 -> x0, waiting for transfers between devices: 5.77 us -> none  [per_device(): beyond = lax.ppermute(packed, 'xl', [(0, 1), (1, 0)])]
    all_to_all x1 -> x0, starting transfers between devices: 5.67 us -> none  [copy_for_each(): return lax.all_to_all(copies, axis, split_axis=0, concat_axis=0, tiled=True)]
    ppermute x8, waiting for transfers between devices: 5.74 us -> 1.2 us  [core_swap(): return lax.ppermute(value, 'c', [(0, 1), (1, 0)])]
    unnamed x62 -> x38, local copies, waits for them, and re-layouts: 10.4 us -> 7.62 us
  transfers between devices with their start and end apart: 24 -> 22, of which waited for: 14 -> 11; matrix products, arithmetic and copies ran while one was open for 8% -> 7% of each run, Pallas kernels for 8% -> 0%
where the time goes in v4:
time: 287 us; the launch traced here: 286 us
  waiting for transfers between devices  102 us (36%)
  blocking collectives  84.1 us (29%)
  starting transfers between devices  29 us (10%)
  Pallas kernels  24.8 us (9%)
  other arithmetic  19.4 us (7%)
  matrix products  13.4 us (5%)
  local copies, waits for them, and re-layouts  12.2 us (4%)
    ppermute x12, waiting for transfers between devices, y_hop(): return lax.ppermute(value, ('y', 'c'), pairs)  76.6 us
    all_to_all x3, blocking collectives, copy_for_each(): return lax.all_to_all(copies, axis, split_axis=0, concat_axis=0, tiled=True)  54.5 us
    all_to_all x1, blocking collectives, per_device(): lax.all_to_all(sent, ISLAND, split_axis=0, concat_axis=0, tiled=True)  29.6 us
    pallas_call x2, Pallas kernels, forward(): pl.pallas_call(kernel, out_shape=(jax.ShapeDtypeStruct((tokens, features)...  24.8 us
    ppermute x2, waiting for transfers between devices, x_swap(): return lax.ppermute(value, 'xh', [(0, 1), (1, 0)])  24.7 us
    dot_general x4, matrix products, over_tokens(): jnp.einsum('td,tf->df', rows, residual_grad[:, columns], preferred_elemen...  13.4 us
    ppermute x12, starting transfers between devices, y_hop(): return lax.ppermute(value, ('y', 'c'), pairs)  13.2 us
    ppermute x8, starting transfers between devices, core_swap(): return lax.ppermute(value, 'c', [(0, 1), (1, 0)])  12.8 us
  transfers between devices with their start and end apart: 22, of which 11 were waited for; matrix products, arithmetic and copies ran while one was open for 7% of the time, Pallas kernels for 0%

profile of v4, /device:TPU:1, one launch (start us, length us, event | category | flops | bytes accessed | tf_op | source)
XLA Modules:
  0.0 286.3 jit_solution(15457672301773881231)
XLA Ops:
  2.5 33.4 %all_to_all.20.refs_8_ = bf16[8,528,256]{2,1,0:T(8,128)(2,1)S(1)} all-to-all(bf16[8,528,256]{2,1,0:T(8,128)(2,1)S(1)} %broadcast_in_dim.9), channel_id=1, replica_groups=mesh['xl'=2,'z'=4,'y'=4,'xh'=2,'c'=2] {'xl','z'}, dimensions={0} | all-to-all | bytes 4325376 | tf_op jit(solution)/shard_map/all_to_all | solution.py:46
  36.0 2.3 collective-permute-start.7
  39.3 2.5 collective-permute-start
  41.8 2.7 collective-permute-start.1
  46.9 13.2 %collective-permute-done.refs_1_ = bf16[96,4096]{1,0:T(8,128)(2,1)} collective-permute-done((bf16[96,4096]{1,0:T(8,128)(2,1)}, bf16[96,4096]{1,0:T(8,128)(2,1)}, u32[]{:S(2)}, u32[]{:S(2)}) %collective-permute-start) | collective-permute-done | bytes 786464 | tf_op jit(solution)/shard_map/ppermute | solution.py:32
  64.4 11.7 %collective-permute-done.4.refs_5_ = bf16[96,4096]{1,0:T(8,128)(2,1)} collective-permute-done((bf16[96,4096]{1,0:T(8,128)(2,1)}, bf16[96,4096]{1,0:T(8,128)(2,1)}, u32[]{:S(2)}, u32[]{:S(2)}) %collective-permute-start.4) | collective-permute-done | bytes 786464 | tf_op jit(solution)/shard_map/ppermute | solution.py:41
  80.5 12.3 %collective-permute-done.2.refs_3_ = bf16[96,4096]{1,0:T(8,128)(2,1)} collective-permute-done((bf16[96,4096]{1,0:T(8,128)(2,1)}, bf16[96,4096]{1,0:T(8,128)(2,1)}, u32[]{:S(2)}, u32[]{:S(2)}) %collective-permute-start.2) | collective-permute-done | bytes 786464 | tf_op jit(solution)/shard_map/ppermute | solution.py:41
  92.9 6.5 %collective-permute-done.5.refs_6_ = bf16[96,4096]{1,0:T(8,128)(2,1)} collective-permute-done((bf16[96,4096]{1,0:T(8,128)(2,1)}, bf16[96,4096]{1,0:T(8,128)(2,1)}, u32[]{:S(2)}, u32[]{:S(2)}) %collective-permute-start.5) | collective-permute-done | bytes 786464 | tf_op jit(solution)/shard_map/ppermute | solution.py:41
  99.4 6.8 %collective-permute-done.6.refs_7_ = bf16[96,4096]{1,0:T(8,128)(2,1)} collective-permute-done((bf16[96,4096]{1,0:T(8,128)(2,1)}, bf16[96,4096]{1,0:T(8,128)(2,1)}, u32[]{:S(2)}, u32[]{:S(2)}) %collective-permute-start.6) | collective-permute-done | bytes 786464 | tf_op jit(solution)/shard_map/ppermute | solution.py:41
  106.2 1.6 copy-done.1
  109.0 13.9 %forward.2 = (f32[768,512]{1,0:T(8,128)S(1)}, bf16[768,4096]{1,0:T(8,128)(2,1)}) custom-call(bf16[96,4096]{1,0:T(8,128)(2,1)} %get-tuple-element.53.refs_0_, bf16[96,4096]{1,0:T(8,128)(2,1)} %collective-permute-done.refs_1_, bf16[96,4096]{1,0:T(8,128)(2,1)} %collective-permute-done.1.refs_2_, bf16[96,4096]{1,0:T(8,128)(2,1)} %collective-permute-done.2.refs_3_, ...), custom_call_target="tpu_custom_call" | custom-call | flops 3221225472 | bytes 16777216 | tf_op jit(solution)/shard_map/forward/pallas_call | solution.py:133
  123.4 11.9 %all_to_all.21 = f32[8,1,2304]{2,1,0:T(1,128)S(1)} all-to-all(f32[8,1,2304]{2,1,0:T(1,128)S(1)} %broadcast_in_dim.10), channel_id=1, replica_groups=mesh['xl'=2,'z'=4,'y'=4,'xh'=2,'c'=2] {'y','xh'}, dimensions={0} | all-to-all | bytes 147456 | tf_op jit(solution)/shard_map/all_to_all | solution.py:46
  136.5 1.8 copy-done.16
  138.2 2.0 convolution_convert_fusion.2
  140.2 4.2 %collective-permute-start.10 = (bf16[4096,256]{1,0:T(8,128)(2,1)S(1)}, bf16[4096,256]{1,0:T(8,128)(2,1)S(1)}, u32[]{:S(2)}, u32[]{:S(2)}) collective-permute-start(bf16[4096,256]{1,0:T(8,128)(2,1)S(1)} %convolution_convert_fusion.2), channel_id=1, source_target_pairs={{0,1},{1,0},{2,3},{3,2},{4,5},{5,4},{6,7},{7,6},{8,9},{9,8},{10,11... | collective-permute-start | bytes 6291464 | tf_op jit(solution)/shard_map/ppermute | solution.py:28
  145.0 2.0 convolution_convert_fusion.3
  148.2 3.8 %fusion.49 = (bf16[4096,256]{1,0:T(8,128)(2,1)S(1)}, bf16[4096,256]{1,0:T(8,128)(2,1)}, bf16[4096,256]{1,0:T(8,128)(2,1)}) fusion(bf16[4096,256]{1,0:T(8,128)(2,1)S(1)} %collective-permute-done.10, bf16[4096,256]{1,0:T(8,128)(2,1)S(1)} %convolution_convert_fusion.3, bf16[8,512,256]{2,1,0:T(8,128)(2,1)S(1)} %slice.140), kind=kLoop, calls=%fused_computation.122 | loop fusion | flops 16777216 | bytes 12582912 | tf_op jit(solution)/shard_map/convert_element_type | solution.py:252
  153.2 11.5 %collective-permute-done.11.refs_1_ = bf16[96,4096]{1,0:T(8,128)(2,1)S(1)} collective-permute-done((bf16[96,4096]{1,0:T(8,128)(2,1)S(1)}, bf16[96,4096]{1,0:T(8,128)(2,1)S(1)}, u32[]{:S(2)}, u32[]{:S(2)}) %collective-permute-start.11) | collective-permute-done | bytes 786464 | tf_op jit(solution)/shard_map/ppermute | solution.py:32
  165.0 2.0 collective-permute-start.19
  167.6 2.1 collective-permute-start.14
  169.7 11.9 %collective-permute-done.15.refs_5_ = bf16[96,4096]{1,0:T(8,128)(2,1)S(1)} collective-permute-done((bf16[96,4096]{1,0:T(8,128)(2,1)S(1)}, bf16[96,4096]{1,0:T(8,128)(2,1)S(1)}, u32[]{:S(2)}, u32[]{:S(2)}) %collective-permute-start.15) | collective-permute-done | bytes 786464 | tf_op jit(solution)/shard_map/ppermute | solution.py:41
  183.0 15.4 %collective-permute-done.13.refs_3_ = bf16[96,4096]{1,0:T(8,128)(2,1)S(1)} collective-permute-done((bf16[96,4096]{1,0:T(8,128)(2,1)S(1)}, bf16[96,4096]{1,0:T(8,128)(2,1)S(1)}, u32[]{:S(2)}, u32[]{:S(2)}) %collective-permute-start.13) | collective-permute-done | bytes 786464 | tf_op jit(solution)/shard_map/ppermute | solution.py:41
  198.4 5.6 %collective-permute-done.16.refs_6_ = bf16[96,4096]{1,0:T(8,128)(2,1)S(1)} collective-permute-done((bf16[96,4096]{1,0:T(8,128)(2,1)S(1)}, bf16[96,4096]{1,0:T(8,128)(2,1)S(1)}, u32[]{:S(2)}, u32[]{:S(2)}) %collective-permute-start.16) | collective-permute-done | bytes 786464 | tf_op jit(solution)/shard_map/ppermute | solution.py:41
  204.0 6.5 %collective-permute-done.17.refs_7_ = bf16[96,4096]{1,0:T(8,128)(2,1)S(1)} collective-permute-done((bf16[96,4096]{1,0:T(8,128)(2,1)S(1)}, bf16[96,4096]{1,0:T(8,128)(2,1)S(1)}, u32[]{:S(2)}, u32[]{:S(2)}) %collective-permute-start.17) | collective-permute-done | bytes 786464 | tf_op jit(solution)/shard_map/ppermute | solution.py:41
  210.5 10.9 %forward.3 = (f32[768,512]{1,0:T(8,128)S(1)}, bf16[768,4096]{1,0:T(8,128)(2,1)}) custom-call(bf16[96,4096]{1,0:T(8,128)(2,1)S(1)} %get-tuple-element.54.refs_0_, bf16[96,4096]{1,0:T(8,128)(2,1)S(1)} %collective-permute-done.11.refs_1_, bf16[96,4096]{1,0:T(8,128)(2,1)S(1)} %collective-permute-done.12.refs_2_, ...), custom_call_target="tpu_custom_call" | custom-call | flops 3221225472 | bytes 16777216 | tf_op jit(solution)/shard_map/forward/pallas_call | solution.py:133
  222.0 9.1 %all_to_all.22 = f32[8,1,2304]{2,1,0:T(1,128)S(1)} all-to-all(f32[8,1,2304]{2,1,0:T(1,128)S(1)} %broadcast_in_dim.11), channel_id=1, replica_groups=mesh['xl'=2,'z'=4,'y'=4,'xh'=2,'c'=2] {'y','xh'}, dimensions={0} | all-to-all | bytes 147456 | tf_op jit(solution)/shard_map/all_to_all | solution.py:46
  232.3 2.0 copy-done.17
  234.3 3.3 %convolution_convert_fusion = bf16[4096,256]{1,0:T(8,128)(2,1)} fusion(bf16[768,4096]{1,0:T(8,128)(2,1)S(1)} %copy-done.17, bf16[768,512]{1,0:T(8,128)(2,1)S(1)} %get-tuple-element.37), kind=kOutput, calls=%fused_computation.7 | convolution fusion | flops 1611661312 | bytes 8781824 | tf_op jit(solution)/shard_map/td,tf->df/dot_general | solution.py:238
  237.6 3.5 %collective-permute-start.20 = (bf16[4096,256]{1,0:T(8,128)(2,1)}, bf16[4096,256]{1,0:T(8,128)(2,1)}, u32[]{:S(2)}, u32[]{:S(2)}) collective-permute-start(bf16[4096,256]{1,0:T(8,128)(2,1)} %convolution_convert_fusion), channel_id=1, source_target_pairs={{0,1},{1,0},{2,3},{3,2},{4,5},{5,4},{6,7},{7,6},{8,9},{9,8},{10,11... | collective-permute-start | bytes 6291464 | tf_op jit(solution)/shard_map/ppermute | solution.py:28
  241.3 6.1 %convolution_convert_fusion.1 = bf16[4096,256]{1,0:T(8,128)(2,1)} fusion(bf16[768,4096]{1,0:T(8,128)(2,1)} %get-tuple-element.16, bf16[768,512]{1,0:T(8,128)(2,1)} %copy-done.12), kind=kOutput, calls=%fused_computation.8 | convolution fusion | flops 1611661312 | bytes 8781824 | tf_op jit(solution)/shard_map/td,tf->df/dot_general | solution.py:238
  247.8 5.9 %fusion.1 = bf16[4096,256]{1,0:T(8,128)(2,1)S(1)} fusion(bf16[4096,256]{1,0:T(8,128)(2,1)} %get-tuple-element.13, bf16[4096,256]{1,0:T(8,128)(2,1)} %get-tuple-element.14, bf16[4096,256]{1,0:T(8,128)(2,1)} %collective-permute-done.20, bf16[4096,256]{1,0:T(8,128)(2,1)} %convolution_convert_fusion.1, bf16[8,512,256]{2,1,0:T(8,128)(2,1)S(1)} %copy-done.6), kind=kLoop, calls=%fused_computation.14 | loop fusion | flops 26214400 | bytes 12582912 | tf_op jit(solution)/shard_map/convert_element_type | solution.py:269
  253.8 29.6 %all_to_all.23 = bf16[8,528,256]{2,1,0:T(8,128)(2,1)S(1)} all-to-all(bf16[8,528,256]{2,1,0:T(8,128)(2,1)S(1)} %fusion.13), channel_id=1, replica_groups=mesh['xl'=2,'z'=4,'y'=4,'xh'=2,'c'=2] {'xl','z'}, dimensions={0} | all-to-all | bytes 4325376 | tf_op jit(solution)/shard_map/all_to_all | solution.py:272
  (112 shorter events, 27.5 us)
Async XLA Ops:
  2.5 35.7 %copy-start.10 = (bf16[1,2,96,4096]{3,2,1,0:T(8,128)(2,1)S(1)}, bf16[1,2,96,4096]{3,2,1,0:T(8,128)(2,1)}, u32[]{:S(2)}) copy-start(bf16[1,2,96,4096]{3,2,1,0:T(8,128)(2,1)} %param.11) | copy-start | bytes 4718596
  36.0 43.6 %copy-start = (bf16[8,528,256]{2,1,0:T(8,128)(2,1)}, bf16[8,528,256]{2,1,0:T(8,128)(2,1)S(1)}, u32[]{:S(2)}) copy-start(bf16[8,528,256]{2,1,0:T(8,128)(2,1)S(1)} %all_to_all.20.refs_8_) | copy-start | bytes 6488068
  36.0 43.7 %collective-permute-start.7 = (bf16[8,528,256]{2,1,0:T(8,128)(2,1)S(1)}, bf16[8,528,256]{2,1,0:T(8,128)(2,1)}, u32[]{:S(2)}, u32[]{:S(2)}) collective-permute-start(bf16[8,528,256]{2,1,0:T(8,128)(2,1)S(1)} %all_to_all.20.refs_8_), channel_id=1, source_target_pairs={{0,1},{1,0},{2,3},{3,2},{4,5},{5,4},{6,7},{7,6},{8,9},{9,8},{10,11... | collective-permute-start | bytes 6488072 | tf_op jit(solution)/shard_map/ppermute | solution.py:28
  39.3 20.7 %collective-permute-start = (bf16[96,4096]{1,0:T(8,128)(2,1)}, bf16[96,4096]{1,0:T(8,128)(2,1)}, u32[]{:S(2)}, u32[]{:S(2)}) collective-permute-start(bf16[96,4096]{1,0:T(8,128)(2,1)} %get-tuple-element.53.refs_0_), channel_id=1, source_target_pairs={{0,2},{2,0},{1,3},{3,1},{4,6},{6,4},{5,7},{7,5},{8,10},{10,8},{9,1... | collective-permute-start | bytes 2359304 | tf_op jit(solution)/shard_map/ppermute | solution.py:32
  41.8 20.9 %collective-permute-start.1 = (bf16[96,4096]{1,0:T(8,128)(2,1)}, bf16[96,4096]{1,0:T(8,128)(2,1)}, u32[]{:S(2)}, u32[]{:S(2)}) collective-permute-start(bf16[96,4096]{1,0:T(8,128)(2,1)} %get-tuple-element.53.refs_0_), channel_id=1, source_target_pairs={{0,4},{1,13},{4,8},{5,1},{8,12},{9,5},{12,0},{13,9},{2,6},{3,15},{... | collective-permute-start | bytes 2359304 | tf_op jit(solution)/shard_map/ppermute | solution.py:41
  46.1 15.2 %collective-permute-start.8 = (bf16[2,8,96,256]{3,2,1,0:T(8,128)(2,1)S(1)}, bf16[2,8,96,256]{3,2,1,0:T(8,128)(2,1)S(1)}, u32[]{:S(2)}, u32[]{:S(2)}) collective-permute-start(bf16[2,8,96,256]{3,2,1,0:T(8,128)(2,1)S(1)} %get-tuple-element.51), channel_id=1, source_target_pairs={{0,1},{1,0},{2,3},{3,2},{4,5},{5,4},{6,7},{7,6},{8,9},{9,8},{10,11... | collective-permute-start | bytes 2359304 | tf_op jit(solution)/shard_map/ppermute | solution.py:28
  46.5 17.5 %collective-permute-start.9 = (bf16[2,8,96,256]{3,2,1,0:T(8,128)(2,1)S(1)}, bf16[2,8,96,256]{3,2,1,0:T(8,128)(2,1)S(1)}, u32[]{:S(2)}, u32[]{:S(2)}) collective-permute-start(bf16[2,8,96,256]{3,2,1,0:T(8,128)(2,1)S(1)} %get-tuple-element.49), channel_id=1, source_target_pairs={{0,1},{1,0},{2,3},{3,2},{4,5},{5,4},{6,7},{7,6},{8,9},{9,8},{10,11... | collective-permute-start | bytes 2359304 | tf_op jit(solution)/shard_map/ppermute | solution.py:28
  60.1 15.9 %collective-permute-start.4 = (bf16[96,4096]{1,0:T(8,128)(2,1)}, bf16[96,4096]{1,0:T(8,128)(2,1)}, u32[]{:S(2)}, u32[]{:S(2)}) collective-permute-start(bf16[96,4096]{1,0:T(8,128)(2,1)} %collective-permute-done.refs_1_), channel_id=1, source_target_pairs={{0,12},{1,5},{4,0},{5,9},{8,4},{9,13},{12,8},{13,1},{2,14},{3,7},{... | collective-permute-start | bytes 2359304 | tf_op jit(solution)/shard_map/ppermute | solution.py:41
  61.4 31.5 %collective-permute-start.2 = (bf16[96,4096]{1,0:T(8,128)(2,1)}, bf16[96,4096]{1,0:T(8,128)(2,1)}, u32[]{:S(2)}, u32[]{:S(2)}) collective-permute-start(bf16[96,4096]{1,0:T(8,128)(2,1)} %get-tuple-element.53.refs_0_), channel_id=1, source_target_pairs={{0,12},{1,5},{4,0},{5,9},{8,4},{9,13},{12,8},{13,1},{2,14},{3,7},{... | collective-permute-start | bytes 2359304 | tf_op jit(solution)/shard_map/ppermute | solution.py:41
  62.7 30.2 %collective-permute-start.3 = (bf16[96,4096]{1,0:T(8,128)(2,1)}, bf16[96,4096]{1,0:T(8,128)(2,1)}, u32[]{:S(2)}, u32[]{:S(2)}) collective-permute-start(bf16[96,4096]{1,0:T(8,128)(2,1)} %collective-permute-done.refs_1_), channel_id=1, source_target_pairs={{0,4},{1,13},{4,8},{5,1},{8,12},{9,5},{12,0},{13,9},{2,6},{3,15},{... | collective-permute-start | bytes 2359304 | tf_op jit(solution)/shard_map/ppermute | solution.py:41
  64.1 35.3 %collective-permute-start.5 = (bf16[96,4096]{1,0:T(8,128)(2,1)}, bf16[96,4096]{1,0:T(8,128)(2,1)}, u32[]{:S(2)}, u32[]{:S(2)}) collective-permute-start(bf16[96,4096]{1,0:T(8,128)(2,1)} %collective-permute-done.1.refs_2_), channel_id=1, source_target_pairs={{0,4},{1,13},{4,8},{5,1},{8,12},{9,5},{12,0},{13,9},{2,6},{3,15},{... | collective-permute-start | bytes 2359304 | tf_op jit(solution)/shard_map/ppermute | solution.py:41
  76.0 30.2 %collective-permute-start.6 = (bf16[96,4096]{1,0:T(8,128)(2,1)}, bf16[96,4096]{1,0:T(8,128)(2,1)}, u32[]{:S(2)}, u32[]{:S(2)}) collective-permute-start(bf16[96,4096]{1,0:T(8,128)(2,1)} %collective-permute-done.4.refs_5_), channel_id=1, source_target_pairs={{0,12},{1,5},{4,0},{5,9},{8,4},{9,13},{12,8},{13,1},{2,14},{3,7},{... | collective-permute-start | bytes 2359304 | tf_op jit(solution)/shard_map/ppermute | solution.py:41
  109.0 13.9 %copy-start.8 = (bf16[1,8,96,512]{3,2,1,0:T(8,128)(2,1)S(1)}, bf16[1,8,96,512]{3,2,1,0:T(8,128)(2,1)}, u32[]{:S(2)}) copy-start(bf16[1,8,96,512]{3,2,1,0:T(8,128)(2,1)} %get-tuple-element.46) | copy-start | bytes 2359300
  138.2 6.6 %copy-start.2 = (bf16[8,528,256]{2,1,0:T(8,128)(2,1)S(1)}, bf16[8,528,256]{2,1,0:T(8,128)(2,1)}, u32[]{:S(2)}) copy-start(bf16[8,528,256]{2,1,0:T(8,128)(2,1)} %copy-done) | copy-start | bytes 6488068
  140.2 8.0 %collective-permute-start.10 = (bf16[4096,256]{1,0:T(8,128)(2,1)S(1)}, bf16[4096,256]{1,0:T(8,128)(2,1)S(1)}, u32[]{:S(2)}, u32[]{:S(2)}) collective-permute-start(bf16[4096,256]{1,0:T(8,128)(2,1)S(1)} %convolution_convert_fusion.2), channel_id=1, source_target_pairs={{0,1},{1,0},{2,3},{3,2},{4,5},{5,4},{6,7},{7,6},{8,9},{9,8},{10,11... | collective-permute-start | bytes 6291464 | tf_op jit(solution)/shard_map/ppermute | solution.py:28
  144.4 20.3 %collective-permute-start.11 = (bf16[96,4096]{1,0:T(8,128)(2,1)S(1)}, bf16[96,4096]{1,0:T(8,128)(2,1)S(1)}, u32[]{:S(2)}, u32[]{:S(2)}) collective-permute-start(bf16[96,4096]{1,0:T(8,128)(2,1)S(1)} %get-tuple-element.54.refs_0_), channel_id=1, source_target_pairs={{0,2},{2,0},{1,3},{3,1},{4,6},{6,4},{5,7},{7,5},{8,10},{10,8},{9,1... | collective-permute-start | bytes 2359304 | tf_op jit(solution)/shard_map/ppermute | solution.py:32
  145.0 3.2 %copy-start.5 = (bf16[8,512,256]{2,1,0:T(8,128)(2,1)}, bf16[8,512,256]{2,1,0:T(8,128)(2,1)S(1)}, u32[]{:S(2)}) copy-start(bf16[8,512,256]{2,1,0:T(8,128)(2,1)S(1)} %slice.140) | copy-start | bytes 6291460
  147.0 63.5 %copy-start.3 = (bf16[1,8,96,512]{3,2,1,0:T(8,128)(2,1)S(1)}, bf16[1,8,96,512]{3,2,1,0:T(8,128)(2,1)}, u32[]{:S(2)}) copy-start(bf16[1,8,96,512]{3,2,1,0:T(8,128)(2,1)} %get-tuple-element.47) | copy-start | bytes 2359300
  151.9 58.5 %collective-permute-start.18 = (bf16[8,512,256]{2,1,0:T(8,128)(2,1)S(1)}, bf16[8,512,256]{2,1,0:T(8,128)(2,1)S(1)}, u32[]{:S(2)}, u32[]{:S(2)}) collective-permute-start(bf16[8,512,256]{2,1,0:T(8,128)(2,1)S(1)} %bitcast.54), channel_id=1, source_target_pairs={{0,1},{1,0},{2,3},{3,2},{4,5},{5,4},{6,7},{7,6},{8,9},{9,8},{10,11... | collective-permute-start | bytes 6291464 | tf_op jit(solution)/shard_map/ppermute | solution.py:28
  152.3 15.3 %collective-permute-start.12 = (bf16[96,4096]{1,0:T(8,128)(2,1)S(1)}, bf16[96,4096]{1,0:T(8,128)(2,1)S(1)}, u32[]{:S(2)}, u32[]{:S(2)}) collective-permute-start(bf16[96,4096]{1,0:T(8,128)(2,1)S(1)} %get-tuple-element.54.refs_0_), channel_id=1, source_target_pairs={{0,4},{1,13},{4,8},{5,1},{8,12},{9,5},{12,0},{13,9},{2,6},{3,15},{... | collective-permute-start | bytes 2359304 | tf_op jit(solution)/shard_map/ppermute | solution.py:41
  164.7 16.8 %collective-permute-start.15 = (bf16[96,4096]{1,0:T(8,128)(2,1)S(1)}, bf16[96,4096]{1,0:T(8,128)(2,1)S(1)}, u32[]{:S(2)}, u32[]{:S(2)}) collective-permute-start(bf16[96,4096]{1,0:T(8,128)(2,1)S(1)} %collective-permute-done.11.refs_1_), channel_id=1, source_target_pairs={{0,12},{1,5},{4,0},{5,9},{8,4},{9,13},{12,8},{13,1},{2,14},{3,7},{... | collective-permute-start | bytes 2359304 | tf_op jit(solution)/shard_map/ppermute | solution.py:41
  165.0 16.6 %collective-permute-start.19 = (f32[512]{0:T(512)S(1)}, f32[512]{0:T(512)S(1)}, u32[]{:S(2)}, u32[]{:S(2)}) collective-permute-start(f32[512]{0:T(512)S(1)} %get-tuple-element.39), channel_id=1, source_target_pairs={{0,1},{1,0},{2,3},{3,2},{4,5},{5,4},{6,7},{7,6},{8,9},{9,8},{10,11... | collective-permute-start | bytes 6152 | tf_op jit(solution)/shard_map/ppermute | solution.py:28
  167.0 31.4 %collective-permute-start.13 = (bf16[96,4096]{1,0:T(8,128)(2,1)S(1)}, bf16[96,4096]{1,0:T(8,128)(2,1)S(1)}, u32[]{:S(2)}, u32[]{:S(2)}) collective-permute-start(bf16[96,4096]{1,0:T(8,128)(2,1)S(1)} %get-tuple-element.54.refs_0_), channel_id=1, source_target_pairs={{0,12},{1,5},{4,0},{5,9},{8,4},{9,13},{12,8},{13,1},{2,14},{3,7},{... | collective-permute-start | bytes 2359304 | tf_op jit(solution)/shard_map/ppermute | solution.py:41
  167.6 30.8 %collective-permute-start.14 = (bf16[96,4096]{1,0:T(8,128)(2,1)S(1)}, bf16[96,4096]{1,0:T(8,128)(2,1)S(1)}, u32[]{:S(2)}, u32[]{:S(2)}) collective-permute-start(bf16[96,4096]{1,0:T(8,128)(2,1)S(1)} %collective-permute-done.11.refs_1_), channel_id=1, source_target_pairs={{0,4},{1,13},{4,8},{5,1},{8,12},{9,5},{12,0},{13,9},{2,6},{3,15},{... | collective-permute-start | bytes 2359304 | tf_op jit(solution)/shard_map/ppermute | solution.py:41
  181.5 22.5 %collective-permute-start.16 = (bf16[96,4096]{1,0:T(8,128)(2,1)S(1)}, bf16[96,4096]{1,0:T(8,128)(2,1)S(1)}, u32[]{:S(2)}, u32[]{:S(2)}) collective-permute-start(bf16[96,4096]{1,0:T(8,128)(2,1)S(1)} %collective-permute-done.12.refs_2_), channel_id=1, source_target_pairs={{0,4},{1,13},{4,8},{5,1},{8,12},{9,5},{12,0},{13,9},{2,6},{3,15},{... | collective-permute-start | bytes 2359304 | tf_op jit(solution)/shard_map/ppermute | solution.py:41
  181.5 28.9 %collective-permute-start.17 = (bf16[96,4096]{1,0:T(8,128)(2,1)S(1)}, bf16[96,4096]{1,0:T(8,128)(2,1)S(1)}, u32[]{:S(2)}, u32[]{:S(2)}) collective-permute-start(bf16[96,4096]{1,0:T(8,128)(2,1)S(1)} %collective-permute-done.15.refs_5_), channel_id=1, source_target_pairs={{0,12},{1,5},{4,0},{5,9},{8,4},{9,13},{12,8},{13,1},{2,14},{3,7},{... | collective-permute-start | bytes 2359304 | tf_op jit(solution)/shard_map/ppermute | solution.py:41
  210.5 10.9 %copy-start.7 = (bf16[1,8,96,512]{3,2,1,0:T(8,128)(2,1)S(1)}, bf16[1,8,96,512]{3,2,1,0:T(8,128)(2,1)}, u32[]{:S(2)}) copy-start(bf16[1,8,96,512]{3,2,1,0:T(8,128)(2,1)} %get-tuple-element.45) | copy-start | bytes 2359300
  231.2 3.1 %copy-start.17 = (bf16[768,4096]{1,0:T(8,128)(2,1)S(1)}, bf16[768,4096]{1,0:T(8,128)(2,1)}, u32[]{:S(2)}) copy-start(bf16[768,4096]{1,0:T(8,128)(2,1)} %get-tuple-element.16) | copy-start | bytes 18874372
  232.2 5.3 %copy-start.12 = (bf16[768,512]{1,0:T(8,128)(2,1)}, bf16[768,512]{1,0:T(8,128)(2,1)S(1)}, u32[]{:S(2)}) copy-start(bf16[768,512]{1,0:T(8,128)(2,1)S(1)} %get-tuple-element.37) | copy-start | bytes 2359300
  237.6 10.2 %collective-permute-start.20 = (bf16[4096,256]{1,0:T(8,128)(2,1)}, bf16[4096,256]{1,0:T(8,128)(2,1)}, u32[]{:S(2)}, u32[]{:S(2)}) collective-permute-start(bf16[4096,256]{1,0:T(8,128)(2,1)} %convolution_convert_fusion), channel_id=1, source_target_pairs={{0,1},{1,0},{2,3},{3,2},{4,5},{5,4},{6,7},{7,6},{8,9},{9,8},{10,11... | collective-permute-start | bytes 6291464 | tf_op jit(solution)/shard_map/ppermute | solution.py:28
  241.3 6.5 %copy-start.6 = (bf16[8,512,256]{2,1,0:T(8,128)(2,1)S(1)}, bf16[8,512,256]{2,1,0:T(8,128)(2,1)}, u32[]{:S(2)}) copy-start(bf16[8,512,256]{2,1,0:T(8,128)(2,1)} %copy-done.5) | copy-start | bytes 6291460
  241.3 6.3 %collective-permute-start.21 = (f32[512]{0:T(512)S(1)}, f32[512]{0:T(512)S(1)}, u32[]{:S(2)}, u32[]{:S(2)}) collective-permute-start(f32[512]{0:T(512)S(1)} %get-tuple-element.38), channel_id=1, source_target_pairs={{0,1},{1,0},{2,3},{3,2},{4,5},{5,4},{6,7},{7,6},{8,9},{9,8},{10,11... | collective-permute-start | bytes 6152 | tf_op jit(solution)/shard_map/ppermute | solution.py:28
  (8 other events, 13.7 us)

commit v5 on v4

--- a/solution.py
+++ b/solution.py
@@ -101,22 +101,30 @@
         pltpu.make_async_copy(made.at[at], residual_out.at[to], sent.at[i])
         for i, (at, to) in enumerate(zip(own, places))
     ]
-    for copy in (loads[0], *takes, *flows, loads[1]):
+    for copy in (loads[0], *takes[:4], *flows[:4], loads[1], *takes[4:], *flows[4:]):
         copy.start()
-    for take, give in zip(takes, gives):
-        take.wait()
-        give.start()
-    for load in flows:
-        load.wait()
-    for half in range(2):
-        loads[half].wait()
-        projected = jnp.dot(
-            rows[...], weights[half].reshape(D, wide), preferred_element_type=jnp.float32
-        )
-        columns = slice(half * wide, (half + 1) * wide)
-        made[:, columns] = held[:, columns].astype(jnp.float32) + projected * D ** (-0.5)
-    for send in sends:
-        send.start()
+    for group in range(2):
+        members = range(group * 4, group * 4 + 4)
+        these = pl.ds(group * 4 * BLOCK, 4 * BLOCK)
+        for i in members:
+            takes[i].wait()
+            gives[i].start()
+        for i in members:
+            flows[i].wait()
+        for half in range(2):
+            if group == 0:
+                loads[half].wait()
+            projected = jnp.dot(
+                rows[these, :],
+                weights[half].reshape(D, wide),
+                preferred_element_type=jnp.float32,
+            )
+            columns = slice(half * wide, (half + 1) * wide)
+            made[these, columns] = (
+                held[these, columns].astype(jnp.float32) + projected * D ** (-0.5)
+            )
+        for i in members:
+            sends[i].start()
     for copy in (*gives, *sends):
         copy.wait()
 

time: 287 us -> 282 us (0.983)
  Pallas kernels: 24.8 us -> 20.1 us
    pallas_call x2, Pallas kernels: 24.8 us -> 20.1 us  [forward(): pl.pallas_call(kernel, out_shape=(jax.ShapeDtypeStruct((tokens, features)...]
where the time goes in v5:
time: 282 us
  waiting for transfers between devices  102 us (36%)
  blocking collectives  84.1 us (30%)
  starting transfers between devices  29 us (10%)
  Pallas kernels  20.1 us (7%)
  other arithmetic  19.4 us (7%)
  matrix products  13.4 us (5%)
  local copies, waits for them, and re-layouts  12.2 us (4%)
    ppermute x12, waiting for transfers between devices, y_hop(): return lax.ppermute(value, ('y', 'c'), pairs)  76.6 us
    all_to_all x3, blocking collectives, copy_for_each(): return lax.all_to_all(copies, axis, split_axis=0, concat_axis=0, tiled=True)  54.5 us
    all_to_all x1, blocking collectives, per_device(): lax.all_to_all(sent, ISLAND, split_axis=0, concat_axis=0, tiled=True)  29.6 us
    ppermute x2, waiting for transfers between devices, x_swap(): return lax.ppermute(value, 'xh', [(0, 1), (1, 0)])  24.7 us
    pallas_call x2, Pallas kernels, forward(): pl.pallas_call(kernel, out_shape=(jax.ShapeDtypeStruct((tokens, features)...  20.1 us
    dot_general x4, matrix products, over_tokens(): jnp.einsum('td,tf->df', rows, residual_grad[:, columns], preferred_elemen...  13.4 us
    ppermute x12, starting transfers between devices, y_hop(): return lax.ppermute(value, ('y', 'c'), pairs)  13.2 us
    ppermute x8, starting transfers between devices, core_swap(): return lax.ppermute(value, 'c', [(0, 1), (1, 0)])  12.8 us
  transfers between devices with their start and end apart: 22, of which 11 were waited for; matrix products, arithmetic and copies ran while one was open for 7% of the time, Pallas kernels for 0%

profile of v5, /device:TPU:1, one launch (start us, length us, event | category | flops | bytes accessed | tf_op | source)
XLA Modules:
  0.0 281.6 jit_solution(6156952421683649467)
XLA Ops:
  2.5 33.4 %all_to_all.20.refs_8_ = bf16[8,528,256]{2,1,0:T(8,128)(2,1)S(1)} all-to-all(bf16[8,528,256]{2,1,0:T(8,128)(2,1)S(1)} %broadcast_in_dim.9), channel_id=1, replica_groups=mesh['xl'=2,'z'=4,'y'=4,'xh'=2,'c'=2] {'xl','z'}, dimensions={0} | all-to-all | bytes 4325376 | tf_op jit(solution)/shard_map/all_to_all | solution.py:46
  36.0 2.3 collective-permute-start.7
  39.3 2.5 collective-permute-start
  41.8 2.7 collective-permute-start.1
  46.9 13.2 %collective-permute-done.refs_1_ = bf16[96,4096]{1,0:T(8,128)(2,1)} collective-permute-done((bf16[96,4096]{1,0:T(8,128)(2,1)}, bf16[96,4096]{1,0:T(8,128)(2,1)}, u32[]{:S(2)}, u32[]{:S(2)}) %collective-permute-start) | collective-permute-done | bytes 786464 | tf_op jit(solution)/shard_map/ppermute | solution.py:32
  64.4 11.7 %collective-permute-done.4.refs_5_ = bf16[96,4096]{1,0:T(8,128)(2,1)} collective-permute-done((bf16[96,4096]{1,0:T(8,128)(2,1)}, bf16[96,4096]{1,0:T(8,128)(2,1)}, u32[]{:S(2)}, u32[]{:S(2)}) %collective-permute-start.4) | collective-permute-done | bytes 786464 | tf_op jit(solution)/shard_map/ppermute | solution.py:41
  80.5 12.3 %collective-permute-done.2.refs_3_ = bf16[96,4096]{1,0:T(8,128)(2,1)} collective-permute-done((bf16[96,4096]{1,0:T(8,128)(2,1)}, bf16[96,4096]{1,0:T(8,128)(2,1)}, u32[]{:S(2)}, u32[]{:S(2)}) %collective-permute-start.2) | collective-permute-done | bytes 786464 | tf_op jit(solution)/shard_map/ppermute | solution.py:41
  92.9 6.5 %collective-permute-done.5.refs_6_ = bf16[96,4096]{1,0:T(8,128)(2,1)} collective-permute-done((bf16[96,4096]{1,0:T(8,128)(2,1)}, bf16[96,4096]{1,0:T(8,128)(2,1)}, u32[]{:S(2)}, u32[]{:S(2)}) %collective-permute-start.5) | collective-permute-done | bytes 786464 | tf_op jit(solution)/shard_map/ppermute | solution.py:41
  99.4 6.8 %collective-permute-done.6.refs_7_ = bf16[96,4096]{1,0:T(8,128)(2,1)} collective-permute-done((bf16[96,4096]{1,0:T(8,128)(2,1)}, bf16[96,4096]{1,0:T(8,128)(2,1)}, u32[]{:S(2)}, u32[]{:S(2)}) %collective-permute-start.6) | collective-permute-done | bytes 786464 | tf_op jit(solution)/shard_map/ppermute | solution.py:41
  106.2 1.6 copy-done.1
  109.0 10.7 %forward.2 = (f32[768,512]{1,0:T(8,128)S(1)}, bf16[768,4096]{1,0:T(8,128)(2,1)}) custom-call(bf16[96,4096]{1,0:T(8,128)(2,1)} %get-tuple-element.53.refs_0_, bf16[96,4096]{1,0:T(8,128)(2,1)} %collective-permute-done.refs_1_, bf16[96,4096]{1,0:T(8,128)(2,1)} %collective-permute-done.1.refs_2_, bf16[96,4096]{1,0:T(8,128)(2,1)} %collective-permute-done.2.refs_3_, ...), custom_call_target="tpu_custom_call" | custom-call | flops 3221225472 | bytes 16777216 | tf_op jit(solution)/shard_map/forward/pallas_call | solution.py:141
  120.2 11.9 %all_to_all.21 = f32[8,1,2304]{2,1,0:T(1,128)S(1)} all-to-all(f32[8,1,2304]{2,1,0:T(1,128)S(1)} %broadcast_in_dim.10), channel_id=1, replica_groups=mesh['xl'=2,'z'=4,'y'=4,'xh'=2,'c'=2] {'y','xh'}, dimensions={0} | all-to-all | bytes 147456 | tf_op jit(solution)/shard_map/all_to_all | solution.py:46
  133.3 1.8 copy-done.16
  135.0 2.0 convolution_convert_fusion.2
  137.0 4.2 %collective-permute-start.10 = (bf16[4096,256]{1,0:T(8,128)(2,1)S(1)}, bf16[4096,256]{1,0:T(8,128)(2,1)S(1)}, u32[]{:S(2)}, u32[]{:S(2)}) collective-permute-start(bf16[4096,256]{1,0:T(8,128)(2,1)S(1)} %convolution_convert_fusion.2), channel_id=1, source_target_pairs={{0,1},{1,0},{2,3},{3,2},{4,5},{5,4},{6,7},{7,6},{8,9},{9,8},{10,11... | collective-permute-start | bytes 6291464 | tf_op jit(solution)/shard_map/ppermute | solution.py:28
  141.8 2.0 convolution_convert_fusion.3
  145.0 3.8 %fusion.49 = (bf16[4096,256]{1,0:T(8,128)(2,1)S(1)}, bf16[4096,256]{1,0:T(8,128)(2,1)}, bf16[4096,256]{1,0:T(8,128)(2,1)}) fusion(bf16[4096,256]{1,0:T(8,128)(2,1)S(1)} %collective-permute-done.10, bf16[4096,256]{1,0:T(8,128)(2,1)S(1)} %convolution_convert_fusion.3, bf16[8,512,256]{2,1,0:T(8,128)(2,1)S(1)} %slice.140), kind=kLoop, calls=%fused_computation.122 | loop fusion | flops 16777216 | bytes 12582912 | tf_op jit(solution)/shard_map/convert_element_type | solution.py:260
  150.0 11.5 %collective-permute-done.11.refs_1_ = bf16[96,4096]{1,0:T(8,128)(2,1)S(1)} collective-permute-done((bf16[96,4096]{1,0:T(8,128)(2,1)S(1)}, bf16[96,4096]{1,0:T(8,128)(2,1)S(1)}, u32[]{:S(2)}, u32[]{:S(2)}) %collective-permute-start.11) | collective-permute-done | bytes 786464 | tf_op jit(solution)/shard_map/ppermute | solution.py:32
  161.8 2.0 collective-permute-start.19
  164.4 2.1 collective-permute-start.14
  166.5 11.9 %collective-permute-done.15.refs_5_ = bf16[96,4096]{1,0:T(8,128)(2,1)S(1)} collective-permute-done((bf16[96,4096]{1,0:T(8,128)(2,1)S(1)}, bf16[96,4096]{1,0:T(8,128)(2,1)S(1)}, u32[]{:S(2)}, u32[]{:S(2)}) %collective-permute-start.15) | collective-permute-done | bytes 786464 | tf_op jit(solution)/shard_map/ppermute | solution.py:41
  179.8 15.4 %collective-permute-done.13.refs_3_ = bf16[96,4096]{1,0:T(8,128)(2,1)S(1)} collective-permute-done((bf16[96,4096]{1,0:T(8,128)(2,1)S(1)}, bf16[96,4096]{1,0:T(8,128)(2,1)S(1)}, u32[]{:S(2)}, u32[]{:S(2)}) %collective-permute-start.13) | collective-permute-done | bytes 786464 | tf_op jit(solution)/shard_map/ppermute | solution.py:41
  195.2 5.6 %collective-permute-done.16.refs_6_ = bf16[96,4096]{1,0:T(8,128)(2,1)S(1)} collective-permute-done((bf16[96,4096]{1,0:T(8,128)(2,1)S(1)}, bf16[96,4096]{1,0:T(8,128)(2,1)S(1)}, u32[]{:S(2)}, u32[]{:S(2)}) %collective-permute-start.16) | collective-permute-done | bytes 786464 | tf_op jit(solution)/shard_map/ppermute | solution.py:41
  200.8 6.5 %collective-permute-done.17.refs_7_ = bf16[96,4096]{1,0:T(8,128)(2,1)S(1)} collective-permute-done((bf16[96,4096]{1,0:T(8,128)(2,1)S(1)}, bf16[96,4096]{1,0:T(8,128)(2,1)S(1)}, u32[]{:S(2)}, u32[]{:S(2)}) %collective-permute-start.17) | collective-permute-done | bytes 786464 | tf_op jit(solution)/shard_map/ppermute | solution.py:41
  207.3 9.5 %forward.3 = (f32[768,512]{1,0:T(8,128)S(1)}, bf16[768,4096]{1,0:T(8,128)(2,1)}) custom-call(bf16[96,4096]{1,0:T(8,128)(2,1)S(1)} %get-tuple-element.54.refs_0_, bf16[96,4096]{1,0:T(8,128)(2,1)S(1)} %collective-permute-done.11.refs_1_, bf16[96,4096]{1,0:T(8,128)(2,1)S(1)} %collective-permute-done.12.refs_2_, ...), custom_call_target="tpu_custom_call" | custom-call | flops 3221225472 | bytes 16777216 | tf_op jit(solution)/shard_map/forward/pallas_call | solution.py:141
  217.3 9.1 %all_to_all.22 = f32[8,1,2304]{2,1,0:T(1,128)S(1)} all-to-all(f32[8,1,2304]{2,1,0:T(1,128)S(1)} %broadcast_in_dim.11), channel_id=1, replica_groups=mesh['xl'=2,'z'=4,'y'=4,'xh'=2,'c'=2] {'y','xh'}, dimensions={0} | all-to-all | bytes 147456 | tf_op jit(solution)/shard_map/all_to_all | solution.py:46
  227.6 2.0 copy-done.17
  229.6 3.3 %convolution_convert_fusion = bf16[4096,256]{1,0:T(8,128)(2,1)} fusion(bf16[768,4096]{1,0:T(8,128)(2,1)S(1)} %copy-done.17, bf16[768,512]{1,0:T(8,128)(2,1)S(1)} %get-tuple-element.37), kind=kOutput, calls=%fused_computation.7 | convolution fusion | flops 1611661312 | bytes 8781824 | tf_op jit(solution)/shard_map/td,tf->df/dot_general | solution.py:246
  232.9 3.5 %collective-permute-start.20 = (bf16[4096,256]{1,0:T(8,128)(2,1)}, bf16[4096,256]{1,0:T(8,128)(2,1)}, u32[]{:S(2)}, u32[]{:S(2)}) collective-permute-start(bf16[4096,256]{1,0:T(8,128)(2,1)} %convolution_convert_fusion), channel_id=1, source_target_pairs={{0,1},{1,0},{2,3},{3,2},{4,5},{5,4},{6,7},{7,6},{8,9},{9,8},{10,11... | collective-permute-start | bytes 6291464 | tf_op jit(solution)/shard_map/ppermute | solution.py:28
  236.7 6.2 %convolution_convert_fusion.1 = bf16[4096,256]{1,0:T(8,128)(2,1)} fusion(bf16[768,4096]{1,0:T(8,128)(2,1)} %get-tuple-element.16, bf16[768,512]{1,0:T(8,128)(2,1)} %copy-done.12), kind=kOutput, calls=%fused_computation.8 | convolution fusion | flops 1611661312 | bytes 8781824 | tf_op jit(solution)/shard_map/td,tf->df/dot_general | solution.py:246
  243.1 5.9 %fusion.1 = bf16[4096,256]{1,0:T(8,128)(2,1)S(1)} fusion(bf16[4096,256]{1,0:T(8,128)(2,1)} %get-tuple-element.13, bf16[4096,256]{1,0:T(8,128)(2,1)} %get-tuple-element.14, bf16[4096,256]{1,0:T(8,128)(2,1)} %collective-permute-done.20, bf16[4096,256]{1,0:T(8,128)(2,1)} %convolution_convert_fusion.1, bf16[8,512,256]{2,1,0:T(8,128)(2,1)S(1)} %copy-done.6), kind=kLoop, calls=%fused_computation.14 | loop fusion | flops 26214400 | bytes 12582912 | tf_op jit(solution)/shard_map/convert_element_type | solution.py:277
  249.2 29.6 %all_to_all.23 = bf16[8,528,256]{2,1,0:T(8,128)(2,1)S(1)} all-to-all(bf16[8,528,256]{2,1,0:T(8,128)(2,1)S(1)} %fusion.13), channel_id=1, replica_groups=mesh['xl'=2,'z'=4,'y'=4,'xh'=2,'c'=2] {'xl','z'}, dimensions={0} | all-to-all | bytes 4325376 | tf_op jit(solution)/shard_map/all_to_all | solution.py:280
  (112 shorter events, 27.5 us)
Async XLA Ops:
  2.5 35.7 %copy-start.10 = (bf16[1,2,96,4096]{3,2,1,0:T(8,128)(2,1)S(1)}, bf16[1,2,96,4096]{3,2,1,0:T(8,128)(2,1)}, u32[]{:S(2)}) copy-start(bf16[1,2,96,4096]{3,2,1,0:T(8,128)(2,1)} %param.11) | copy-start | bytes 4718596
  36.0 43.6 %copy-start = (bf16[8,528,256]{2,1,0:T(8,128)(2,1)}, bf16[8,528,256]{2,1,0:T(8,128)(2,1)S(1)}, u32[]{:S(2)}) copy-start(bf16[8,528,256]{2,1,0:T(8,128)(2,1)S(1)} %all_to_all.20.refs_8_) | copy-start | bytes 6488068
  36.0 43.7 %collective-permute-start.7 = (bf16[8,528,256]{2,1,0:T(8,128)(2,1)S(1)}, bf16[8,528,256]{2,1,0:T(8,128)(2,1)}, u32[]{:S(2)}, u32[]{:S(2)}) collective-permute-start(bf16[8,528,256]{2,1,0:T(8,128)(2,1)S(1)} %all_to_all.20.refs_8_), channel_id=1, source_target_pairs={{0,1},{1,0},{2,3},{3,2},{4,5},{5,4},{6,7},{7,6},{8,9},{9,8},{10,11... | collective-permute-start | bytes 6488072 | tf_op jit(solution)/shard_map/ppermute | solution.py:28
  39.3 20.7 %collective-permute-start = (bf16[96,4096]{1,0:T(8,128)(2,1)}, bf16[96,4096]{1,0:T(8,128)(2,1)}, u32[]{:S(2)}, u32[]{:S(2)}) collective-permute-start(bf16[96,4096]{1,0:T(8,128)(2,1)} %get-tuple-element.53.refs_0_), channel_id=1, source_target_pairs={{0,2},{2,0},{1,3},{3,1},{4,6},{6,4},{5,7},{7,5},{8,10},{10,8},{9,1... | collective-permute-start | bytes 2359304 | tf_op jit(solution)/shard_map/ppermute | solution.py:32
  41.8 20.9 %collective-permute-start.1 = (bf16[96,4096]{1,0:T(8,128)(2,1)}, bf16[96,4096]{1,0:T(8,128)(2,1)}, u32[]{:S(2)}, u32[]{:S(2)}) collective-permute-start(bf16[96,4096]{1,0:T(8,128)(2,1)} %get-tuple-element.53.refs_0_), channel_id=1, source_target_pairs={{0,4},{1,13},{4,8},{5,1},{8,12},{9,5},{12,0},{13,9},{2,6},{3,15},{... | collective-permute-start | bytes 2359304 | tf_op jit(solution)/shard_map/ppermute | solution.py:41
  46.1 15.2 %collective-permute-start.8 = (bf16[2,8,96,256]{3,2,1,0:T(8,128)(2,1)S(1)}, bf16[2,8,96,256]{3,2,1,0:T(8,128)(2,1)S(1)}, u32[]{:S(2)}, u32[]{:S(2)}) collective-permute-start(bf16[2,8,96,256]{3,2,1,0:T(8,128)(2,1)S(1)} %get-tuple-element.51), channel_id=1, source_target_pairs={{0,1},{1,0},{2,3},{3,2},{4,5},{5,4},{6,7},{7,6},{8,9},{9,8},{10,11... | collective-permute-start | bytes 2359304 | tf_op jit(solution)/shard_map/ppermute | solution.py:28
  46.5 17.5 %collective-permute-start.9 = (bf16[2,8,96,256]{3,2,1,0:T(8,128)(2,1)S(1)}, bf16[2,8,96,256]{3,2,1,0:T(8,128)(2,1)S(1)}, u32[]{:S(2)}, u32[]{:S(2)}) collective-permute-start(bf16[2,8,96,256]{3,2,1,0:T(8,128)(2,1)S(1)} %get-tuple-element.49), channel_id=1, source_target_pairs={{0,1},{1,0},{2,3},{3,2},{4,5},{5,4},{6,7},{7,6},{8,9},{9,8},{10,11... | collective-permute-start | bytes 2359304 | tf_op jit(solution)/shard_map/ppermute | solution.py:28
  60.1 15.9 %collective-permute-start.4 = (bf16[96,4096]{1,0:T(8,128)(2,1)}, bf16[96,4096]{1,0:T(8,128)(2,1)}, u32[]{:S(2)}, u32[]{:S(2)}) collective-permute-start(bf16[96,4096]{1,0:T(8,128)(2,1)} %collective-permute-done.refs_1_), channel_id=1, source_target_pairs={{0,12},{1,5},{4,0},{5,9},{8,4},{9,13},{12,8},{13,1},{2,14},{3,7},{... | collective-permute-start | bytes 2359304 | tf_op jit(solution)/shard_map/ppermute | solution.py:41
  61.4 31.5 %collective-permute-start.2 = (bf16[96,4096]{1,0:T(8,128)(2,1)}, bf16[96,4096]{1,0:T(8,128)(2,1)}, u32[]{:S(2)}, u32[]{:S(2)}) collective-permute-start(bf16[96,4096]{1,0:T(8,128)(2,1)} %get-tuple-element.53.refs_0_), channel_id=1, source_target_pairs={{0,12},{1,5},{4,0},{5,9},{8,4},{9,13},{12,8},{13,1},{2,14},{3,7},{... | collective-permute-start | bytes 2359304 | tf_op jit(solution)/shard_map/ppermute | solution.py:41
  62.7 30.2 %collective-permute-start.3 = (bf16[96,4096]{1,0:T(8,128)(2,1)}, bf16[96,4096]{1,0:T(8,128)(2,1)}, u32[]{:S(2)}, u32[]{:S(2)}) collective-permute-start(bf16[96,4096]{1,0:T(8,128)(2,1)} %collective-permute-done.refs_1_), channel_id=1, source_target_pairs={{0,4},{1,13},{4,8},{5,1},{8,12},{9,5},{12,0},{13,9},{2,6},{3,15},{... | collective-permute-start | bytes 2359304 | tf_op jit(solution)/shard_map/ppermute | solution.py:41
  64.1 35.3 %collective-permute-start.5 = (bf16[96,4096]{1,0:T(8,128)(2,1)}, bf16[96,4096]{1,0:T(8,128)(2,1)}, u32[]{:S(2)}, u32[]{:S(2)}) collective-permute-start(bf16[96,4096]{1,0:T(8,128)(2,1)} %collective-permute-done.1.refs_2_), channel_id=1, source_target_pairs={{0,4},{1,13},{4,8},{5,1},{8,12},{9,5},{12,0},{13,9},{2,6},{3,15},{... | collective-permute-start | bytes 2359304 | tf_op jit(solution)/shard_map/ppermute | solution.py:41
  76.0 30.2 %collective-permute-start.6 = (bf16[96,4096]{1,0:T(8,128)(2,1)}, bf16[96,4096]{1,0:T(8,128)(2,1)}, u32[]{:S(2)}, u32[]{:S(2)}) collective-permute-start(bf16[96,4096]{1,0:T(8,128)(2,1)} %collective-permute-done.4.refs_5_), channel_id=1, source_target_pairs={{0,12},{1,5},{4,0},{5,9},{8,4},{9,13},{12,8},{13,1},{2,14},{3,7},{... | collective-permute-start | bytes 2359304 | tf_op jit(solution)/shard_map/ppermute | solution.py:41
  109.0 10.7 %copy-start.8 = (bf16[1,8,96,512]{3,2,1,0:T(8,128)(2,1)S(1)}, bf16[1,8,96,512]{3,2,1,0:T(8,128)(2,1)}, u32[]{:S(2)}) copy-start(bf16[1,8,96,512]{3,2,1,0:T(8,128)(2,1)} %get-tuple-element.46) | copy-start | bytes 2359300
  135.0 6.6 %copy-start.2 = (bf16[8,528,256]{2,1,0:T(8,128)(2,1)S(1)}, bf16[8,528,256]{2,1,0:T(8,128)(2,1)}, u32[]{:S(2)}) copy-start(bf16[8,528,256]{2,1,0:T(8,128)(2,1)} %copy-done) | copy-start | bytes 6488068
  137.0 8.0 %collective-permute-start.10 = (bf16[4096,256]{1,0:T(8,128)(2,1)S(1)}, bf16[4096,256]{1,0:T(8,128)(2,1)S(1)}, u32[]{:S(2)}, u32[]{:S(2)}) collective-permute-start(bf16[4096,256]{1,0:T(8,128)(2,1)S(1)} %convolution_convert_fusion.2), channel_id=1, source_target_pairs={{0,1},{1,0},{2,3},{3,2},{4,5},{5,4},{6,7},{7,6},{8,9},{9,8},{10,11... | collective-permute-start | bytes 6291464 | tf_op jit(solution)/shard_map/ppermute | solution.py:28
  141.2 20.3 %collective-permute-start.11 = (bf16[96,4096]{1,0:T(8,128)(2,1)S(1)}, bf16[96,4096]{1,0:T(8,128)(2,1)S(1)}, u32[]{:S(2)}, u32[]{:S(2)}) collective-permute-start(bf16[96,4096]{1,0:T(8,128)(2,1)S(1)} %get-tuple-element.54.refs_0_), channel_id=1, source_target_pairs={{0,2},{2,0},{1,3},{3,1},{4,6},{6,4},{5,7},{7,5},{8,10},{10,8},{9,1... | collective-permute-start | bytes 2359304 | tf_op jit(solution)/shard_map/ppermute | solution.py:32
  141.8 3.2 %copy-start.5 = (bf16[8,512,256]{2,1,0:T(8,128)(2,1)}, bf16[8,512,256]{2,1,0:T(8,128)(2,1)S(1)}, u32[]{:S(2)}) copy-start(bf16[8,512,256]{2,1,0:T(8,128)(2,1)S(1)} %slice.140) | copy-start | bytes 6291460
  143.8 63.5 %copy-start.3 = (bf16[1,8,96,512]{3,2,1,0:T(8,128)(2,1)S(1)}, bf16[1,8,96,512]{3,2,1,0:T(8,128)(2,1)}, u32[]{:S(2)}) copy-start(bf16[1,8,96,512]{3,2,1,0:T(8,128)(2,1)} %get-tuple-element.47) | copy-start | bytes 2359300
  148.7 58.5 %collective-permute-start.18 = (bf16[8,512,256]{2,1,0:T(8,128)(2,1)S(1)}, bf16[8,512,256]{2,1,0:T(8,128)(2,1)S(1)}, u32[]{:S(2)}, u32[]{:S(2)}) collective-permute-start(bf16[8,512,256]{2,1,0:T(8,128)(2,1)S(1)} %bitcast.54), channel_id=1, source_target_pairs={{0,1},{1,0},{2,3},{3,2},{4,5},{5,4},{6,7},{7,6},{8,9},{9,8},{10,11... | collective-permute-start | bytes 6291464 | tf_op jit(solution)/shard_map/ppermute | solution.py:28
  149.1 15.3 %collective-permute-start.12 = (bf16[96,4096]{1,0:T(8,128)(2,1)S(1)}, bf16[96,4096]{1,0:T(8,128)(2,1)S(1)}, u32[]{:S(2)}, u32[]{:S(2)}) collective-permute-start(bf16[96,4096]{1,0:T(8,128)(2,1)S(1)} %get-tuple-element.54.refs_0_), channel_id=1, source_target_pairs={{0,4},{1,13},{4,8},{5,1},{8,12},{9,5},{12,0},{13,9},{2,6},{3,15},{... | collective-permute-start | bytes 2359304 | tf_op jit(solution)/shard_map/ppermute | solution.py:41
  161.5 16.8 %collective-permute-start.15 = (bf16[96,4096]{1,0:T(8,128)(2,1)S(1)}, bf16[96,4096]{1,0:T(8,128)(2,1)S(1)}, u32[]{:S(2)}, u32[]{:S(2)}) collective-permute-start(bf16[96,4096]{1,0:T(8,128)(2,1)S(1)} %collective-permute-done.11.refs_1_), channel_id=1, source_target_pairs={{0,12},{1,5},{4,0},{5,9},{8,4},{9,13},{12,8},{13,1},{2,14},{3,7},{... | collective-permute-start | bytes 2359304 | tf_op jit(solution)/shard_map/ppermute | solution.py:41
  161.8 16.6 %collective-permute-start.19 = (f32[512]{0:T(512)S(1)}, f32[512]{0:T(512)S(1)}, u32[]{:S(2)}, u32[]{:S(2)}) collective-permute-start(f32[512]{0:T(512)S(1)} %get-tuple-element.39), channel_id=1, source_target_pairs={{0,1},{1,0},{2,3},{3,2},{4,5},{5,4},{6,7},{7,6},{8,9},{9,8},{10,11... | collective-permute-start | bytes 6152 | tf_op jit(solution)/shard_map/ppermute | solution.py:28
  163.8 31.4 %collective-permute-start.13 = (bf16[96,4096]{1,0:T(8,128)(2,1)S(1)}, bf16[96,4096]{1,0:T(8,128)(2,1)S(1)}, u32[]{:S(2)}, u32[]{:S(2)}) collective-permute-start(bf16[96,4096]{1,0:T(8,128)(2,1)S(1)} %get-tuple-element.54.refs_0_), channel_id=1, source_target_pairs={{0,12},{1,5},{4,0},{5,9},{8,4},{9,13},{12,8},{13,1},{2,14},{3,7},{... | collective-permute-start | bytes 2359304 | tf_op jit(solution)/shard_map/ppermute | solution.py:41
  164.4 30.8 %collective-permute-start.14 = (bf16[96,4096]{1,0:T(8,128)(2,1)S(1)}, bf16[96,4096]{1,0:T(8,128)(2,1)S(1)}, u32[]{:S(2)}, u32[]{:S(2)}) collective-permute-start(bf16[96,4096]{1,0:T(8,128)(2,1)S(1)} %collective-permute-done.11.refs_1_), channel_id=1, source_target_pairs={{0,4},{1,13},{4,8},{5,1},{8,12},{9,5},{12,0},{13,9},{2,6},{3,15},{... | collective-permute-start | bytes 2359304 | tf_op jit(solution)/shard_map/ppermute | solution.py:41
  178.3 22.5 %collective-permute-start.16 = (bf16[96,4096]{1,0:T(8,128)(2,1)S(1)}, bf16[96,4096]{1,0:T(8,128)(2,1)S(1)}, u32[]{:S(2)}, u32[]{:S(2)}) collective-permute-start(bf16[96,4096]{1,0:T(8,128)(2,1)S(1)} %collective-permute-done.12.refs_2_), channel_id=1, source_target_pairs={{0,4},{1,13},{4,8},{5,1},{8,12},{9,5},{12,0},{13,9},{2,6},{3,15},{... | collective-permute-start | bytes 2359304 | tf_op jit(solution)/shard_map/ppermute | solution.py:41
  178.3 28.9 %collective-permute-start.17 = (bf16[96,4096]{1,0:T(8,128)(2,1)S(1)}, bf16[96,4096]{1,0:T(8,128)(2,1)S(1)}, u32[]{:S(2)}, u32[]{:S(2)}) collective-permute-start(bf16[96,4096]{1,0:T(8,128)(2,1)S(1)} %collective-permute-done.15.refs_5_), channel_id=1, source_target_pairs={{0,12},{1,5},{4,0},{5,9},{8,4},{9,13},{12,8},{13,1},{2,14},{3,7},{... | collective-permute-start | bytes 2359304 | tf_op jit(solution)/shard_map/ppermute | solution.py:41
  207.3 9.5 %copy-start.7 = (bf16[1,8,96,512]{3,2,1,0:T(8,128)(2,1)S(1)}, bf16[1,8,96,512]{3,2,1,0:T(8,128)(2,1)}, u32[]{:S(2)}) copy-start(bf16[1,8,96,512]{3,2,1,0:T(8,128)(2,1)} %get-tuple-element.45) | copy-start | bytes 2359300
  226.6 3.1 %copy-start.17 = (bf16[768,4096]{1,0:T(8,128)(2,1)S(1)}, bf16[768,4096]{1,0:T(8,128)(2,1)}, u32[]{:S(2)}) copy-start(bf16[768,4096]{1,0:T(8,128)(2,1)} %get-tuple-element.16) | copy-start | bytes 18874372
  227.6 5.3 %copy-start.12 = (bf16[768,512]{1,0:T(8,128)(2,1)}, bf16[768,512]{1,0:T(8,128)(2,1)S(1)}, u32[]{:S(2)}) copy-start(bf16[768,512]{1,0:T(8,128)(2,1)S(1)} %get-tuple-element.37) | copy-start | bytes 2359300
  232.9 10.2 %collective-permute-start.20 = (bf16[4096,256]{1,0:T(8,128)(2,1)}, bf16[4096,256]{1,0:T(8,128)(2,1)}, u32[]{:S(2)}, u32[]{:S(2)}) collective-permute-start(bf16[4096,256]{1,0:T(8,128)(2,1)} %convolution_convert_fusion), channel_id=1, source_target_pairs={{0,1},{1,0},{2,3},{3,2},{4,5},{5,4},{6,7},{7,6},{8,9},{9,8},{10,11... | collective-permute-start | bytes 6291464 | tf_op jit(solution)/shard_map/ppermute | solution.py:28
  236.6 6.5 %copy-start.6 = (bf16[8,512,256]{2,1,0:T(8,128)(2,1)S(1)}, bf16[8,512,256]{2,1,0:T(8,128)(2,1)}, u32[]{:S(2)}) copy-start(bf16[8,512,256]{2,1,0:T(8,128)(2,1)} %copy-done.5) | copy-start | bytes 6291460
  236.7 6.3 %collective-permute-start.21 = (f32[512]{0:T(512)S(1)}, f32[512]{0:T(512)S(1)}, u32[]{:S(2)}, u32[]{:S(2)}) collective-permute-start(f32[512]{0:T(512)S(1)} %get-tuple-element.38), channel_id=1, source_target_pairs={{0,1},{1,0},{2,3},{3,2},{4,5},{5,4},{6,7},{7,6},{8,9},{9,8},{10,11... | collective-permute-start | bytes 6152 | tf_op jit(solution)/shard_map/ppermute | solution.py:28
  (8 other events, 13.7 us)

commit v6 on v1

--- a/solution.py
+++ b/solution.py
@@ -10,7 +10,8 @@
 D = 4096
 STEPS = 2
 SHARD = ("y", "xh", "c")
-SHARD_ISLAND = ("y", "xh", "c", "island")
+ISLAND = ("xl", "z")
+SHARD_ISLAND = ("y", "xh", "c", "xl", "z")
 
 
 norm_epsilon = 1e-05
@@ -57,6 +58,7 @@
 
 
 BLOCK = 96
+VMEM_LIMIT = 40 * 1024 * 1024
 
 
 def forward_kernel(*refs):
@@ -144,7 +146,7 @@
             pltpu.SemaphoreType.DMA((2,)),
             pltpu.SemaphoreType.DMA((8,)),
         ],
-        compiler_params=pltpu.CompilerParams(vmem_limit_bytes=24 * 1024 * 1024),
+        compiler_params=pltpu.CompilerParams(vmem_limit_bytes=VMEM_LIMIT),
         cost_estimate=pl.CostEstimate(
             flops=2 * tokens * depth * features,
             bytes_accessed=4 * tokens * depth + 2 * depth * features,
@@ -158,17 +160,18 @@
     return param - inner_rate * (gradient / (jnp.abs(gradient) + adam_epsilon) + decay * param)
 
 
-def second_update(param, before, gradient, decay):
+def second_change(anchor, change, before, gradient, decay):
     beside = (1.0 - beta_one) / (1.0 - beta_one**2)
     first_hat = (beta_one * beside) * before + beside * gradient
     beside = (1.0 - beta_two) / (1.0 - beta_two**2)
     second_hat = (beta_two * beside) * (before * before) + beside * (gradient * gradient)
     root = second_hat * lax.rsqrt(jnp.maximum(second_hat, 1e-37))
-    return param - inner_rate * (first_hat / (root + adam_epsilon) + decay * param)
+    param = anchor - change
+    return change + inner_rate * (first_hat / (root + adam_epsilon) + decay * param)
 
 
 def per_device(weight_master, gain_master, weight_moment, gain_moment, attended, stream, targets):
-    islands = lax.axis_size("island")
+    islands = lax.axis_size(ISLAND)
     width_scale = D ** (-0.5)
     c = lax.axis_index("c")
     wide = weight_master.shape[1]
@@ -181,7 +184,7 @@
 
     owned, share = weight_master.shape[0], gain_master.shape[0]
     packed = with_gain(weight_master.astype(jnp.bfloat16), gain_master.astype(jnp.bfloat16))
-    packed = copy_for_each(packed, "island")
+    packed = copy_for_each(packed, ISLAND)
     packed_other = core_swap(packed)
     anchor_low = packed[:, :owned].reshape(D, wide)
     gain_anchor = packed[:, owned, :share].reshape(wide).astype(jnp.float32)
@@ -199,7 +202,6 @@
 
     weight_anchor = anchor_low.astype(jnp.float32)
     gain = jnp.concatenate([gain_anchor, gain_other])
-    weight = weight_anchor
     for step in range(STEPS):
         if step == 0:
             held, held_other = packed, packed_other
@@ -235,26 +237,35 @@
 
         other = over_tokens(slice(wide, None)).astype(jnp.bfloat16)
         other = core_swap(other)
-        mine = lax.optimization_barrier(over_tokens(slice(0, wide)))
-        weight_grad = (mine + other.astype(jnp.float32)) * width_scale
+        mine = lax.optimization_barrier(over_tokens(slice(0, wide)).astype(jnp.bfloat16))
+        weight_grad = (mine.astype(jnp.float32) + other.astype(jnp.float32)) * width_scale
         gain_other = core_swap(gain_grad)
         gain_grad = gain_grad + jnp.concatenate([gain_other[wide:], gain_other[:wide]])
         if step == 0:
-            weight = first_update(weight, weight_grad, decay_rate)
-            gain = first_update(gain, gain_grad, 0.0)
-            weight_low = weight.astype(jnp.bfloat16)
-            weight, weight_before, gain_before, weight_low = lax.optimization_barrier(
-                (weight, weight_grad, gain_grad, weight_low)
+            weight_low = first_update(weight_anchor, weight_grad, decay_rate)
+            weight_change = (weight_anchor - weight_low).astype(jnp.bfloat16)
+            weight_before = weight_grad.astype(jnp.bfloat16)
+            weight_low = weight_low.astype(jnp.bfloat16)
+            gain_first = gain
+            gain_before, gain = gain_grad, first_update(gain, gain_grad, 0.0)
+            weight_change, weight_before, weight_low = lax.optimization_barrier(
+                (weight_change, weight_before, weight_low)
             )
         else:
-            weight = second_update(weight, weight_before, weight_grad, decay_rate)
-            gain = second_update(gain, gain_before, gain_grad, 0.0)
+            weight_change = second_change(
+                weight_anchor,
+                weight_change.astype(jnp.float32),
+                weight_before.astype(jnp.float32),
+                weight_grad,
+                decay_rate,
+            )
+            gain_change = second_change(gain_first, gain_first - gain, gain_before, gain_grad, 0.0)
 
     sent = with_gain(
-        (weight_anchor - weight).astype(jnp.bfloat16).reshape(islands, owned, wide),
-        (gain_anchor - gain[:wide]).astype(jnp.bfloat16).reshape(islands, share),
+        weight_change.astype(jnp.bfloat16).reshape(islands, owned, wide),
+        gain_change[:wide].astype(jnp.bfloat16).reshape(islands, share),
     )
-    arrived = lax.all_to_all(sent, "island", split_axis=0, concat_axis=0, tiled=True)
+    arrived = lax.all_to_all(sent, ISLAND, split_axis=0, concat_axis=0, tiled=True)
     pseudo = arrived.astype(jnp.float32).sum(axis=0) / islands
     weight_pseudo, gain_pseudo = pseudo[:owned], pseudo[owned, :share]
     weight_velocity = outer_momentum * weight_moment + weight_pseudo
@@ -265,21 +276,19 @@
 
 
 def solution(mesh):
-    torus = Mesh(
-        mesh.devices.reshape(mesh.shape["island"], 4, 2, 2), ("island", "y", "xh", "c")
-    )
+    torus = Mesh(mesh.devices.reshape(2, 4, 4, 2, 2), (*ISLAND, *SHARD))
     return jax.shard_map(
         per_device,
         mesh=torus,
         in_specs=(
-            P("island", SHARD),
+            P(ISLAND, SHARD),
             P(SHARD_ISLAND),
-            P("island", SHARD),
+            P(ISLAND, SHARD),
             P(SHARD_ISLAND),
-            P("island", None, SHARD, None),
-            P("island", None, None, SHARD),
-            P("island", None, None, SHARD),
+            P(ISLAND, None, SHARD, None),
+            P(ISLAND, None, None, SHARD),
+            P(ISLAND, None, None, SHARD),
         ),
-        out_specs=(P("island", SHARD), P(SHARD_ISLAND), P("island", SHARD), P(SHARD_ISLAND)),
+        out_specs=(P(ISLAND, SHARD), P(SHARD_ISLAND), P(ISLAND, SHARD), P(SHARD_ISLAND)),
         check_vma=False,
     )

time: 280 us -> 277 us (0.989)
  local copies, waits for them, and re-layouts: 16.2 us -> 12.2 us
  other arithmetic: 22.4 us -> 19.4 us
    unnamed x38, local copies, waits for them, and re-layouts: 12.1 us -> 7.62 us
    convert_element_type x3, other arithmetic: 12.7 us -> 9.65 us  [the longest x1 5.86 us: per_device(): weight_change.astype(jnp.bfloat16).reshape(islands, owned, wide)]
  transfers between devices with their start and end apart: 22 -> 22, of which waited for: 12 -> 11; matrix products, arithmetic and copies ran while one was open for 6% -> 7% of each run, Pallas kernels for 0% -> 0%
where the time goes in v6:
time: 277 us; the launch traced here: 276 us
  waiting for transfers between devices  102 us (37%)
  blocking collectives  84.1 us (30%)
  starting transfers between devices  29 us (10%)
  other arithmetic  19.4 us (7%)
  Pallas kernels  14.6 us (5%)
  matrix products  13.4 us (5%)
  local copies, waits for them, and re-layouts  12.2 us (4%)
    ppermute x12, waiting for transfers between devices, y_hop(): return lax.ppermute(value, ('y', 'c'), pairs)  76.6 us
    all_to_all x3, blocking collectives, copy_for_each(): return lax.all_to_all(copies, axis, split_axis=0, concat_axis=0, tiled=True)  54.5 us
    all_to_all x1, blocking collectives, per_device(): lax.all_to_all(sent, ISLAND, split_axis=0, concat_axis=0, tiled=True)  29.6 us
    ppermute x2, waiting for transfers between devices, x_swap(): return lax.ppermute(value, 'xh', [(0, 1), (1, 0)])  24.7 us
    pallas_call x2, Pallas kernels, forward(): pl.pallas_call(forward_kernel, out_shape=(jax.ShapeDtypeStruct((tokens, f...  14.6 us
    dot_general x4, matrix products, over_tokens(): jnp.einsum('td,tf->df', rows, residual_grad[:, columns], preferred_elemen...  13.4 us
    ppermute x12, starting transfers between devices, y_hop(): return lax.ppermute(value, ('y', 'c'), pairs)  13.2 us
    ppermute x8, starting transfers between devices, core_swap(): return lax.ppermute(value, 'c', [(0, 1), (1, 0)])  12.8 us
  transfers between devices with their start and end apart: 22, of which 11 were waited for; matrix products, arithmetic and copies ran while one was open for 7% of the time, Pallas kernels for 0%

profile of v6, /device:TPU:1, one launch (start us, length us, event | category | flops | bytes accessed | tf_op | source)
XLA Modules:
  0.0 276.1 jit_solution(5087071532986911328)
XLA Ops:
  2.5 33.4 %all_to_all.20.refs_8_ = bf16[8,528,256]{2,1,0:T(8,128)(2,1)S(1)} all-to-all(bf16[8,528,256]{2,1,0:T(8,128)(2,1)S(1)} %broadcast_in_dim.9), channel_id=1, replica_groups=mesh['xl'=2,'z'=4,'y'=4,'xh'=2,'c'=2] {'xl','z'}, dimensions={0} | all-to-all | bytes 4325376 | tf_op jit(solution)/shard_map/all_to_all | solution.py:46
  36.0 2.3 collective-permute-start.7
  39.3 2.5 collective-permute-start
  41.8 2.7 collective-permute-start.1
  46.9 13.2 %collective-permute-done.refs_1_ = bf16[96,4096]{1,0:T(8,128)(2,1)} collective-permute-done((bf16[96,4096]{1,0:T(8,128)(2,1)}, bf16[96,4096]{1,0:T(8,128)(2,1)}, u32[]{:S(2)}, u32[]{:S(2)}) %collective-permute-start) | collective-permute-done | bytes 786464 | tf_op jit(solution)/shard_map/ppermute | solution.py:32
  64.4 11.7 %collective-permute-done.4.refs_5_ = bf16[96,4096]{1,0:T(8,128)(2,1)} collective-permute-done((bf16[96,4096]{1,0:T(8,128)(2,1)}, bf16[96,4096]{1,0:T(8,128)(2,1)}, u32[]{:S(2)}, u32[]{:S(2)}) %collective-permute-start.4) | collective-permute-done | bytes 786464 | tf_op jit(solution)/shard_map/ppermute | solution.py:41
  80.5 12.3 %collective-permute-done.2.refs_3_ = bf16[96,4096]{1,0:T(8,128)(2,1)} collective-permute-done((bf16[96,4096]{1,0:T(8,128)(2,1)}, bf16[96,4096]{1,0:T(8,128)(2,1)}, u32[]{:S(2)}, u32[]{:S(2)}) %collective-permute-start.2) | collective-permute-done | bytes 786464 | tf_op jit(solution)/shard_map/ppermute | solution.py:41
  92.9 6.5 %collective-permute-done.5.refs_6_ = bf16[96,4096]{1,0:T(8,128)(2,1)} collective-permute-done((bf16[96,4096]{1,0:T(8,128)(2,1)}, bf16[96,4096]{1,0:T(8,128)(2,1)}, u32[]{:S(2)}, u32[]{:S(2)}) %collective-permute-start.5) | collective-permute-done | bytes 786464 | tf_op jit(solution)/shard_map/ppermute | solution.py:41
  99.4 6.8 %collective-permute-done.6.refs_7_ = bf16[96,4096]{1,0:T(8,128)(2,1)} collective-permute-done((bf16[96,4096]{1,0:T(8,128)(2,1)}, bf16[96,4096]{1,0:T(8,128)(2,1)}, u32[]{:S(2)}, u32[]{:S(2)}) %collective-permute-start.6) | collective-permute-done | bytes 786464 | tf_op jit(solution)/shard_map/ppermute | solution.py:41
  106.2 1.6 copy-done.1
  109.0 8.4 %forward.2 = (f32[768,512]{1,0:T(8,128)S(1)}, bf16[768,4096]{1,0:T(8,128)(2,1)}) custom-call(bf16[96,4096]{1,0:T(8,128)(2,1)} %get-tuple-element.53.refs_0_, bf16[96,4096]{1,0:T(8,128)(2,1)} %collective-permute-done.refs_1_, bf16[96,4096]{1,0:T(8,128)(2,1)} %collective-permute-done.1.refs_2_, bf16[96,4096]{1,0:T(8,128)(2,1)} %collective-permute-done.2.refs_3_, ...), custom_call_target="tpu_custom_call" | custom-call | flops 3221225472 | bytes 16777216 | tf_op jit(solution)/shard_map/forward/pallas_call | solution.py:134
  117.9 11.9 %all_to_all.21 = f32[8,1,2304]{2,1,0:T(1,128)S(1)} all-to-all(f32[8,1,2304]{2,1,0:T(1,128)S(1)} %broadcast_in_dim.10), channel_id=1, replica_groups=mesh['xl'=2,'z'=4,'y'=4,'xh'=2,'c'=2] {'y','xh'}, dimensions={0} | all-to-all | bytes 147456 | tf_op jit(solution)/shard_map/all_to_all | solution.py:46
  131.0 1.8 copy-done.16
  132.7 2.0 convolution_convert_fusion.2
  134.7 4.2 %collective-permute-start.10 = (bf16[4096,256]{1,0:T(8,128)(2,1)S(1)}, bf16[4096,256]{1,0:T(8,128)(2,1)S(1)}, u32[]{:S(2)}, u32[]{:S(2)}) collective-permute-start(bf16[4096,256]{1,0:T(8,128)(2,1)S(1)} %convolution_convert_fusion.2), channel_id=1, source_target_pairs={{0,1},{1,0},{2,3},{3,2},{4,5},{5,4},{6,7},{7,6},{8,9},{9,8},{10,11... | collective-permute-start | bytes 6291464 | tf_op jit(solution)/shard_map/ppermute | solution.py:28
  139.5 2.0 convolution_convert_fusion.3
  142.7 3.8 %fusion.49 = (bf16[4096,256]{1,0:T(8,128)(2,1)S(1)}, bf16[4096,256]{1,0:T(8,128)(2,1)}, bf16[4096,256]{1,0:T(8,128)(2,1)}) fusion(bf16[4096,256]{1,0:T(8,128)(2,1)S(1)} %collective-permute-done.10, bf16[4096,256]{1,0:T(8,128)(2,1)S(1)} %convolution_convert_fusion.3, bf16[8,512,256]{2,1,0:T(8,128)(2,1)S(1)} %slice.140), kind=kLoop, calls=%fused_computation.122 | loop fusion | flops 16777216 | bytes 12582912 | tf_op jit(solution)/shard_map/convert_element_type | solution.py:248
  147.7 11.5 %collective-permute-done.11.refs_1_ = bf16[96,4096]{1,0:T(8,128)(2,1)S(1)} collective-permute-done((bf16[96,4096]{1,0:T(8,128)(2,1)S(1)}, bf16[96,4096]{1,0:T(8,128)(2,1)S(1)}, u32[]{:S(2)}, u32[]{:S(2)}) %collective-permute-start.11) | collective-permute-done | bytes 786464 | tf_op jit(solution)/shard_map/ppermute | solution.py:32
  159.5 2.0 collective-permute-start.19
  162.1 2.1 collective-permute-start.14
  164.2 11.9 %collective-permute-done.15.refs_5_ = bf16[96,4096]{1,0:T(8,128)(2,1)S(1)} collective-permute-done((bf16[96,4096]{1,0:T(8,128)(2,1)S(1)}, bf16[96,4096]{1,0:T(8,128)(2,1)S(1)}, u32[]{:S(2)}, u32[]{:S(2)}) %collective-permute-start.15) | collective-permute-done | bytes 786464 | tf_op jit(solution)/shard_map/ppermute | solution.py:41
  177.5 15.4 %collective-permute-done.13.refs_3_ = bf16[96,4096]{1,0:T(8,128)(2,1)S(1)} collective-permute-done((bf16[96,4096]{1,0:T(8,128)(2,1)S(1)}, bf16[96,4096]{1,0:T(8,128)(2,1)S(1)}, u32[]{:S(2)}, u32[]{:S(2)}) %collective-permute-start.13) | collective-permute-done | bytes 786464 | tf_op jit(solution)/shard_map/ppermute | solution.py:41
  192.9 5.6 %collective-permute-done.16.refs_6_ = bf16[96,4096]{1,0:T(8,128)(2,1)S(1)} collective-permute-done((bf16[96,4096]{1,0:T(8,128)(2,1)S(1)}, bf16[96,4096]{1,0:T(8,128)(2,1)S(1)}, u32[]{:S(2)}, u32[]{:S(2)}) %collective-permute-start.16) | collective-permute-done | bytes 786464 | tf_op jit(solution)/shard_map/ppermute | solution.py:41
  198.5 6.5 %collective-permute-done.17.refs_7_ = bf16[96,4096]{1,0:T(8,128)(2,1)S(1)} collective-permute-done((bf16[96,4096]{1,0:T(8,128)(2,1)S(1)}, bf16[96,4096]{1,0:T(8,128)(2,1)S(1)}, u32[]{:S(2)}, u32[]{:S(2)}) %collective-permute-start.17) | collective-permute-done | bytes 786464 | tf_op jit(solution)/shard_map/ppermute | solution.py:41
  205.0 6.3 %forward.3 = (f32[768,512]{1,0:T(8,128)S(1)}, bf16[768,4096]{1,0:T(8,128)(2,1)}) custom-call(bf16[96,4096]{1,0:T(8,128)(2,1)S(1)} %get-tuple-element.54.refs_0_, bf16[96,4096]{1,0:T(8,128)(2,1)S(1)} %collective-permute-done.11.refs_1_, bf16[96,4096]{1,0:T(8,128)(2,1)S(1)} %collective-permute-done.12.refs_2_, ...), custom_call_target="tpu_custom_call" | custom-call | flops 3221225472 | bytes 16777216 | tf_op jit(solution)/shard_map/forward/pallas_call | solution.py:134
  211.8 9.1 %all_to_all.22 = f32[8,1,2304]{2,1,0:T(1,128)S(1)} all-to-all(f32[8,1,2304]{2,1,0:T(1,128)S(1)} %broadcast_in_dim.11), channel_id=1, replica_groups=mesh['xl'=2,'z'=4,'y'=4,'xh'=2,'c'=2] {'y','xh'}, dimensions={0} | all-to-all | bytes 147456 | tf_op jit(solution)/shard_map/all_to_all | solution.py:46
  222.1 2.0 copy-done.17
  224.2 3.3 %convolution_convert_fusion = bf16[4096,256]{1,0:T(8,128)(2,1)} fusion(bf16[768,4096]{1,0:T(8,128)(2,1)S(1)} %copy-done.17, bf16[768,512]{1,0:T(8,128)(2,1)S(1)} %get-tuple-element.37), kind=kOutput, calls=%fused_computation.7 | convolution fusion | flops 1611661312 | bytes 8781824 | tf_op jit(solution)/shard_map/td,tf->df/dot_general | solution.py:234
  227.5 3.5 %collective-permute-start.20 = (bf16[4096,256]{1,0:T(8,128)(2,1)}, bf16[4096,256]{1,0:T(8,128)(2,1)}, u32[]{:S(2)}, u32[]{:S(2)}) collective-permute-start(bf16[4096,256]{1,0:T(8,128)(2,1)} %convolution_convert_fusion), channel_id=1, source_target_pairs={{0,1},{1,0},{2,3},{3,2},{4,5},{5,4},{6,7},{7,6},{8,9},{9,8},{10,11... | collective-permute-start | bytes 6291464 | tf_op jit(solution)/shard_map/ppermute | solution.py:28
  231.2 6.1 %convolution_convert_fusion.1 = bf16[4096,256]{1,0:T(8,128)(2,1)} fusion(bf16[768,4096]{1,0:T(8,128)(2,1)} %get-tuple-element.16, bf16[768,512]{1,0:T(8,128)(2,1)} %copy-done.12), kind=kOutput, calls=%fused_computation.8 | convolution fusion | flops 1611661312 | bytes 8781824 | tf_op jit(solution)/shard_map/td,tf->df/dot_general | solution.py:234
  237.7 5.9 %fusion.1 = bf16[4096,256]{1,0:T(8,128)(2,1)S(1)} fusion(bf16[4096,256]{1,0:T(8,128)(2,1)} %get-tuple-element.13, bf16[4096,256]{1,0:T(8,128)(2,1)} %get-tuple-element.14, bf16[4096,256]{1,0:T(8,128)(2,1)} %collective-permute-done.20, bf16[4096,256]{1,0:T(8,128)(2,1)} %convolution_convert_fusion.1, bf16[8,512,256]{2,1,0:T(8,128)(2,1)S(1)} %copy-done.6), kind=kLoop, calls=%fused_computation.14 | loop fusion | flops 26214400 | bytes 12582912 | tf_op jit(solution)/shard_map/convert_element_type | solution.py:265
  243.7 29.6 %all_to_all.23 = bf16[8,528,256]{2,1,0:T(8,128)(2,1)S(1)} all-to-all(bf16[8,528,256]{2,1,0:T(8,128)(2,1)S(1)} %fusion.13), channel_id=1, replica_groups=mesh['xl'=2,'z'=4,'y'=4,'xh'=2,'c'=2] {'xl','z'}, dimensions={0} | all-to-all | bytes 4325376 | tf_op jit(solution)/shard_map/all_to_all | solution.py:268
  (112 shorter events, 27.5 us)
Async XLA Ops:
  2.5 35.7 %copy-start.10 = (bf16[1,2,96,4096]{3,2,1,0:T(8,128)(2,1)S(1)}, bf16[1,2,96,4096]{3,2,1,0:T(8,128)(2,1)}, u32[]{:S(2)}) copy-start(bf16[1,2,96,4096]{3,2,1,0:T(8,128)(2,1)} %param.11) | copy-start | bytes 4718596
  36.0 43.6 %copy-start = (bf16[8,528,256]{2,1,0:T(8,128)(2,1)}, bf16[8,528,256]{2,1,0:T(8,128)(2,1)S(1)}, u32[]{:S(2)}) copy-start(bf16[8,528,256]{2,1,0:T(8,128)(2,1)S(1)} %all_to_all.20.refs_8_) | copy-start | bytes 6488068
  36.0 43.7 %collective-permute-start.7 = (bf16[8,528,256]{2,1,0:T(8,128)(2,1)S(1)}, bf16[8,528,256]{2,1,0:T(8,128)(2,1)}, u32[]{:S(2)}, u32[]{:S(2)}) collective-permute-start(bf16[8,528,256]{2,1,0:T(8,128)(2,1)S(1)} %all_to_all.20.refs_8_), channel_id=1, source_target_pairs={{0,1},{1,0},{2,3},{3,2},{4,5},{5,4},{6,7},{7,6},{8,9},{9,8},{10,11... | collective-permute-start | bytes 6488072 | tf_op jit(solution)/shard_map/ppermute | solution.py:28
  39.3 20.7 %collective-permute-start = (bf16[96,4096]{1,0:T(8,128)(2,1)}, bf16[96,4096]{1,0:T(8,128)(2,1)}, u32[]{:S(2)}, u32[]{:S(2)}) collective-permute-start(bf16[96,4096]{1,0:T(8,128)(2,1)} %get-tuple-element.53.refs_0_), channel_id=1, source_target_pairs={{0,2},{2,0},{1,3},{3,1},{4,6},{6,4},{5,7},{7,5},{8,10},{10,8},{9,1... | collective-permute-start | bytes 2359304 | tf_op jit(solution)/shard_map/ppermute | solution.py:32
  41.8 20.9 %collective-permute-start.1 = (bf16[96,4096]{1,0:T(8,128)(2,1)}, bf16[96,4096]{1,0:T(8,128)(2,1)}, u32[]{:S(2)}, u32[]{:S(2)}) collective-permute-start(bf16[96,4096]{1,0:T(8,128)(2,1)} %get-tuple-element.53.refs_0_), channel_id=1, source_target_pairs={{0,4},{1,13},{4,8},{5,1},{8,12},{9,5},{12,0},{13,9},{2,6},{3,15},{... | collective-permute-start | bytes 2359304 | tf_op jit(solution)/shard_map/ppermute | solution.py:41
  46.1 15.2 %collective-permute-start.8 = (bf16[2,8,96,256]{3,2,1,0:T(8,128)(2,1)S(1)}, bf16[2,8,96,256]{3,2,1,0:T(8,128)(2,1)S(1)}, u32[]{:S(2)}, u32[]{:S(2)}) collective-permute-start(bf16[2,8,96,256]{3,2,1,0:T(8,128)(2,1)S(1)} %get-tuple-element.51), channel_id=1, source_target_pairs={{0,1},{1,0},{2,3},{3,2},{4,5},{5,4},{6,7},{7,6},{8,9},{9,8},{10,11... | collective-permute-start | bytes 2359304 | tf_op jit(solution)/shard_map/ppermute | solution.py:28
  46.5 17.5 %collective-permute-start.9 = (bf16[2,8,96,256]{3,2,1,0:T(8,128)(2,1)S(1)}, bf16[2,8,96,256]{3,2,1,0:T(8,128)(2,1)S(1)}, u32[]{:S(2)}, u32[]{:S(2)}) collective-permute-start(bf16[2,8,96,256]{3,2,1,0:T(8,128)(2,1)S(1)} %get-tuple-element.49), channel_id=1, source_target_pairs={{0,1},{1,0},{2,3},{3,2},{4,5},{5,4},{6,7},{7,6},{8,9},{9,8},{10,11... | collective-permute-start | bytes 2359304 | tf_op jit(solution)/shard_map/ppermute | solution.py:28
  60.1 15.9 %collective-permute-start.4 = (bf16[96,4096]{1,0:T(8,128)(2,1)}, bf16[96,4096]{1,0:T(8,128)(2,1)}, u32[]{:S(2)}, u32[]{:S(2)}) collective-permute-start(bf16[96,4096]{1,0:T(8,128)(2,1)} %collective-permute-done.refs_1_), channel_id=1, source_target_pairs={{0,12},{1,5},{4,0},{5,9},{8,4},{9,13},{12,8},{13,1},{2,14},{3,7},{... | collective-permute-start | bytes 2359304 | tf_op jit(solution)/shard_map/ppermute | solution.py:41
  61.4 31.5 %collective-permute-start.2 = (bf16[96,4096]{1,0:T(8,128)(2,1)}, bf16[96,4096]{1,0:T(8,128)(2,1)}, u32[]{:S(2)}, u32[]{:S(2)}) collective-permute-start(bf16[96,4096]{1,0:T(8,128)(2,1)} %get-tuple-element.53.refs_0_), channel_id=1, source_target_pairs={{0,12},{1,5},{4,0},{5,9},{8,4},{9,13},{12,8},{13,1},{2,14},{3,7},{... | collective-permute-start | bytes 2359304 | tf_op jit(solution)/shard_map/ppermute | solution.py:41
  62.7 30.2 %collective-permute-start.3 = (bf16[96,4096]{1,0:T(8,128)(2,1)}, bf16[96,4096]{1,0:T(8,128)(2,1)}, u32[]{:S(2)}, u32[]{:S(2)}) collective-permute-start(bf16[96,4096]{1,0:T(8,128)(2,1)} %collective-permute-done.refs_1_), channel_id=1, source_target_pairs={{0,4},{1,13},{4,8},{5,1},{8,12},{9,5},{12,0},{13,9},{2,6},{3,15},{... | collective-permute-start | bytes 2359304 | tf_op jit(solution)/shard_map/ppermute | solution.py:41
  64.1 35.3 %collective-permute-start.5 = (bf16[96,4096]{1,0:T(8,128)(2,1)}, bf16[96,4096]{1,0:T(8,128)(2,1)}, u32[]{:S(2)}, u32[]{:S(2)}) collective-permute-start(bf16[96,4096]{1,0:T(8,128)(2,1)} %collective-permute-done.1.refs_2_), channel_id=1, source_target_pairs={{0,4},{1,13},{4,8},{5,1},{8,12},{9,5},{12,0},{13,9},{2,6},{3,15},{... | collective-permute-start | bytes 2359304 | tf_op jit(solution)/shard_map/ppermute | solution.py:41
  76.0 30.2 %collective-permute-start.6 = (bf16[96,4096]{1,0:T(8,128)(2,1)}, bf16[96,4096]{1,0:T(8,128)(2,1)}, u32[]{:S(2)}, u32[]{:S(2)}) collective-permute-start(bf16[96,4096]{1,0:T(8,128)(2,1)} %collective-permute-done.4.refs_5_), channel_id=1, source_target_pairs={{0,12},{1,5},{4,0},{5,9},{8,4},{9,13},{12,8},{13,1},{2,14},{3,7},{... | collective-permute-start | bytes 2359304 | tf_op jit(solution)/shard_map/ppermute | solution.py:41
  109.0 8.4 %copy-start.8 = (bf16[1,8,96,512]{3,2,1,0:T(8,128)(2,1)S(1)}, bf16[1,8,96,512]{3,2,1,0:T(8,128)(2,1)}, u32[]{:S(2)}) copy-start(bf16[1,8,96,512]{3,2,1,0:T(8,128)(2,1)} %get-tuple-element.46) | copy-start | bytes 2359300
  132.7 6.6 %copy-start.2 = (bf16[8,528,256]{2,1,0:T(8,128)(2,1)S(1)}, bf16[8,528,256]{2,1,0:T(8,128)(2,1)}, u32[]{:S(2)}) copy-start(bf16[8,528,256]{2,1,0:T(8,128)(2,1)} %copy-done) | copy-start | bytes 6488068
  134.7 8.0 %collective-permute-start.10 = (bf16[4096,256]{1,0:T(8,128)(2,1)S(1)}, bf16[4096,256]{1,0:T(8,128)(2,1)S(1)}, u32[]{:S(2)}, u32[]{:S(2)}) collective-permute-start(bf16[4096,256]{1,0:T(8,128)(2,1)S(1)} %convolution_convert_fusion.2), channel_id=1, source_target_pairs={{0,1},{1,0},{2,3},{3,2},{4,5},{5,4},{6,7},{7,6},{8,9},{9,8},{10,11... | collective-permute-start | bytes 6291464 | tf_op jit(solution)/shard_map/ppermute | solution.py:28
  138.9 20.3 %collective-permute-start.11 = (bf16[96,4096]{1,0:T(8,128)(2,1)S(1)}, bf16[96,4096]{1,0:T(8,128)(2,1)S(1)}, u32[]{:S(2)}, u32[]{:S(2)}) collective-permute-start(bf16[96,4096]{1,0:T(8,128)(2,1)S(1)} %get-tuple-element.54.refs_0_), channel_id=1, source_target_pairs={{0,2},{2,0},{1,3},{3,1},{4,6},{6,4},{5,7},{7,5},{8,10},{10,8},{9,1... | collective-permute-start | bytes 2359304 | tf_op jit(solution)/shard_map/ppermute | solution.py:32
  139.5 3.2 %copy-start.5 = (bf16[8,512,256]{2,1,0:T(8,128)(2,1)}, bf16[8,512,256]{2,1,0:T(8,128)(2,1)S(1)}, u32[]{:S(2)}) copy-start(bf16[8,512,256]{2,1,0:T(8,128)(2,1)S(1)} %slice.140) | copy-start | bytes 6291460
  141.5 63.5 %copy-start.3 = (bf16[1,8,96,512]{3,2,1,0:T(8,128)(2,1)S(1)}, bf16[1,8,96,512]{3,2,1,0:T(8,128)(2,1)}, u32[]{:S(2)}) copy-start(bf16[1,8,96,512]{3,2,1,0:T(8,128)(2,1)} %get-tuple-element.47) | copy-start | bytes 2359300
  146.4 58.5 %collective-permute-start.18 = (bf16[8,512,256]{2,1,0:T(8,128)(2,1)S(1)}, bf16[8,512,256]{2,1,0:T(8,128)(2,1)S(1)}, u32[]{:S(2)}, u32[]{:S(2)}) collective-permute-start(bf16[8,512,256]{2,1,0:T(8,128)(2,1)S(1)} %bitcast.54), channel_id=1, source_target_pairs={{0,1},{1,0},{2,3},{3,2},{4,5},{5,4},{6,7},{7,6},{8,9},{9,8},{10,11... | collective-permute-start | bytes 6291464 | tf_op jit(solution)/shard_map/ppermute | solution.py:28
  146.8 15.3 %collective-permute-start.12 = (bf16[96,4096]{1,0:T(8,128)(2,1)S(1)}, bf16[96,4096]{1,0:T(8,128)(2,1)S(1)}, u32[]{:S(2)}, u32[]{:S(2)}) collective-permute-start(bf16[96,4096]{1,0:T(8,128)(2,1)S(1)} %get-tuple-element.54.refs_0_), channel_id=1, source_target_pairs={{0,4},{1,13},{4,8},{5,1},{8,12},{9,5},{12,0},{13,9},{2,6},{3,15},{... | collective-permute-start | bytes 2359304 | tf_op jit(solution)/shard_map/ppermute | solution.py:41
  159.2 16.8 %collective-permute-start.15 = (bf16[96,4096]{1,0:T(8,128)(2,1)S(1)}, bf16[96,4096]{1,0:T(8,128)(2,1)S(1)}, u32[]{:S(2)}, u32[]{:S(2)}) collective-permute-start(bf16[96,4096]{1,0:T(8,128)(2,1)S(1)} %collective-permute-done.11.refs_1_), channel_id=1, source_target_pairs={{0,12},{1,5},{4,0},{5,9},{8,4},{9,13},{12,8},{13,1},{2,14},{3,7},{... | collective-permute-start | bytes 2359304 | tf_op jit(solution)/shard_map/ppermute | solution.py:41
  159.5 16.6 %collective-permute-start.19 = (f32[512]{0:T(512)S(1)}, f32[512]{0:T(512)S(1)}, u32[]{:S(2)}, u32[]{:S(2)}) collective-permute-start(f32[512]{0:T(512)S(1)} %get-tuple-element.39), channel_id=1, source_target_pairs={{0,1},{1,0},{2,3},{3,2},{4,5},{5,4},{6,7},{7,6},{8,9},{9,8},{10,11... | collective-permute-start | bytes 6152 | tf_op jit(solution)/shard_map/ppermute | solution.py:28
  161.5 31.4 %collective-permute-start.13 = (bf16[96,4096]{1,0:T(8,128)(2,1)S(1)}, bf16[96,4096]{1,0:T(8,128)(2,1)S(1)}, u32[]{:S(2)}, u32[]{:S(2)}) collective-permute-start(bf16[96,4096]{1,0:T(8,128)(2,1)S(1)} %get-tuple-element.54.refs_0_), channel_id=1, source_target_pairs={{0,12},{1,5},{4,0},{5,9},{8,4},{9,13},{12,8},{13,1},{2,14},{3,7},{... | collective-permute-start | bytes 2359304 | tf_op jit(solution)/shard_map/ppermute | solution.py:41
  162.1 30.8 %collective-permute-start.14 = (bf16[96,4096]{1,0:T(8,128)(2,1)S(1)}, bf16[96,4096]{1,0:T(8,128)(2,1)S(1)}, u32[]{:S(2)}, u32[]{:S(2)}) collective-permute-start(bf16[96,4096]{1,0:T(8,128)(2,1)S(1)} %collective-permute-done.11.refs_1_), channel_id=1, source_target_pairs={{0,4},{1,13},{4,8},{5,1},{8,12},{9,5},{12,0},{13,9},{2,6},{3,15},{... | collective-permute-start | bytes 2359304 | tf_op jit(solution)/shard_map/ppermute | solution.py:41
  176.0 22.5 %collective-permute-start.16 = (bf16[96,4096]{1,0:T(8,128)(2,1)S(1)}, bf16[96,4096]{1,0:T(8,128)(2,1)S(1)}, u32[]{:S(2)}, u32[]{:S(2)}) collective-permute-start(bf16[96,4096]{1,0:T(8,128)(2,1)S(1)} %collective-permute-done.12.refs_2_), channel_id=1, source_target_pairs={{0,4},{1,13},{4,8},{5,1},{8,12},{9,5},{12,0},{13,9},{2,6},{3,15},{... | collective-permute-start | bytes 2359304 | tf_op jit(solution)/shard_map/ppermute | solution.py:41
  176.0 28.9 %collective-permute-start.17 = (bf16[96,4096]{1,0:T(8,128)(2,1)S(1)}, bf16[96,4096]{1,0:T(8,128)(2,1)S(1)}, u32[]{:S(2)}, u32[]{:S(2)}) collective-permute-start(bf16[96,4096]{1,0:T(8,128)(2,1)S(1)} %collective-permute-done.15.refs_5_), channel_id=1, source_target_pairs={{0,12},{1,5},{4,0},{5,9},{8,4},{9,13},{12,8},{13,1},{2,14},{3,7},{... | collective-permute-start | bytes 2359304 | tf_op jit(solution)/shard_map/ppermute | solution.py:41
  205.0 6.3 %copy-start.7 = (bf16[1,8,96,512]{3,2,1,0:T(8,128)(2,1)S(1)}, bf16[1,8,96,512]{3,2,1,0:T(8,128)(2,1)}, u32[]{:S(2)}) copy-start(bf16[1,8,96,512]{3,2,1,0:T(8,128)(2,1)} %get-tuple-element.45) | copy-start | bytes 2359300
  221.1 3.1 %copy-start.17 = (bf16[768,4096]{1,0:T(8,128)(2,1)S(1)}, bf16[768,4096]{1,0:T(8,128)(2,1)}, u32[]{:S(2)}) copy-start(bf16[768,4096]{1,0:T(8,128)(2,1)} %get-tuple-element.16) | copy-start | bytes 18874372
  222.1 5.4 %copy-start.12 = (bf16[768,512]{1,0:T(8,128)(2,1)}, bf16[768,512]{1,0:T(8,128)(2,1)S(1)}, u32[]{:S(2)}) copy-start(bf16[768,512]{1,0:T(8,128)(2,1)S(1)} %get-tuple-element.37) | copy-start | bytes 2359300
  227.5 10.2 %collective-permute-start.20 = (bf16[4096,256]{1,0:T(8,128)(2,1)}, bf16[4096,256]{1,0:T(8,128)(2,1)}, u32[]{:S(2)}, u32[]{:S(2)}) collective-permute-start(bf16[4096,256]{1,0:T(8,128)(2,1)} %convolution_convert_fusion), channel_id=1, source_target_pairs={{0,1},{1,0},{2,3},{3,2},{4,5},{5,4},{6,7},{7,6},{8,9},{9,8},{10,11... | collective-permute-start | bytes 6291464 | tf_op jit(solution)/shard_map/ppermute | solution.py:28
  231.2 6.5 %copy-start.6 = (bf16[8,512,256]{2,1,0:T(8,128)(2,1)S(1)}, bf16[8,512,256]{2,1,0:T(8,128)(2,1)}, u32[]{:S(2)}) copy-start(bf16[8,512,256]{2,1,0:T(8,128)(2,1)} %copy-done.5) | copy-start | bytes 6291460
  231.2 6.3 %collective-permute-start.21 = (f32[512]{0:T(512)S(1)}, f32[512]{0:T(512)S(1)}, u32[]{:S(2)}, u32[]{:S(2)}) collective-permute-start(f32[512]{0:T(512)S(1)} %get-tuple-element.38), channel_id=1, source_target_pairs={{0,1},{1,0},{2,3},{3,2},{4,5},{5,4},{6,7},{7,6},{8,9},{9,8},{10,11... | collective-permute-start | bytes 6152 | tf_op jit(solution)/shard_map/ppermute | solution.py:28
  (8 other events, 13.7 us)

commit v7 on v6

--- a/solution.py
+++ b/solution.py
@@ -58,7 +58,7 @@
 
 
 BLOCK = 96
-VMEM_LIMIT = 40 * 1024 * 1024
+VMEM_LIMITS = (40, 40)
 
 
 def forward_kernel(*refs):
@@ -125,7 +125,7 @@
         give.wait()
 
 
-def forward(pieces, weight, weight_other, flow):
+def forward(pieces, weight, weight_other, flow, vmem_limit):
     anywhere = pl.BlockSpec(memory_space=pl.ANY)
     inside = pl.BlockSpec(memory_space=pltpu.VMEM)
     tokens, features = flow.shape
@@ -146,7 +146,7 @@
             pltpu.SemaphoreType.DMA((2,)),
             pltpu.SemaphoreType.DMA((8,)),
         ],
-        compiler_params=pltpu.CompilerParams(vmem_limit_bytes=VMEM_LIMIT),
+        compiler_params=pltpu.CompilerParams(vmem_limit_bytes=vmem_limit * 1024 * 1024),
         cost_estimate=pl.CostEstimate(
             flops=2 * tokens * depth * features,
             bytes_accessed=4 * tokens * depth + 2 * depth * features,
@@ -176,7 +176,9 @@
     c = lax.axis_index("c")
     wide = weight_master.shape[1]
 
-    pieces = [gathered_pieces(attended[0][step]) for step in range(STEPS)]
+    pieces = [gathered_pieces(attended[0][0])]
+    later, _ = lax.optimization_barrier((attended, pieces[0][2]))
+    pieces.append(gathered_pieces(later[0][1]))
 
     def with_gain(weight_rows, gain_rows):
         filled = [(0, 0)] * (gain_rows.ndim - 1) + [(0, 15), (0, wide - gain_rows.shape[-1])]
@@ -208,7 +210,9 @@
         else:
             held = weight_low.reshape(islands, owned, wide)
             held_other = core_swap(held)
-        residual, rows = forward(pieces[step], held, held_other, stream_half[step])
+        residual, rows = forward(
+            pieces[step], held, held_other, stream_half[step], VMEM_LIMITS[step]
+        )
         goal = target_half[step].astype(jnp.float32)
         scaled = residual * gain
         sums = [

time: 277 us -> 276 us (level)
  no operation moved by 1% of the time
where the time goes in v7:
time: 276 us; the launch traced here: 275 us
  waiting for transfers between devices  103 us (37%)
  blocking collectives  84.1 us (30%)
  starting transfers between devices  28.8 us (10%)
  other arithmetic  19.4 us (7%)
  Pallas kernels  14.4 us (5%)
  matrix products  13.4 us (5%)
  local copies, waits for them, and re-layouts  10.9 us (4%)
    ppermute x12, waiting for transfers between devices, y_hop(): return lax.ppermute(value, ('y', 'c'), pairs)  76.9 us
    all_to_all x3, blocking collectives, copy_for_each(): return lax.all_to_all(copies, axis, split_axis=0, concat_axis=0, tiled=True)  54.5 us
    all_to_all x1, blocking collectives, per_device(): lax.all_to_all(sent, ISLAND, split_axis=0, concat_axis=0, tiled=True)  29.6 us
    ppermute x2, waiting for transfers between devices, x_swap(): return lax.ppermute(value, 'xh', [(0, 1), (1, 0)])  25.2 us
    pallas_call x2, Pallas kernels, forward(): pl.pallas_call(forward_kernel, out_shape=(jax.ShapeDtypeStruct((tokens, f...  14.4 us
    dot_general x4, matrix products, over_tokens(): jnp.einsum('td,tf->df', rows, residual_grad[:, columns], preferred_elemen...  13.4 us
    ppermute x12, starting transfers between devices, y_hop(): return lax.ppermute(value, ('y', 'c'), pairs)  13.2 us
    ppermute x8, starting transfers between devices, core_swap(): return lax.ppermute(value, 'c', [(0, 1), (1, 0)])  12.3 us
  transfers between devices with their start and end apart: 22, of which 11 were waited for; matrix products, arithmetic and copies ran while one was open for 7% of the time, Pallas kernels for 0%

profile of v7, /device:TPU:1, one launch (start us, length us, event | category | flops | bytes accessed | tf_op | source)
XLA Modules:
  0.0 275.0 jit_solution(487158529273227523)
XLA Ops:
  2.5 33.4 %all_to_all.20.refs_8_ = bf16[8,528,256]{2,1,0:T(8,128)(2,1)S(1)} all-to-all(bf16[8,528,256]{2,1,0:T(8,128)(2,1)S(1)} %broadcast_in_dim.9), channel_id=1, replica_groups=mesh['xl'=2,'z'=4,'y'=4,'xh'=2,'c'=2] {'xl','z'}, dimensions={0} | all-to-all | bytes 4325376 | tf_op jit(solution)/shard_map/all_to_all | solution.py:46
  36.0 2.3 collective-permute-start.7
  38.3 2.5 collective-permute-start
  40.9 2.7 collective-permute-start.1
  46.0 13.1 %collective-permute-done.refs_1_ = bf16[96,4096]{1,0:T(8,128)(2,1)} collective-permute-done((bf16[96,4096]{1,0:T(8,128)(2,1)S(1)}, bf16[96,4096]{1,0:T(8,128)(2,1)}, u32[]{:S(2)}, u32[]{:S(2)}) %collective-permute-start) | collective-permute-done | bytes 786464 | tf_op jit(solution)/shard_map/ppermute | solution.py:32
  63.4 11.8 %collective-permute-done.4.refs_5_ = bf16[96,4096]{1,0:T(8,128)(2,1)} collective-permute-done((bf16[96,4096]{1,0:T(8,128)(2,1)}, bf16[96,4096]{1,0:T(8,128)(2,1)}, u32[]{:S(2)}, u32[]{:S(2)}) %collective-permute-start.4) | collective-permute-done | bytes 786464 | tf_op jit(solution)/shard_map/ppermute | solution.py:41
  79.8 12.3 %collective-permute-done.2.refs_3_ = bf16[96,4096]{1,0:T(8,128)(2,1)} collective-permute-done((bf16[96,4096]{1,0:T(8,128)(2,1)S(1)}, bf16[96,4096]{1,0:T(8,128)(2,1)}, u32[]{:S(2)}, u32[]{:S(2)}) %collective-permute-start.2) | collective-permute-done | bytes 786464 | tf_op jit(solution)/shard_map/ppermute | solution.py:41
  92.1 6.4 %collective-permute-done.5.refs_6_ = bf16[96,4096]{1,0:T(8,128)(2,1)} collective-permute-done((bf16[96,4096]{1,0:T(8,128)(2,1)}, bf16[96,4096]{1,0:T(8,128)(2,1)}, u32[]{:S(2)}, u32[]{:S(2)}) %collective-permute-start.5) | collective-permute-done | bytes 786464 | tf_op jit(solution)/shard_map/ppermute | solution.py:41
  98.5 6.8 %collective-permute-done.6.refs_7_ = bf16[96,4096]{1,0:T(8,128)(2,1)} collective-permute-done((bf16[96,4096]{1,0:T(8,128)(2,1)}, bf16[96,4096]{1,0:T(8,128)(2,1)}, u32[]{:S(2)}, u32[]{:S(2)}) %collective-permute-start.6) | collective-permute-done | bytes 786464 | tf_op jit(solution)/shard_map/ppermute | solution.py:41
  105.3 1.6 copy-done.1
  108.0 8.2 %forward.2 = (f32[768,512]{1,0:T(8,128)S(1)}, bf16[768,4096]{1,0:T(8,128)(2,1)}) custom-call(bf16[96,4096]{1,0:T(8,128)(2,1)S(1)} %slice_bitcast_fusion.1.refs_0_, bf16[96,4096]{1,0:T(8,128)(2,1)} %collective-permute-done.refs_1_, bf16[96,4096]{1,0:T(8,128)(2,1)} %collective-permute-done.1.refs_2_, bf16[96,4096]{1,0:T(8,128)(2,1)} %collective-permute-done.2.refs_3_, ...), custom_call_target="tpu_custom_call" | custom-call | flops 3221225472 | bytes 16777216 | tf_op jit(solution)/shard_map/forward/pallas_call | solution.py:134
  116.7 11.9 %all_to_all.21 = f32[8,1,2304]{2,1,0:T(1,128)S(1)} all-to-all(f32[8,1,2304]{2,1,0:T(1,128)S(1)} %broadcast_in_dim.10), channel_id=1, replica_groups=mesh['xl'=2,'z'=4,'y'=4,'xh'=2,'c'=2] {'y','xh'}, dimensions={0} | all-to-all | bytes 147456 | tf_op jit(solution)/shard_map/all_to_all | solution.py:46
  129.8 1.8 copy-done.16
  131.6 2.0 convolution_convert_fusion.2
  133.5 4.2 %collective-permute-start.10 = (bf16[4096,256]{1,0:T(8,128)(2,1)S(1)}, bf16[4096,256]{1,0:T(8,128)(2,1)S(1)}, u32[]{:S(2)}, u32[]{:S(2)}) collective-permute-start(bf16[4096,256]{1,0:T(8,128)(2,1)S(1)} %convolution_convert_fusion.2), channel_id=1, source_target_pairs={{0,1},{1,0},{2,3},{3,2},{4,5},{5,4},{6,7},{7,6},{8,9},{9,8},{10,11... | collective-permute-start | bytes 6291464 | tf_op jit(solution)/shard_map/ppermute | solution.py:28
  138.7 2.0 convolution_convert_fusion.3
  141.5 3.8 %fusion.49 = (bf16[4096,256]{1,0:T(8,128)(2,1)S(1)}, bf16[4096,256]{1,0:T(8,128)(2,1)}, bf16[4096,256]{1,0:T(8,128)(2,1)}) fusion(bf16[4096,256]{1,0:T(8,128)(2,1)S(1)} %collective-permute-done.10, bf16[4096,256]{1,0:T(8,128)(2,1)S(1)} %convolution_convert_fusion.3, bf16[8,512,256]{2,1,0:T(8,128)(2,1)S(1)} %slice.140), kind=kLoop, calls=%fused_computation.122 | loop fusion | flops 16777216 | bytes 12582912 | tf_op jit(solution)/shard_map/convert_element_type | solution.py:252
  146.5 12.1 %collective-permute-done.11.refs_1_ = bf16[96,4096]{1,0:T(8,128)(2,1)S(1)} collective-permute-done((bf16[96,4096]{1,0:T(8,128)(2,1)S(1)}, bf16[96,4096]{1,0:T(8,128)(2,1)S(1)}, u32[]{:S(2)}, u32[]{:S(2)}) %collective-permute-start.11) | collective-permute-done | bytes 786464 | tf_op jit(solution)/shard_map/ppermute | solution.py:32
  158.9 1.8 collective-permute-start.19
  161.2 2.1 collective-permute-start.14
  163.3 12.1 %collective-permute-done.15.refs_5_ = bf16[96,4096]{1,0:T(8,128)(2,1)S(1)} collective-permute-done((bf16[96,4096]{1,0:T(8,128)(2,1)S(1)}, bf16[96,4096]{1,0:T(8,128)(2,1)S(1)}, u32[]{:S(2)}, u32[]{:S(2)}) %collective-permute-start.15) | collective-permute-done | bytes 786464 | tf_op jit(solution)/shard_map/ppermute | solution.py:41
  176.9 15.4 %collective-permute-done.13.refs_3_ = bf16[96,4096]{1,0:T(8,128)(2,1)S(1)} collective-permute-done((bf16[96,4096]{1,0:T(8,128)(2,1)S(1)}, bf16[96,4096]{1,0:T(8,128)(2,1)S(1)}, u32[]{:S(2)}, u32[]{:S(2)}) %collective-permute-start.13) | collective-permute-done | bytes 786464 | tf_op jit(solution)/shard_map/ppermute | solution.py:41
  192.3 5.4 %collective-permute-done.16.refs_6_ = bf16[96,4096]{1,0:T(8,128)(2,1)S(1)} collective-permute-done((bf16[96,4096]{1,0:T(8,128)(2,1)S(1)}, bf16[96,4096]{1,0:T(8,128)(2,1)S(1)}, u32[]{:S(2)}, u32[]{:S(2)}) %collective-permute-start.16) | collective-permute-done | bytes 786464 | tf_op jit(solution)/shard_map/ppermute | solution.py:41
  197.7 6.7 %collective-permute-done.17.refs_7_ = bf16[96,4096]{1,0:T(8,128)(2,1)S(1)} collective-permute-done((bf16[96,4096]{1,0:T(8,128)(2,1)S(1)}, bf16[96,4096]{1,0:T(8,128)(2,1)S(1)}, u32[]{:S(2)}, u32[]{:S(2)}) %collective-permute-start.17) | collective-permute-done | bytes 786464 | tf_op jit(solution)/shard_map/ppermute | solution.py:41
  204.4 6.3 %forward.3 = (f32[768,512]{1,0:T(8,128)S(1)}, bf16[768,4096]{1,0:T(8,128)(2,1)}) custom-call(bf16[96,4096]{1,0:T(8,128)(2,1)S(1)} %slice_bitcast_fusion.refs_0_, bf16[96,4096]{1,0:T(8,128)(2,1)S(1)} %collective-permute-done.11.refs_1_, bf16[96,4096]{1,0:T(8,128)(2,1)S(1)} %collective-permute-done.12.refs_2_, ...), custom_call_target="tpu_custom_call" | custom-call | flops 3221225472 | bytes 16777216 | tf_op jit(solution)/shard_map/forward/pallas_call | solution.py:134
  211.3 9.1 %all_to_all.22 = f32[8,1,2304]{2,1,0:T(1,128)S(1)} all-to-all(f32[8,1,2304]{2,1,0:T(1,128)S(1)} %broadcast_in_dim.11), channel_id=1, replica_groups=mesh['xl'=2,'z'=4,'y'=4,'xh'=2,'c'=2] {'y','xh'}, dimensions={0} | all-to-all | bytes 147456 | tf_op jit(solution)/shard_map/all_to_all | solution.py:46
  221.5 1.8 copy-done.17
  223.3 3.3 %convolution_convert_fusion = bf16[4096,256]{1,0:T(8,128)(2,1)} fusion(bf16[768,4096]{1,0:T(8,128)(2,1)S(1)} %copy-done.17, bf16[768,512]{1,0:T(8,128)(2,1)S(1)} %get-tuple-element.39), kind=kOutput, calls=%fused_computation.7 | convolution fusion | flops 1611661312 | bytes 8781824 | tf_op jit(solution)/shard_map/td,tf->df/dot_general | solution.py:238
  226.6 3.2 %collective-permute-start.20 = (bf16[4096,256]{1,0:T(8,128)(2,1)}, bf16[4096,256]{1,0:T(8,128)(2,1)}, u32[]{:S(2)}, u32[]{:S(2)}) collective-permute-start(bf16[4096,256]{1,0:T(8,128)(2,1)} %convolution_convert_fusion), channel_id=1, source_target_pairs={{0,1},{1,0},{2,3},{3,2},{4,5},{5,4},{6,7},{7,6},{8,9},{9,8},{10,11... | collective-permute-start | bytes 6291464 | tf_op jit(solution)/shard_map/ppermute | solution.py:28
  230.1 6.1 %convolution_convert_fusion.1 = bf16[4096,256]{1,0:T(8,128)(2,1)} fusion(bf16[768,4096]{1,0:T(8,128)(2,1)} %get-tuple-element.18, bf16[768,512]{1,0:T(8,128)(2,1)S(1)} %get-tuple-element.39), kind=kOutput, calls=%fused_computation.8 | convolution fusion | flops 1611661312 | bytes 8781824 | tf_op jit(solution)/shard_map/td,tf->df/dot_general | solution.py:238
  236.5 5.9 %fusion.1 = bf16[4096,256]{1,0:T(8,128)(2,1)S(1)} fusion(bf16[4096,256]{1,0:T(8,128)(2,1)} %get-tuple-element.14, bf16[4096,256]{1,0:T(8,128)(2,1)} %get-tuple-element.15, bf16[4096,256]{1,0:T(8,128)(2,1)} %collective-permute-done.20, bf16[4096,256]{1,0:T(8,128)(2,1)} %convolution_convert_fusion.1, bf16[8,512,256]{2,1,0:T(8,128)(2,1)S(1)} %copy-done.6), kind=kLoop, calls=%fused_computation.14 | loop fusion | flops 26214400 | bytes 12582912 | tf_op jit(solution)/shard_map/convert_element_type | solution.py:269
  242.5 29.6 %all_to_all.23 = bf16[8,528,256]{2,1,0:T(8,128)(2,1)S(1)} all-to-all(bf16[8,528,256]{2,1,0:T(8,128)(2,1)S(1)} %fusion.13), channel_id=1, replica_groups=mesh['xl'=2,'z'=4,'y'=4,'xh'=2,'c'=2] {'xl','z'}, dimensions={0} | all-to-all | bytes 4325376 | tf_op jit(solution)/shard_map/all_to_all | solution.py:272
  (113 shorter events, 26.5 us)
Async XLA Ops:
  2.5 35.7 %copy-start.11 = (bf16[1,2,96,4096]{3,2,1,0:T(8,128)(2,1)S(1)}, bf16[1,2,96,4096]{3,2,1,0:T(8,128)(2,1)}, u32[]{:S(2)}) copy-start(bf16[1,2,96,4096]{3,2,1,0:T(8,128)(2,1)} %param.11) | copy-start | bytes 4718596
  36.0 42.8 %copy-start = (bf16[8,528,256]{2,1,0:T(8,128)(2,1)}, bf16[8,528,256]{2,1,0:T(8,128)(2,1)S(1)}, u32[]{:S(2)}) copy-start(bf16[8,528,256]{2,1,0:T(8,128)(2,1)S(1)} %all_to_all.20.refs_8_) | copy-start | bytes 6488068
  36.0 42.9 %collective-permute-start.7 = (bf16[8,528,256]{2,1,0:T(8,128)(2,1)S(1)}, bf16[8,528,256]{2,1,0:T(8,128)(2,1)}, u32[]{:S(2)}, u32[]{:S(2)}) collective-permute-start(bf16[8,528,256]{2,1,0:T(8,128)(2,1)S(1)} %all_to_all.20.refs_8_), channel_id=1, source_target_pairs={{0,1},{1,0},{2,3},{3,2},{4,5},{5,4},{6,7},{7,6},{8,9},{9,8},{10,11... | collective-permute-start | bytes 6488072 | tf_op jit(solution)/shard_map/ppermute | solution.py:28
  38.3 20.8 %collective-permute-start = (bf16[96,4096]{1,0:T(8,128)(2,1)S(1)}, bf16[96,4096]{1,0:T(8,128)(2,1)}, u32[]{:S(2)}, u32[]{:S(2)}) collective-permute-start(bf16[96,4096]{1,0:T(8,128)(2,1)S(1)} %slice_bitcast_fusion.1.refs_0_), channel_id=1, source_target_pairs={{0,2},{2,0},{1,3},{3,1},{4,6},{6,4},{5,7},{7,5},{8,10},{10,8},{9,1... | collective-permute-start | bytes 2359304 | tf_op jit(solution)/shard_map/ppermute | solution.py:32
  40.9 20.8 %collective-permute-start.1 = (bf16[96,4096]{1,0:T(8,128)(2,1)S(1)}, bf16[96,4096]{1,0:T(8,128)(2,1)}, u32[]{:S(2)}, u32[]{:S(2)}) collective-permute-start(bf16[96,4096]{1,0:T(8,128)(2,1)S(1)} %slice_bitcast_fusion.1.refs_0_), channel_id=1, source_target_pairs={{0,4},{1,13},{4,8},{5,1},{8,12},{9,5},{12,0},{13,9},{2,6},{3,15},{... | collective-permute-start | bytes 2359304 | tf_op jit(solution)/shard_map/ppermute | solution.py:41
  45.2 15.2 %collective-permute-start.8 = (bf16[2,8,96,256]{3,2,1,0:T(8,128)(2,1)S(1)}, bf16[2,8,96,256]{3,2,1,0:T(8,128)(2,1)S(1)}, u32[]{:S(2)}, u32[]{:S(2)}) collective-permute-start(bf16[2,8,96,256]{3,2,1,0:T(8,128)(2,1)S(1)} %get-tuple-element.53), channel_id=1, source_target_pairs={{0,1},{1,0},{2,3},{3,2},{4,5},{5,4},{6,7},{7,6},{8,9},{9,8},{10,11... | collective-permute-start | bytes 2359304 | tf_op jit(solution)/shard_map/ppermute | solution.py:28
  45.6 17.5 %collective-permute-start.9 = (bf16[2,8,96,256]{3,2,1,0:T(8,128)(2,1)S(1)}, bf16[2,8,96,256]{3,2,1,0:T(8,128)(2,1)S(1)}, u32[]{:S(2)}, u32[]{:S(2)}) collective-permute-start(bf16[2,8,96,256]{3,2,1,0:T(8,128)(2,1)S(1)} %get-tuple-element.51), channel_id=1, source_target_pairs={{0,1},{1,0},{2,3},{3,2},{4,5},{5,4},{6,7},{7,6},{8,9},{9,8},{10,11... | collective-permute-start | bytes 2359304 | tf_op jit(solution)/shard_map/ppermute | solution.py:28
  59.1 16.1 %collective-permute-start.4 = (bf16[96,4096]{1,0:T(8,128)(2,1)}, bf16[96,4096]{1,0:T(8,128)(2,1)}, u32[]{:S(2)}, u32[]{:S(2)}) collective-permute-start(bf16[96,4096]{1,0:T(8,128)(2,1)} %collective-permute-done.refs_1_), channel_id=1, source_target_pairs={{0,12},{1,5},{4,0},{5,9},{8,4},{9,13},{12,8},{13,1},{2,14},{3,7},{... | collective-permute-start | bytes 2359304 | tf_op jit(solution)/shard_map/ppermute | solution.py:41
  60.4 31.7 %collective-permute-start.2 = (bf16[96,4096]{1,0:T(8,128)(2,1)S(1)}, bf16[96,4096]{1,0:T(8,128)(2,1)}, u32[]{:S(2)}, u32[]{:S(2)}) collective-permute-start(bf16[96,4096]{1,0:T(8,128)(2,1)S(1)} %slice_bitcast_fusion.1.refs_0_), channel_id=1, source_target_pairs={{0,12},{1,5},{4,0},{5,9},{8,4},{9,13},{12,8},{13,1},{2,14},{3,7},{... | collective-permute-start | bytes 2359304 | tf_op jit(solution)/shard_map/ppermute | solution.py:41
  61.7 30.4 %collective-permute-start.3 = (bf16[96,4096]{1,0:T(8,128)(2,1)}, bf16[96,4096]{1,0:T(8,128)(2,1)}, u32[]{:S(2)}, u32[]{:S(2)}) collective-permute-start(bf16[96,4096]{1,0:T(8,128)(2,1)} %collective-permute-done.refs_1_), channel_id=1, source_target_pairs={{0,4},{1,13},{4,8},{5,1},{8,12},{9,5},{12,0},{13,9},{2,6},{3,15},{... | collective-permute-start | bytes 2359304 | tf_op jit(solution)/shard_map/ppermute | solution.py:41
  63.1 35.3 %collective-permute-start.5 = (bf16[96,4096]{1,0:T(8,128)(2,1)}, bf16[96,4096]{1,0:T(8,128)(2,1)}, u32[]{:S(2)}, u32[]{:S(2)}) collective-permute-start(bf16[96,4096]{1,0:T(8,128)(2,1)} %collective-permute-done.1.refs_2_), channel_id=1, source_target_pairs={{0,4},{1,13},{4,8},{5,1},{8,12},{9,5},{12,0},{13,9},{2,6},{3,15},{... | collective-permute-start | bytes 2359304 | tf_op jit(solution)/shard_map/ppermute | solution.py:41
  75.2 30.0 %collective-permute-start.6 = (bf16[96,4096]{1,0:T(8,128)(2,1)}, bf16[96,4096]{1,0:T(8,128)(2,1)}, u32[]{:S(2)}, u32[]{:S(2)}) collective-permute-start(bf16[96,4096]{1,0:T(8,128)(2,1)} %collective-permute-done.4.refs_5_), channel_id=1, source_target_pairs={{0,12},{1,5},{4,0},{5,9},{8,4},{9,13},{12,8},{13,1},{2,14},{3,7},{... | collective-permute-start | bytes 2359304 | tf_op jit(solution)/shard_map/ppermute | solution.py:41
  108.0 8.2 %copy-start.8 = (bf16[1,8,96,512]{3,2,1,0:T(8,128)(2,1)S(1)}, bf16[1,8,96,512]{3,2,1,0:T(8,128)(2,1)}, u32[]{:S(2)}) copy-start(bf16[1,8,96,512]{3,2,1,0:T(8,128)(2,1)} %get-tuple-element.48) | copy-start | bytes 2359300
  131.6 6.2 %copy-start.12 = (bf16[1,2,96,4096]{3,2,1,0:T(8,128)(2,1)S(1)}, bf16[1,2,96,4096]{3,2,1,0:T(8,128)(2,1)}, u32[]{:S(2)}) copy-start(bf16[1,2,96,4096]{3,2,1,0:T(8,128)(2,1)} %param.11) | copy-start | bytes 4718596
  131.6 6.9 %copy-start.2 = (bf16[8,528,256]{2,1,0:T(8,128)(2,1)S(1)}, bf16[8,528,256]{2,1,0:T(8,128)(2,1)}, u32[]{:S(2)}) copy-start(bf16[8,528,256]{2,1,0:T(8,128)(2,1)} %copy-done) | copy-start | bytes 6488068
  133.5 8.0 %collective-permute-start.10 = (bf16[4096,256]{1,0:T(8,128)(2,1)S(1)}, bf16[4096,256]{1,0:T(8,128)(2,1)S(1)}, u32[]{:S(2)}, u32[]{:S(2)}) collective-permute-start(bf16[4096,256]{1,0:T(8,128)(2,1)S(1)} %convolution_convert_fusion.2), channel_id=1, source_target_pairs={{0,1},{1,0},{2,3},{3,2},{4,5},{5,4},{6,7},{7,6},{8,9},{9,8},{10,11... | collective-permute-start | bytes 6291464 | tf_op jit(solution)/shard_map/ppermute | solution.py:28
  137.8 20.8 %collective-permute-start.11 = (bf16[96,4096]{1,0:T(8,128)(2,1)S(1)}, bf16[96,4096]{1,0:T(8,128)(2,1)S(1)}, u32[]{:S(2)}, u32[]{:S(2)}) collective-permute-start(bf16[96,4096]{1,0:T(8,128)(2,1)S(1)} %slice_bitcast_fusion.refs_0_), channel_id=1, source_target_pairs={{0,2},{2,0},{1,3},{3,1},{4,6},{6,4},{5,7},{7,5},{8,10},{10,8},{9,1... | collective-permute-start | bytes 2359304 | tf_op jit(solution)/shard_map/ppermute | solution.py:32
  138.6 2.9 %copy-start.5 = (bf16[8,512,256]{2,1,0:T(8,128)(2,1)}, bf16[8,512,256]{2,1,0:T(8,128)(2,1)S(1)}, u32[]{:S(2)}) copy-start(bf16[8,512,256]{2,1,0:T(8,128)(2,1)S(1)} %slice.140) | copy-start | bytes 6291460
  140.6 63.7 %copy-start.3 = (bf16[1,8,96,512]{3,2,1,0:T(8,128)(2,1)S(1)}, bf16[1,8,96,512]{3,2,1,0:T(8,128)(2,1)}, u32[]{:S(2)}) copy-start(bf16[1,8,96,512]{3,2,1,0:T(8,128)(2,1)} %get-tuple-element.49) | copy-start | bytes 2359300
  145.3 59.1 %collective-permute-start.18 = (bf16[8,512,256]{2,1,0:T(8,128)(2,1)S(1)}, bf16[8,512,256]{2,1,0:T(8,128)(2,1)S(1)}, u32[]{:S(2)}, u32[]{:S(2)}) collective-permute-start(bf16[8,512,256]{2,1,0:T(8,128)(2,1)S(1)} %bitcast.54), channel_id=1, source_target_pairs={{0,1},{1,0},{2,3},{3,2},{4,5},{5,4},{6,7},{7,6},{8,9},{9,8},{10,11... | collective-permute-start | bytes 6291464 | tf_op jit(solution)/shard_map/ppermute | solution.py:28
  145.7 15.6 %collective-permute-start.12 = (bf16[96,4096]{1,0:T(8,128)(2,1)S(1)}, bf16[96,4096]{1,0:T(8,128)(2,1)S(1)}, u32[]{:S(2)}, u32[]{:S(2)}) collective-permute-start(bf16[96,4096]{1,0:T(8,128)(2,1)S(1)} %slice_bitcast_fusion.refs_0_), channel_id=1, source_target_pairs={{0,4},{1,13},{4,8},{5,1},{8,12},{9,5},{12,0},{13,9},{2,6},{3,15},{... | collective-permute-start | bytes 2359304 | tf_op jit(solution)/shard_map/ppermute | solution.py:41
  158.6 16.8 %collective-permute-start.15 = (bf16[96,4096]{1,0:T(8,128)(2,1)S(1)}, bf16[96,4096]{1,0:T(8,128)(2,1)S(1)}, u32[]{:S(2)}, u32[]{:S(2)}) collective-permute-start(bf16[96,4096]{1,0:T(8,128)(2,1)S(1)} %collective-permute-done.11.refs_1_), channel_id=1, source_target_pairs={{0,12},{1,5},{4,0},{5,9},{8,4},{9,13},{12,8},{13,1},{2,14},{3,7},{... | collective-permute-start | bytes 2359304 | tf_op jit(solution)/shard_map/ppermute | solution.py:41
  158.9 16.8 %collective-permute-start.19 = (f32[512]{0:T(512)S(1)}, f32[512]{0:T(512)S(1)}, u32[]{:S(2)}, u32[]{:S(2)}) collective-permute-start(f32[512]{0:T(512)S(1)} %get-tuple-element.41), channel_id=1, source_target_pairs={{0,1},{1,0},{2,3},{3,2},{4,5},{5,4},{6,7},{7,6},{8,9},{9,8},{10,11... | collective-permute-start | bytes 6152 | tf_op jit(solution)/shard_map/ppermute | solution.py:28
  160.7 31.6 %collective-permute-start.13 = (bf16[96,4096]{1,0:T(8,128)(2,1)S(1)}, bf16[96,4096]{1,0:T(8,128)(2,1)S(1)}, u32[]{:S(2)}, u32[]{:S(2)}) collective-permute-start(bf16[96,4096]{1,0:T(8,128)(2,1)S(1)} %slice_bitcast_fusion.refs_0_), channel_id=1, source_target_pairs={{0,12},{1,5},{4,0},{5,9},{8,4},{9,13},{12,8},{13,1},{2,14},{3,7},{... | collective-permute-start | bytes 2359304 | tf_op jit(solution)/shard_map/ppermute | solution.py:41
  161.2 31.1 %collective-permute-start.14 = (bf16[96,4096]{1,0:T(8,128)(2,1)S(1)}, bf16[96,4096]{1,0:T(8,128)(2,1)S(1)}, u32[]{:S(2)}, u32[]{:S(2)}) collective-permute-start(bf16[96,4096]{1,0:T(8,128)(2,1)S(1)} %collective-permute-done.11.refs_1_), channel_id=1, source_target_pairs={{0,4},{1,13},{4,8},{5,1},{8,12},{9,5},{12,0},{13,9},{2,6},{3,15},{... | collective-permute-start | bytes 2359304 | tf_op jit(solution)/shard_map/ppermute | solution.py:41
  175.4 22.2 %collective-permute-start.16 = (bf16[96,4096]{1,0:T(8,128)(2,1)S(1)}, bf16[96,4096]{1,0:T(8,128)(2,1)S(1)}, u32[]{:S(2)}, u32[]{:S(2)}) collective-permute-start(bf16[96,4096]{1,0:T(8,128)(2,1)S(1)} %collective-permute-done.12.refs_2_), channel_id=1, source_target_pairs={{0,4},{1,13},{4,8},{5,1},{8,12},{9,5},{12,0},{13,9},{2,6},{3,15},{... | collective-permute-start | bytes 2359304 | tf_op jit(solution)/shard_map/ppermute | solution.py:41
  175.7 28.7 %collective-permute-start.17 = (bf16[96,4096]{1,0:T(8,128)(2,1)S(1)}, bf16[96,4096]{1,0:T(8,128)(2,1)S(1)}, u32[]{:S(2)}, u32[]{:S(2)}) collective-permute-start(bf16[96,4096]{1,0:T(8,128)(2,1)S(1)} %collective-permute-done.15.refs_5_), channel_id=1, source_target_pairs={{0,12},{1,5},{4,0},{5,9},{8,4},{9,13},{12,8},{13,1},{2,14},{3,7},{... | collective-permute-start | bytes 2359304 | tf_op jit(solution)/shard_map/ppermute | solution.py:41
  204.4 6.3 %copy-start.7 = (bf16[1,8,96,512]{3,2,1,0:T(8,128)(2,1)S(1)}, bf16[1,8,96,512]{3,2,1,0:T(8,128)(2,1)}, u32[]{:S(2)}) copy-start(bf16[1,8,96,512]{3,2,1,0:T(8,128)(2,1)} %get-tuple-element.47) | copy-start | bytes 2359300
  220.5 2.8 %copy-start.17 = (bf16[768,4096]{1,0:T(8,128)(2,1)S(1)}, bf16[768,4096]{1,0:T(8,128)(2,1)}, u32[]{:S(2)}) copy-start(bf16[768,4096]{1,0:T(8,128)(2,1)} %get-tuple-element.18) | copy-start | bytes 18874372
  226.6 9.9 %collective-permute-start.20 = (bf16[4096,256]{1,0:T(8,128)(2,1)}, bf16[4096,256]{1,0:T(8,128)(2,1)}, u32[]{:S(2)}, u32[]{:S(2)}) collective-permute-start(bf16[4096,256]{1,0:T(8,128)(2,1)} %convolution_convert_fusion), channel_id=1, source_target_pairs={{0,1},{1,0},{2,3},{3,2},{4,5},{5,4},{6,7},{7,6},{8,9},{9,8},{10,11... | collective-permute-start | bytes 6291464 | tf_op jit(solution)/shard_map/ppermute | solution.py:28
  230.0 6.5 %copy-start.6 = (bf16[8,512,256]{2,1,0:T(8,128)(2,1)S(1)}, bf16[8,512,256]{2,1,0:T(8,128)(2,1)}, u32[]{:S(2)}) copy-start(bf16[8,512,256]{2,1,0:T(8,128)(2,1)} %copy-done.5) | copy-start | bytes 6291460
  230.0 6.2 %collective-permute-start.21 = (f32[512]{0:T(512)S(1)}, f32[512]{0:T(512)S(1)}, u32[]{:S(2)}, u32[]{:S(2)}) collective-permute-start(f32[512]{0:T(512)S(1)} %get-tuple-element.40), channel_id=1, source_target_pairs={{0,1},{1,0},{2,3},{3,2},{4,5},{5,4},{6,7},{7,6},{8,9},{9,8},{10,11... | collective-permute-start | bytes 6152 | tf_op jit(solution)/shard_map/ppermute | solution.py:28
  (8 other events, 13.7 us)
